TPU v7x, 32 devices: a whole 2x2x4 slice. The times are simulated.
32 devices in a mesh: grp: 4 (over y, core), peer: 8 (over z, x).
Axes of the slice: x: 2, y: 2, z: 4, core: 2. Of those that a mesh axis runs over, the one named last changes fastest.
Arguments:
- nodes: bfloat16 [65536, 64], P(('grp', 'peer')), may hold values from -6 to 6
- edges: bfloat16 [1048576, 64], P(('grp', 'peer')), may hold values from -6 to 6
- send_nodes: int32 [1048576], P(('grp', 'peer')), may hold values from 0 to 2047
- block_tile: int32 [8192], P(('grp', 'peer')), may hold values from 0 to 15
- block_count: int32 [8192], P(('grp', 'peer')), may hold values from 1 to 128, 629145 in all
- slot_ids: int32 [1048576], P(('grp', 'peer')), may hold values from 0 to 127
- edge_in_weight: bfloat16 [192, 64], replicated, may hold values from -0.4375 to 0.4375
- edge_in_bias: float32 [64], replicated, may hold values from -3 to 3
- edge_out_weight: bfloat16 [64, 64], replicated, may hold values from -0.75 to 0.75
- edge_out_bias: float32 [64], replicated, may hold values from -3 to 3
- edge_gain: float32 [64], replicated, may hold values from 0.5 to 1.5
- edge_shift: float32 [64], replicated, may hold values from -3 to 3
- node_in_weight: bfloat16 [128, 64], replicated, may hold values from -0.5 to 0.5
- node_in_bias: float32 [64], replicated, may hold values from -3 to 3
- node_out_weight: bfloat16 [64, 64], replicated, may hold values from -0.75 to 0.75
- node_out_bias: float32 [64], replicated, may hold values from -3 to 3
- node_gain: float32 [64], replicated, may hold values from 0.5 to 1.5
- node_shift: float32 [64], replicated, may hold values from -3 to 3
- node_cot: bfloat16 [65536, 64], P(('grp', 'peer')), may hold values from -6 to 6
- edge_cot: bfloat16 [1048576, 64], P(('grp', 'peer')), may hold values from -6 to 6
Outputs:
- node_result: bfloat16 [65536, 64], P(('grp', 'peer'))
- edge_result: bfloat16 [1048576, 64], P(('grp', 'peer'))
- node_grad: float32 [65536, 64], P(('grp', 'peer'))
- edge_grad: float32 [1048576, 64], P(('grp', 'peer'))
- edge_in_weight_grad: float32 [192, 64], replicated
- edge_in_bias_grad: float32 [64], replicated
- edge_out_weight_grad: float32 [64, 64], replicated
- edge_out_bias_grad: float32 [64], replicated
- edge_gain_grad: float32 [64], replicated
- edge_shift_grad: float32 [64], replicated
- node_in_weight_grad: float32 [128, 64], replicated
- node_in_bias_grad: float32 [64], replicated
- node_out_weight_grad: float32 [64, 64], replicated
- node_out_bias_grad: float32 [64], replicated
- node_gain_grad: float32 [64], replicated
- node_shift_grad: float32 [64], replicated
Inputs may be any that keep to these rules, and one draw needn't show every extreme that they name: `block_tile`: tile of 128 receivers among the owner's 16.
All inputs are finite; a program needn't handle non-finite values. No bound on the sum of `block_count` on one device may be relied on, other than what follows from the above.
Results may differ from a plain program's by a relative error of at most 0.0094.
Values may be sent and summed in bfloat16 or wider, within the bound.
No kernel may reach another device: no remote copies, remote signals or barrier semaphores. Data moves between devices by JAX's collectives and lax.ppermute only.
A program may use at most 192 MiB of HBM per device.

v0:
```python
import jax
import jax.numpy as jnp
from jax import lax
from jax.sharding import PartitionSpec as P

epsilon = 1e-05
highest = lax.Precision.HIGHEST


def norm_forward(inputs, gain_vec, shift_vec):
    average = jnp.mean(inputs, axis=-1, keepdims=True)
    centered = inputs - average
    inv_dev = lax.rsqrt(jnp.mean(centered * centered, axis=-1, keepdims=True) + epsilon)
    normed = centered * inv_dev
    return (normed * gain_vec + shift_vec, normed, inv_dev)


def norm_backward(upstream, normed, inv_dev, gain_vec):
    scaled = upstream * gain_vec
    inner = (
        scaled
        - jnp.mean(scaled, axis=-1, keepdims=True)
        - normed * jnp.mean(scaled * normed, axis=-1, keepdims=True)
    )
    return (inner * inv_dev, jnp.sum(upstream * normed, axis=0), jnp.sum(upstream, axis=0))


def silu_slope(inputs):
    sigmoid_val = jax.nn.sigmoid(inputs)
    return sigmoid_val * (1.0 + inputs * (1.0 - sigmoid_val))


def matmul(left_side, right_side):
    return jnp.dot(left_side, right_side, preferred_element_type=jnp.float32)


def matmul_left_t(left_side, right_side):
    return lax.dot_general(
        left_side, right_side, (((0,), (0,)), ((), ())), preferred_element_type=jnp.float32
    )


def matmul_right_t(left_side, right_side):
    return lax.dot_general(
        left_side, right_side, (((1,), (1,)), ((), ())), preferred_element_type=jnp.float32
    )


def onto_nodes(block_values, slot_onehot, tile_onehot):
    partial_sums = jnp.einsum(
        "nrp,nrd->npd", slot_onehot, block_values, preferred_element_type=jnp.float32
    )
    block_total, block_rows, feat_width = partial_sums.shape
    summed = jnp.dot(
        tile_onehot, partial_sums.reshape(block_total, block_rows * feat_width), precision=highest
    )
    return summed.reshape(tile_onehot.shape[0] * block_rows, feat_width)


def from_tiles_low(node_rows, tile_pick, slot_onehot):
    block_rows = slot_onehot.shape[1]
    feat_width = node_rows.shape[1]
    tile_rows = node_rows.reshape(-1, block_rows * feat_width)
    picked = jnp.dot(tile_pick, tile_rows, preferred_element_type=jnp.float32).astype(jnp.bfloat16)
    picked = picked.reshape(tile_pick.shape[0], block_rows, feat_width)
    placed = jnp.einsum("nrp,npd->nrd", slot_onehot, picked, preferred_element_type=jnp.float32)
    return placed.astype(jnp.bfloat16).reshape(-1, feat_width)


def from_tiles_wide(node_rows, tile_pick, slot_onehot):
    block_rows = slot_onehot.shape[1]
    feat_width = node_rows.shape[1]
    tile_rows = node_rows.reshape(-1, block_rows * feat_width)
    picked = jnp.dot(tile_pick, tile_rows, precision=highest).reshape(
        tile_pick.shape[0], block_rows, feat_width
    )
    placed = jnp.einsum("nrp,npd->nrd", slot_onehot, picked, precision=highest)
    return placed.reshape(-1, feat_width)


def sender_rows(nodes, send_nodes, group_rows):
    node_iota = jnp.arange(nodes.shape[0], dtype=jnp.int32)

    def pick_group(id_group):
        onehot = (id_group[:, None] == node_iota[None, :]).astype(jnp.bfloat16)
        return matmul(onehot, nodes).astype(jnp.bfloat16)

    picked = lax.map(pick_group, send_nodes.reshape(-1, group_rows))
    return picked.reshape(-1, nodes.shape[1])


def sender_sums(grad_rows, send_nodes, node_total, group_rows):
    node_iota = jnp.arange(node_total, dtype=jnp.int32)
    feat_width = grad_rows.shape[1]

    def add_group(total, pieces):
        id_group, grad_group = pieces
        onehot = (id_group[:, None] == node_iota[None, :]).astype(jnp.float32)
        term = lax.dot_general(onehot, grad_group, (((0,), (0,)), ((), ())), precision=highest)
        return (total + term, None)

    start = jnp.zeros((node_total, feat_width), jnp.float32)
    total, unused = lax.scan(
        add_group,
        start,
        (send_nodes.reshape(-1, group_rows), grad_rows.reshape(-1, group_rows, feat_width)),
    )
    return total


def per_device(
    nodes,
    edges,
    send_nodes,
    block_tile,
    block_count,
    slot_ids,
    edge_in_weight,
    edge_in_bias,
    edge_out_weight,
    edge_out_bias,
    edge_gain,
    edge_shift,
    node_in_weight,
    node_in_bias,
    node_out_weight,
    node_out_bias,
    node_gain,
    node_shift,
    node_cot,
    edge_cot,
):
    block_total = block_tile.shape[0]
    block_rows = slot_ids.shape[0] // block_total
    feat_width = nodes.shape[1]
    node_total = nodes.shape[0]
    tile_total = node_total // block_rows
    group_rows = 8 * block_rows
    positions = jnp.arange(block_rows, dtype=jnp.int32)
    slot_grid = slot_ids.reshape(block_total, block_rows)
    live_grid = positions[None, :] < block_count[:, None]
    slot_mask = (slot_grid[:, :, None] == positions[None, None, :]) & live_grid[:, :, None]
    slot_onehot = slot_mask.astype(jnp.bfloat16)
    slot_wide = slot_mask.astype(jnp.float32)
    tile_onehot = (jnp.arange(tile_total, dtype=jnp.int32)[:, None] == block_tile[None, :]).astype(
        jnp.float32
    )
    tile_pick = tile_onehot.T
    outgoing = from_tiles_low(nodes, tile_pick.astype(jnp.bfloat16), slot_onehot)
    receiver_feats = lax.all_to_all(outgoing, "peer", split_axis=0, concat_axis=0, tiled=True)
    sender_feats = sender_rows(nodes, send_nodes, group_rows)
    edge_inputs = jnp.concatenate([sender_feats, receiver_feats, edges], axis=1)
    first_pre = matmul(edge_inputs, edge_in_weight) + edge_in_bias
    first_act = jax.nn.silu(first_pre).astype(jnp.bfloat16)
    second_pre = matmul(first_act, edge_out_weight) + edge_out_bias
    message, edge_normed, edge_inv = norm_forward(second_pre, edge_gain, edge_shift)
    message_low = message.astype(jnp.bfloat16)
    edge_result = (edges.astype(jnp.float32) + message_low.astype(jnp.float32)).astype(jnp.bfloat16)
    arrived = lax.all_to_all(message_low, "peer", split_axis=0, concat_axis=0, tiled=True)
    aggregate = onto_nodes(
        arrived.reshape(block_total, block_rows, feat_width), slot_onehot, tile_onehot
    )
    node_inputs = jnp.concatenate([nodes, aggregate.astype(jnp.bfloat16)], axis=1)
    third_pre = matmul(node_inputs, node_in_weight) + node_in_bias
    third_act = jax.nn.silu(third_pre).astype(jnp.bfloat16)
    fourth_pre = matmul(third_act, node_out_weight) + node_out_bias
    update, node_normed, node_inv = norm_forward(fourth_pre, node_gain, node_shift)
    node_result = (nodes.astype(jnp.float32) + update).astype(jnp.bfloat16)
    node_upstream = node_cot.astype(jnp.float32)
    fourth_grad, node_gain_grad, node_shift_grad = norm_backward(
        node_upstream, node_normed, node_inv, node_gain
    )
    fourth_low = fourth_grad.astype(jnp.bfloat16)
    node_out_bias_grad = jnp.sum(fourth_low.astype(jnp.float32), axis=0)
    node_out_weight_grad = matmul_left_t(third_act, fourth_low)
    third_grad = (matmul_right_t(fourth_low, node_out_weight) * silu_slope(third_pre)).astype(
        jnp.bfloat16
    )
    node_in_bias_grad = jnp.sum(third_grad.astype(jnp.float32), axis=0)
    node_in_weight_grad = matmul_left_t(node_inputs, third_grad)
    input_grad = matmul_right_t(third_grad, node_in_weight)
    aggregate_grad = input_grad[:, feat_width:]
    message_back = from_tiles_wide(aggregate_grad, tile_pick, slot_wide).astype(jnp.bfloat16)
    returned = lax.all_to_all(message_back, "peer", split_axis=0, concat_axis=0, tiled=True)
    edge_upstream = edge_cot.astype(jnp.float32)
    message_grad = edge_upstream + returned.astype(jnp.float32)
    second_grad, edge_gain_grad, edge_shift_grad = norm_backward(
        message_grad, edge_normed, edge_inv, edge_gain
    )
    second_low = second_grad.astype(jnp.bfloat16)
    edge_out_bias_grad = jnp.sum(second_low.astype(jnp.float32), axis=0)
    edge_out_weight_grad = matmul_left_t(first_act, second_low)
    first_grad = (matmul_right_t(second_low, edge_out_weight) * silu_slope(first_pre)).astype(
        jnp.bfloat16
    )
    edge_in_bias_grad = jnp.sum(first_grad.astype(jnp.float32), axis=0)
    edge_in_weight_grad = matmul_left_t(edge_inputs, first_grad)
    edge_input_grad = matmul_right_t(first_grad, edge_in_weight)
    sender_grad = edge_input_grad[:, :feat_width]
    receiver_grad = edge_input_grad[:, feat_width : 2 * feat_width].astype(jnp.bfloat16)
    edge_grad = edge_upstream + edge_input_grad[:, 2 * feat_width :]
    sender_sum = sender_sums(sender_grad, send_nodes, node_total, group_rows)
    back_values = lax.all_to_all(receiver_grad, "peer", split_axis=0, concat_axis=0, tiled=True)
    receiver_sum = onto_nodes(
        back_values.reshape(block_total, block_rows, feat_width), slot_onehot, tile_onehot
    )
    node_grad = node_upstream + input_grad[:, :feat_width] + sender_sum + receiver_sum
    weight_sums = lax.psum(
        (
            edge_in_weight_grad,
            edge_in_bias_grad,
            edge_out_weight_grad,
            edge_out_bias_grad,
            edge_gain_grad,
            edge_shift_grad,
            node_in_weight_grad,
            node_in_bias_grad,
            node_out_weight_grad,
            node_out_bias_grad,
            node_gain_grad,
            node_shift_grad,
        ),
        ("grp", "peer"),
    )
    return (
        node_result,
        edge_result,
        node_grad,
        edge_grad,
        weight_sums[0],
        weight_sums[1],
        weight_sums[2],
        weight_sums[3],
        weight_sums[4],
        weight_sums[5],
        weight_sums[6],
        weight_sums[7],
        weight_sums[8],
        weight_sums[9],
        weight_sums[10],
        weight_sums[11],
    )


def solution(mesh):
    placed = (
        P(("grp", "peer"), None),
        P(("grp", "peer"), None),
        P(("grp", "peer")),
        P(("grp", "peer")),
        P(("grp", "peer")),
        P(("grp", "peer")),
        P(),
        P(),
        P(),
        P(),
        P(),
        P(),
        P(),
        P(),
        P(),
        P(),
        P(),
        P(),
        P(("grp", "peer"), None),
        P(("grp", "peer"), None),
    )
    return jax.shard_map(
        per_device,
        mesh=mesh,
        in_specs=placed,
        out_specs=(
            P(("grp", "peer"), None),
            P(("grp", "peer"), None),
            P(("grp", "peer"), None),
            P(("grp", "peer"), None),
            P(),
            P(),
            P(),
            P(),
            P(),
            P(),
            P(),
            P(),
            P(),
            P(),
            P(),
            P(),
        ),
        check_vma=False,
    )
```

profile of v0, /device:TPU:0, one launch (start us, length us, event | category | flops | bytes accessed | tf_op | source)
XLA Modules:
  0.0 807.5 jit_solution(7611168785021974217)
XLA Ops:
  13.7 6.4 copy.55
  20.1 7.3 copy.56
  27.4 13.4 %fusion.36 = bf16[256,128,64]{1,2,0:T(8,128)(2,1)S(1)} fusion(bf16[256,128,64]{1,2,0:T(8,128)(2,1)} %copy.56, s32[256,128]{1,0:T(8,128)S(1)} %bitcast.102, pred[256,128]{1,0:T(8,128)(4,1)S(1)} %iota_compare_fusion.14), kind=kOutput, calls=%fused_computation.58 | convolution fusion | flops 547356672 | bytes 8552448 | tf_op jit(solution)/shard_map/nrp,npd->nrd/dot_general | solution.py:66
  45.6 7.3 all_to_all.24
  52.8 6.5 copy.58
  59.3 7.6 all-to-all-start
  67.0 80.3 %while.22 = (s32[]{:T(128)}, bf16[32,1024,64]{1,2,0:T(8,128)(2,1)}, s32[32,1024]{1,0:T(8,128)S(1)}, bf16[2048,64]{0,1:T(8,128)(2,1)S(1)}, s32[]{:T(128)}) while((s32[]{:T(128)}, bf16[32,1024,64]{1,2,0:T(8,128)(2,1)}, s32[32,1024]{1,0:T(8,128)S(1)}, bf16[2048,64]{0,1:T(8,128)(2,1)S(1)}, s32[]{:T(128)}) %tuple.74), condition=%wide.region_1.2_spmd.clone, body=%wide.region_0.1_spmd.clone.sunk | while | flops 270598144 | bytes 405581 | solution.py:88
  152.2 7.9 all-to-all-done
  167.4 11.5 %multiply_convert_fusion.1 = (bf16[32768,64]{0,1:T(8,128)(2,1)S(1)}, f32[32768,64]{0,1:T(8,128)}) fusion(f32[64]{0:T(128)S(1)} %copy-done.34, bf16[192,64]{0,1:T(8,128)(2,1)S(1)} %copy-done, bf16[32768,192]{0,1:T(8,128)(2,1)} %constant_dynamic-update-slice_fusion), kind=kOutput, calls=%fused_computation.42 | convolution fusion | flops 817889280 | bytes 25190656 | tf_op jit(solution)/shard_map/dot_general | solution.py:34
  185.3 96.8 %all_to_all.36 = bf16[8,4096,64]{1,2,0:T(8,128)(2,1)S(1)} all-to-all(bf16[8,4096,64]{1,2,0:T(8,128)(2,1)S(1)} %bitcast.96), channel_id=1, replica_groups=mesh['grp'=4,'peer'=8] {'peer'}, dimensions={0} | all-to-all | bytes 8388608 | tf_op jit(solution)/shard_map/all_to_all | solution.py:159
  286.4 7.4 reshape.168
  293.8 13.8 %fusion.21 = f32[256,128,64]{1,2,0:T(8,128)} fusion(s32[256,128]{1,0:T(8,128)S(1)} %bitcast.103, pred[256,128]{1,0:T(8,128)(4,1)S(1)} %iota_compare_fusion.14, bf16[256,128,64]{1,0,2:T(8,128)(2,1)} %reshape.168), kind=kOutput, calls=%fused_computation.25 | convolution fusion | flops 545259520 | bytes 12746752 | tf_op jit(solution)/shard_map/nrp,nrd->npd/dot_general | solution.py:50
  307.6 9.7 %copy.63 = f32[256,128,64]{0,2,1:T(8,128)} copy(f32[256,128,64]{1,2,0:T(8,128)} %fusion.21) | data formatting | bytes 16777216 | tf_op jit(solution)/shard_map/nrp,nrd->npd/dot_general | solution.py:50
  317.4 7.2 convolution_convert_fusion.1
  341.3 28.1 %fusion.39 = bf16[256,128,64]{1,2,0:T(8,128)(2,1)S(1)} fusion(f32[256,128,64]{1,0,2:T(8,128)S(1)} %fusion.59, s32[256,128]{1,0:T(8,128)S(1)} %bitcast.104, pred[256,128]{1,0:T(8,128)(4,1)S(1)} %iota_compare_fusion.14), kind=kOutput, calls=%fused_computation.59 | convolution fusion | flops 3231711232 | bytes 12746752 | tf_op jit(solution)/shard_map/nrp,npd->nrd/dot_general | solution.py:77
  374.1 7.3 convert_element_type.113
  381.4 6.5 copy.69
  394.3 90.3 %all-to-all-done.2 = bf16[8,4096,64]{1,2,0:T(8,128)(2,1)} async-done(((bf16[8,4096,64]{1,2,0:T(8,128)(2,1)}), bf16[8,4096,64]{1,2,0:T(8,128)(2,1)}, u32[]{:S(2)}, u32[]{:S(2)}) %all-to-all-start.2) | async-done | bytes 4194336 | tf_op jit(solution)/shard_map/all_to_all | solution.py:184
  484.6 6.7 convert_bitcast_fusion
  497.2 5.7 multiply_reduce_fusion
  503.0 4.9 convert_reduce_fusion
  507.9 5.4 fusion.73
  513.3 7.2 convert_reduce_fusion.1
  525.3 10.1 %fusion.71 = f32[32768,192]{0,1:T(8,128)} fusion(bf16[32768,64]{0,1:T(8,128)(2,1)S(1)} %get-tuple-element.165, bf16[192,64]{0,1:T(8,128)(2,1)S(1)} %copy-done), kind=kOutput, calls=%fused_computation.115 | convolution fusion | flops 805306368 | bytes 29384704 | tf_op jit(solution)/shard_map/dot_general | solution.py:44
  539.2 11.6 %convert_add_fusion = (f32[32768,64]{0,1:T(8,128)}, f32[32768,64]{0,1:T(8,128)}) fusion(bf16[32768,64]{0,1:T(8,128)(2,1)S(1)} %copy-done.2, f32[32768,192]{0,1:T(8,128)} %fusion.71), kind=kLoop, calls=%fused_computation.27 | loop fusion | flops 4194304 | bytes 37748736 | tf_op jit(solution)/shard_map/add | solution.py:201
  557.7 12.5 %copy.77 = f32[32768,64]{1,0:T(8,128)} copy(f32[32768,64]{0,1:T(8,128)} %get-tuple-element.154) | data formatting | bytes 16777216
  570.3 168.1 %while.23 = (s32[]{:T(128)}, f32[2048,64]{0,1:T(8,128)S(1)}, s32[32,1024]{1,0:T(8,128)}, f32[32,1024,64]{2,1,0:T(8,128)}, s32[]{:T(128)}, /*index=5*/s32[]{:T(128)}) while((s32[]{:T(128)}, f32[2048,64]{0,1:T(8,128)S(1)}, s32[32,1024]{1,0:T(8,128)}, f32[32,1024,64]{2,1,0:T(8,128)}, s32[]{:T(128)}, /*index=5*/s32[]{:T(128)}) %tuple.76), condition=%wide.region_11.12_spmd.clone, body=%wide.region_10.11_spmd.clone.sunk | while | flops 1612972032 | bytes 1585247 | solution.py:103
  738.5 6.7 copy.73
  745.2 7.4 reshape.172
  752.6 13.8 %fusion.17 = f32[256,128,64]{1,2,0:T(8,128)} fusion(s32[256,128]{1,0:T(8,128)S(1)} %bitcast.105, pred[256,128]{1,0:T(8,128)(4,1)S(1)} %copy-done.19, bf16[256,128,64]{1,0,2:T(8,128)(2,1)} %reshape.172), kind=kOutput, calls=%fused_computation.23 | convolution fusion | flops 545259520 | bytes 12746752 | tf_op jit(solution)/shard_map/nrp,nrd->npd/dot_general | solution.py:50
  766.5 9.3 %copy.75 = f32[256,128,64]{0,2,1:T(8,128)} copy(f32[256,128,64]{1,2,0:T(8,128)} %fusion.17) | data formatting | bytes 16777216 | tf_op jit(solution)/shard_map/nrp,nrd->npd/dot_general | solution.py:50
  775.7 7.2 fusion.57
  (279 shorter events, 348.1 us)
Async XLA Ops:
  7.2 160.2 %copy-start = (bf16[192,64]{0,1:T(8,128)(2,1)S(1)}, bf16[192,64]{0,1:T(8,128)(2,1)}, u32[]{:S(2)}) copy-start(bf16[192,64]{0,1:T(8,128)(2,1)} %param.30) | copy-start | bytes 73732
  8.0 333.3 %copy-start.18 = (pred[256,128]{1,0:T(8,128)(4,1)}, pred[256,128]{1,0:T(8,128)(4,1)S(1)}, u32[]{:S(2)}) copy-start(pred[256,128]{1,0:T(8,128)(4,1)S(1)} %iota_compare_fusion.14) | copy-start | bytes 98308
  13.7 13.7 %copy-start.31 = (s32[32768]{0:T(1024)S(1)}, s32[32768]{0:T(1024)}, u32[]{:S(2)}) copy-start(s32[32768]{0:T(1024)} %param.29) | copy-start | bytes 393220
  52.8 14.1 %copy-start.17 = (s32[32768]{0:T(1024)S(1)}, s32[32768]{0:T(1024)}, u32[]{:S(2)}) copy-start(s32[32768]{0:T(1024)} %param.26) | copy-start | bytes 393220
  52.8 14.1 %copy-start.9 = (bf16[2048,64]{0,1:T(8,128)(2,1)S(1)}, bf16[2048,64]{0,1:T(8,128)(2,1)}, u32[]{:S(2)}) copy-start(bf16[2048,64]{0,1:T(8,128)(2,1)} %param.24) | copy-start | bytes 786436
  59.3 100.8 %all-to-all-start = ((bf16[8,4096,64]{1,2,0:T(8,128)(2,1)}), bf16[8,4096,64]{1,2,0:T(8,128)(2,1)}, u32[]{:S(2)}, u32[]{:S(2)}) async-start(bf16[8,4096,64]{1,2,0:T(8,128)(2,1)} %copy.58), calls=%async_computation | async-start | bytes 8388608 | tf_op jit(solution)/shard_map/all_to_all | solution.py:150
  167.4 11.5 %copy-start.20 = (bf16[64,64]{1,0:T(8,128)(2,1)S(1)}, bf16[64,64]{1,0:T(8,128)(2,1)}, u32[]{:S(2)}) copy-start(bf16[64,64]{1,0:T(8,128)(2,1)} %param.32) | copy-start | bytes 24580
  167.4 11.5 %copy-start.27 = (f32[64]{0:T(128)S(1)}, f32[64]{0:T(128)}, u32[]{:S(2)}) copy-start(f32[64]{0:T(128)} %param.33) | copy-start | bytes 772
  307.6 9.8 %copy-start.21 = (s32[256]{0:T(256)S(1)}, s32[256]{0:T(256)}, u32[]{:S(2)}) copy-start(s32[256]{0:T(256)} %param.27) | copy-start | bytes 3076
  317.3 7.8 copy-start.23
  317.3 7.8 copy-start.35
  317.3 9.1 %copy-start.22 = (bf16[64,64]{1,0:T(8,128)(2,1)S(1)}, bf16[64,64]{1,0:T(8,128)(2,1)}, u32[]{:S(2)}) copy-start(bf16[64,64]{1,0:T(8,128)(2,1)} %param.38) | copy-start | bytes 24580
  317.3 9.1 %copy-start.30 = (f32[64]{0:T(128)S(1)}, f32[64]{0:T(128)}, u32[]{:S(2)}) copy-start(f32[64]{0:T(128)} %param.39) | copy-start | bytes 772
  317.3 9.4 %copy-start.6 = (bf16[2048,64]{0,1:T(8,128)(2,1)S(1)}, bf16[2048,64]{0,1:T(8,128)(2,1)}, u32[]{:S(2)}) copy-start(bf16[2048,64]{0,1:T(8,128)(2,1)} %param.42) | copy-start | bytes 786436
  317.4 9.4 %copy-start.26 = (f32[64]{0:T(128)S(1)}, f32[64]{0:T(128)}, u32[]{:S(2)}) copy-start(f32[64]{0:T(128)} %param.40) | copy-start | bytes 772
  317.4 10.2 %copy-start.28 = (f32[64]{0:T(128)S(1)}, f32[64]{0:T(128)}, u32[]{:S(2)}) copy-start(f32[64]{0:T(128)} %param.41) | copy-start | bytes 772
  381.4 11.1 %copy-start.8 = (bf16[2048,64]{1,0:T(8,128)(2,1)S(1)}, bf16[2048,64]{1,0:T(8,128)(2,1)}, u32[]{:S(2)}) copy-start(bf16[2048,64]{1,0:T(8,128)(2,1)} %copy-done.7) | copy-start | bytes 786436
  381.4 11.1 %copy-start.13 = (bf16[2048,64]{0,1:T(8,128)(2,1)S(1)}, bf16[2048,64]{0,1:T(8,128)(2,1)}, u32[]{:S(2)}) copy-start(bf16[2048,64]{0,1:T(8,128)(2,1)} %copy-done.12) | copy-start | bytes 786436
  381.4 12.1 %copy-start.11 = (bf16[2048,64]{0,1:T(8,128)(2,1)S(1)}, bf16[2048,64]{0,1:T(8,128)(2,1)}, u32[]{:S(2)}) copy-start(bf16[2048,64]{0,1:T(8,128)(2,1)} %copy-done.10) | copy-start | bytes 786436
  387.9 96.8 %all-to-all-start.2 = ((bf16[8,4096,64]{1,2,0:T(8,128)(2,1)}), bf16[8,4096,64]{1,2,0:T(8,128)(2,1)}, u32[]{:S(2)}, u32[]{:S(2)}) async-start(bf16[8,4096,64]{1,2,0:T(8,128)(2,1)} %copy.69), calls=%async_computation.2 | async-start | bytes 8388608 | tf_op jit(solution)/shard_map/all_to_all | solution.py:184
  484.6 10.8 %slice-start = ((s8[8388608]{0:T(1024)(128)(4,1)}), s8[4194304]{0:T(1024)(128)(4,1)S(1)}, s32[]{:S(2)}) async-start(s8[8388608]{0:T(1024)(128)(4,1)} %bitcast.82), calls=%async_computation.5 | async-start | bytes 8388608
  491.4 5.9 copy-start.2
  497.2 5.8 copy-start.25
  507.9 12.7 %slice-start.2 = ((s8[12582912]{0:T(1024)(128)(4,1)}), s8[4194304]{0:T(1024)(128)(4,1)S(1)}, s32[]{:S(2)}) async-start(s8[12582912]{0:T(1024)(128)(4,1)} %bitcast.86), calls=%async_computation.7 | async-start | bytes 8388608
  513.3 7.2 slice-start.3
  513.3 7.2 slice-start.4
  553.1 185.4 %all-to-all-start.3 = ((bf16[8,4096,64]{1,2,0:T(8,128)(2,1)}), bf16[8,4096,64]{1,2,0:T(8,128)(2,1)}, u32[]{:S(2)}, u32[]{:S(2)}) async-start(bf16[8,4096,64]{1,2,0:T(8,128)(2,1)} %bitcast.91), calls=%async_computation.3 | async-start | bytes 8388608 | tf_op jit(solution)/shard_map/all_to_all | solution.py:203
  557.7 227.9 %all-reduce.3.cloned.1.call-start = ((), (), s32[]{:S(2)}) async-start(), calls=%async_computation.4 | async-start | bytes 335872 | tf_op jit(solution)/shard_map/psum | solution.py:208
  557.7 12.5 %copy-start.14 = (f32[2048,64]{0,1:T(8,128)S(1)}, f32[2048,64]{0,1:T(8,128)}, u32[]{:S(2)}) copy-start(f32[2048,64]{0,1:T(8,128)} %custom-call) | copy-start | bytes 1572868
  738.4 14.2 %copy-start.15 = (f32[2048,64]{0,1:T(8,128)}, f32[2048,64]{0,1:T(8,128)S(1)}, u32[]{:S(2)}) copy-start(f32[2048,64]{0,1:T(8,128)S(1)} %get-tuple-element.71) | copy-start | bytes 1572868
  738.5 14.2 %copy-start.19 = (pred[256,128]{1,0:T(8,128)(4,1)S(1)}, pred[256,128]{1,0:T(8,128)(4,1)}, u32[]{:S(2)}) copy-start(pred[256,128]{1,0:T(8,128)(4,1)} %copy-done.18) | copy-start | bytes 98308
  738.5 14.2 %copy-start.33 = (s32[32768]{0:T(1024)S(1)}, s32[32768]{0:T(1024)}, u32[]{:S(2)}) copy-start(s32[32768]{0:T(1024)} %param.29) | copy-start | bytes 393220
  (13 other events, 48.1 us)
Sparse Core Ops, SparseCore 0:
  570.4 181.9 all-reduce.2
where the time goes:
time: 820 us; the launch traced here: 807 us
  matrix products  359 us (44%)
  local copies, waits for them, and re-layouts  182 us (22%)
  waiting for transfers between devices  98.2 us (12%)
  blocking collectives  96.8 us (12%)
  other arithmetic  38.7 us (5%)
  starting transfers between devices  16.7 us (2%)
  between operations  15 us (2%)
    dot_general x32, matrix products, add_group(): lax.dot_general(onehot, grad_group, (((0,), (0,)), ((), ())), precision=h...  143 us
    all_to_all x1, blocking collectives, per_device(): lax.all_to_all(message_low, 'peer', split_axis=0, concat_axis=0, tiled=True)  96.8 us
    dot_general x36, matrix products, matmul(): return jnp.dot(left_side, right_side, preferred_element_type=jnp.float32)  93.6 us
    all_to_all x1, waiting for transfers between devices, per_device(): lax.all_to_all(message_back, 'peer', split_axis=0, concat_axis=0, tiled=T...  90.3 us
    unnamed x98, local copies, waits for them, and re-layouts  36 us
    dot_general x1, matrix products, from_tiles_wide(): placed = jnp.einsum('nrp,npd->nrd', slot_onehot, picked, precision=highest)  28.1 us
    dot_general x2, matrix products, onto_nodes(): jnp.einsum('nrp,nrd->npd', slot_onehot, block_values, preferred_element_t...  27.6 us
    dynamic_slice x64, local copies, waits for them, and re-layouts, sender_rows(): picked = lax.map(pick_group, send_nodes.reshape(-1, group_rows))  24.8 us
  transfers between devices with their start and end apart: 4, of which 2 were waited for; matrix products, arithmetic and copies ran while one was open for 39% of the time, Pallas kernels for 0%

commit v1 on v0

v1 whole, which is shorter than its diff:
```python
import functools

import jax
import jax.numpy as jnp
from jax import lax
from jax.experimental import pallas as pl
from jax.experimental.pallas import tpu as pltpu
from jax.sharding import PartitionSpec as P

epsilon = 1e-05
bf16 = jnp.bfloat16
f32 = jnp.float32
LANES = 128
WIDE = 256


def dot(left, right):
    return jnp.dot(left, right, preferred_element_type=f32)


def dot_nt(left, right):
    return lax.dot_general(left, right, (((1,), (1,)), ((), ())), preferred_element_type=f32)


def dot_exact(left, right):
    return jnp.dot(left, right, preferred_element_type=f32, precision=lax.Precision.HIGHEST)


def dot_nt_exact(left, right):
    return lax.dot_general(
        left,
        right,
        (((1,), (1,)), ((), ())),
        preferred_element_type=f32,
        precision=lax.Precision.HIGHEST,
    )


def params(limit=56):
    return pltpu.CompilerParams(vmem_limit_bytes=limit * 1024 * 1024)


def spread(column, width):
    return jnp.concatenate([column] * (width // LANES), axis=1)


def fold(values):
    total = values[:, :LANES]
    for start in range(LANES, values.shape[1], LANES):
        total = total + values[:, start : start + LANES]
    return total


def row_join(ref, first, count):
    return jnp.concatenate([ref[first + k : first + k + 1, :] for k in range(count)], axis=1)


def sigmoid(values):
    return 0.5 * jnp.tanh(0.5 * values) + 0.5


def onehot_rows(row, rows):
    width = row.shape[1]
    place = lax.broadcasted_iota(jnp.int32, (rows, width), 0)
    return jnp.where(place == row, 1.0, 0.0).astype(bf16)


def node_groups(node_ref):
    total = node_ref.shape[1]
    return jnp.concatenate(
        [node_ref[:, start : start + WIDE] for start in range(0, total, WIDE)], axis=0
    )


def sender_kernel(piece, node_ref, send_ref, edge_ref, weight_ref, vec_ref, pick_ref, base_ref):
    width = edge_ref.shape[1]
    feat = edge_ref.shape[0]
    groups = node_ref.shape[1] // WIDE
    table = node_groups(node_ref)
    bias = spread(vec_ref[0], piece)
    for start in range(0, width, piece):
        ids = row_join(send_ref, start // LANES, piece // LANES)
        onehot = onehot_rows(ids & (WIDE - 1), WIDE)
        group = lax.shift_right_logical(ids, 8)
        found = dot(table, onehot)
        rows = found[:feat]
        for g in range(1, groups):
            rows = jnp.where(
                jnp.broadcast_to(group == g, (feat, piece)), found[g * feat : (g + 1) * feat], rows
            )
        low = rows.astype(bf16)
        pick_ref[:, start : start + piece] = low
        both = jnp.concatenate([low, edge_ref[:, start : start + piece]], axis=0)
        base_ref[:, start : start + piece] = dot(weight_ref[...], both) + bias


def gather_blocks(meta_ref, first, code_ref, start, count, source_ref):
    feat = source_ref.shape[0]
    parts = []
    for k in range(count):
        block = start + k
        tile = meta_ref[first + block]
        code = code_ref[0, block : block + 1, :]
        index = jnp.broadcast_to(code & (LANES - 1), (feat, LANES))
        rows = source_ref[:, pl.ds(pl.multiple_of(tile * LANES, LANES), LANES)]
        taken = jnp.take_along_axis(rows, index, axis=1)
        parts.append(jnp.where(jnp.broadcast_to(code < LANES, (feat, LANES)), taken, 0.0))
    return jnp.concatenate(parts, axis=1)


def scatter_blocks(meta_ref, first, code_ref, start, count, values, total_ref):
    for k in range(count):
        block = start + k
        tile = meta_ref[first + block]
        onehot = onehot_rows(code_ref[0, block : block + 1, :], LANES)
        term = dot_nt(values[:, k * LANES : (k + 1) * LANES], onehot)
        where_to = pl.ds(pl.multiple_of(tile * LANES, LANES), LANES)
        total_ref[:, where_to] = total_ref[:, where_to] + term


def forward_kernel(peers, blocks, piece, meta_ref, code_ref, base_ref, edge_ref, in_ref, out_ref, vec_ref, *rest):
    shard_refs = rest[:peers]
    result_ref, act_ref, slope_ref, normed_ref, inv_ref, part_ref, proj_ref, total_ref = rest[peers:]
    step = pl.program_id(0)
    inner = pl.program_id(1)

    @pl.when(inner == 0)
    def _():
        for k in range(peers):

            @pl.when(step == k)
            def _():
                proj_ref[...] = dot(in_ref[...], shard_refs[k][...])

        total_ref[...] = jnp.zeros_like(total_ref)

    width = edge_ref.shape[1]
    first = 1 + (meta_ref[0] ^ step) * blocks + inner * (width // LANES)
    bias = spread(vec_ref[1], piece)
    gain = spread(vec_ref[2], piece)
    shift = spread(vec_ref[3], piece)
    per = piece // LANES
    for start in range(0, width, piece):
        lanes = slice(start, start + piece)
        pre = base_ref[:, lanes] + gather_blocks(meta_ref, first, code_ref, start // LANES, per, proj_ref)
        sig = sigmoid(pre)
        act = pre * sig
        slope_ref[:, lanes] = (sig + act * (1.0 - sig)).astype(bf16)
        act_low = act.astype(bf16)
        act_ref[:, lanes] = act_low
        second = dot(out_ref[...], act_low) + bias
        centered = second - jnp.mean(second, axis=0, keepdims=True)
        inv = lax.rsqrt(jnp.mean(centered * centered, axis=0, keepdims=True) + epsilon)
        normed = centered * inv
        normed_ref[:, lanes] = normed.astype(bf16)
        for k in range(per):
            inv_ref[start // LANES + k : start // LANES + k + 1, :] = inv[:, k * LANES : (k + 1) * LANES]
        message = (normed * gain + shift).astype(bf16)
        result_ref[:, lanes] = (edge_ref[:, lanes].astype(f32) + message.astype(f32)).astype(bf16)
        scatter_blocks(meta_ref, first, code_ref, start // LANES, per, message, total_ref)

    @pl.when(inner == pl.num_programs(1) - 1)
    def _():
        part_ref[0] = total_ref[...].astype(bf16)


def node_kernel(peers, node_ref, cot_ref, in_t_ref, in_ref, out_t_ref, out_ref, vec_ref, *rest):
    part_refs = rest[:peers]
    result_ref, base_ref, back_ref, pack_ref = rest[peers:]
    feat, total = node_ref.shape
    aggregate = part_refs[0][...].astype(f32)
    for k in range(1, peers):
        aggregate = aggregate + part_refs[k][...].astype(f32)
    node_inputs = jnp.concatenate([node_ref[...], aggregate.astype(bf16)], axis=0)
    pre = dot(in_t_ref[...], node_inputs) + spread(vec_ref[4], total)
    sig = sigmoid(pre)
    act = pre * sig
    slope = sig + act * (1.0 - sig)
    act_low = act.astype(bf16)
    second = dot(out_t_ref[...], act_low) + spread(vec_ref[5], total)
    centered = second - jnp.mean(second, axis=0, keepdims=True)
    inv = lax.rsqrt(jnp.mean(centered * centered, axis=0, keepdims=True) + epsilon)
    normed = centered * inv
    gain = spread(vec_ref[6], total)
    update = normed * gain + spread(vec_ref[7], total)
    result_ref[...] = (node_ref[...].astype(f32) + update).astype(bf16)
    upstream = cot_ref[...].astype(f32)
    scaled = upstream * gain
    inner = (
        scaled
        - jnp.mean(scaled, axis=0, keepdims=True)
        - normed * jnp.mean(scaled * normed, axis=0, keepdims=True)
    )
    grad = (inner * inv).astype(bf16)
    third = (dot(out_ref[...], grad) * slope).astype(bf16)
    input_grad = dot(in_ref[...], third)
    base_ref[...] = upstream + input_grad[:feat]
    back_ref[...] = input_grad[feat:].astype(bf16)
    pack_ref[...] = jnp.zeros_like(pack_ref)
    pack_ref[:feat, : 2 * feat] = dot_nt(third, node_inputs)
    pack_ref[:feat, 2 * feat : 3 * feat] = dot_nt(act_low, grad)
    ones = jnp.ones((8, LANES), f32)
    sums = (
        fold(third.astype(f32)),
        fold(grad.astype(f32)),
        fold(upstream * normed),
        fold(upstream),
    )
    for k in range(4):
        pack_ref[feat + k : feat + k + 1, :feat] = dot_nt_exact(ones, sums[k])[:1]


def backward_kernel(peers, blocks, piece, meta_ref, code_ref, cot_ref, normed_ref, act_ref, slope_ref, inv_ref, edge_ref, pick_ref, out_ref, in_ref, vec_ref, *rest):
    back_refs = rest[:peers]
    shard_refs = rest[peers : 2 * peers]
    grad_ref, first_ref, part_ref, pack_ref, pull_ref, total_ref, w1_ref, wr_ref, w2_ref, sum_ref = rest[2 * peers :]
    step = pl.program_id(0)
    inner = pl.program_id(1)
    feat, width = edge_ref.shape

    @pl.when((inner == 0) & (step == 0))
    def _():
        w1_ref[...] = jnp.zeros_like(w1_ref)
        wr_ref[...] = jnp.zeros_like(wr_ref)
        w2_ref[...] = jnp.zeros_like(w2_ref)
        sum_ref[...] = jnp.zeros_like(sum_ref)

    @pl.when(inner == 0)
    def _():
        for k in range(peers):

            @pl.when(step == k)
            def _():
                pull_ref[...] = back_refs[k][...].astype(f32)

        total_ref[...] = jnp.zeros_like(total_ref)

    first = 1 + (meta_ref[0] ^ step) * blocks + inner * (width // LANES)
    gain = spread(vec_ref[2], piece)
    per = piece // LANES
    for start in range(0, width, piece):
        lanes = slice(start, start + piece)
        cot = cot_ref[:, lanes].astype(f32)
        upstream = cot + gather_blocks(meta_ref, first, code_ref, start // LANES, per, pull_ref)
        normed = normed_ref[:, lanes].astype(f32)
        scaled = upstream * gain
        inner_grad = (
            scaled
            - jnp.mean(scaled, axis=0, keepdims=True)
            - normed * jnp.mean(scaled * normed, axis=0, keepdims=True)
        )
        inv = row_join(inv_ref, start // LANES, per)
        second = (inner_grad * inv).astype(bf16)
        sum_ref[2] += fold(upstream * normed)
        sum_ref[3] += fold(upstream)
        sum_ref[1] += fold(second.astype(f32))
        w2_ref[...] += dot_nt(act_ref[:, lanes], second)
        grad = (dot(out_ref[...], second) * slope_ref[:, lanes].astype(f32)).astype(bf16)
        first_ref[:, lanes] = grad
        sum_ref[0] += fold(grad.astype(f32))
        grad_ref[:, lanes] = cot + dot(in_ref[...], grad)
        both = jnp.concatenate([pick_ref[:, lanes], edge_ref[:, lanes]], axis=0)
        w1_ref[...] += dot_nt(grad, both)
        scatter_blocks(meta_ref, first, code_ref, start // LANES, per, grad, total_ref)

    @pl.when(inner == pl.num_programs(1) - 1)
    def _():
        low = total_ref[...].astype(bf16)
        part_ref[0] = low
        for k in range(peers):

            @pl.when(step == k)
            def _():
                wr_ref[...] += dot_nt(low, shard_refs[k][...])

    @pl.when((inner == pl.num_programs(1) - 1) & (step == pl.num_programs(0) - 1))
    def _():
        pack_ref[...] = jnp.zeros_like(pack_ref)
        pack_ref[:feat, :feat] = w1_ref[:, :feat]
        pack_ref[:feat, feat : 2 * feat] = wr_ref[...]
        pack_ref[:feat, 2 * feat : 3 * feat] = w1_ref[:, feat:]
        pack_ref[:feat, 3 * feat : 4 * feat] = w2_ref[...]
        ones = jnp.ones((8, LANES), f32)
        for k in range(4):
            pack_ref[feat + k : feat + k + 1, :feat] = dot_nt_exact(ones, sum_ref[k])[:1]


def sender_sum_kernel(grad_ref, send_ref, sum_ref, total_ref):
    feat, width = grad_ref.shape
    groups = sum_ref.shape[1] // WIDE

    @pl.when(pl.program_id(0) == 0)
    def _():
        total_ref[...] = jnp.zeros_like(total_ref)

    ids = row_join(send_ref, 0, width // LANES)
    onehot = onehot_rows(ids & (WIDE - 1), WIDE)
    group = jnp.broadcast_to(lax.shift_right_logical(ids, 8).astype(bf16), (feat, width))
    values = grad_ref[...]
    zero = jnp.zeros((), bf16)
    masked = jnp.concatenate(
        [jnp.where(group == jnp.asarray(g, bf16), values, zero) for g in range(groups)], axis=0
    )
    total_ref[...] += dot_nt(masked, onehot)

    @pl.when(pl.program_id(0) == pl.num_programs(0) - 1)
    def _():
        for g in range(groups):
            sum_ref[:, g * WIDE : (g + 1) * WIDE] = total_ref[g * feat : (g + 1) * feat, :]


def finish_kernel(peers, base_ref, sum_ref, weight_ref, node_pack_ref, edge_pack_ref, *rest):
    part_refs = rest[:peers]
    grad_ref, e1, b1, e2, b2, g1, s1, n1, c1, n2, c2, g2, s2 = rest[peers:]
    total = part_refs[0][...].astype(f32)
    for k in range(1, peers):
        total = total + part_refs[k][...].astype(f32)
    both = jnp.concatenate([sum_ref[...], total], axis=0)
    grad_ref[...] = base_ref[...] + dot_exact(weight_ref[...], both)
    feat = base_ref.shape[0]
    e1[...] = edge_pack_ref[:feat, : 3 * feat]
    e2[...] = edge_pack_ref[:feat, 3 * feat : 4 * feat]
    n1[...] = node_pack_ref[:feat, : 2 * feat]
    n2[...] = node_pack_ref[:feat, 2 * feat : 3 * feat]
    for k, ref in enumerate((b1, b2, g1, s1)):
        ref[...] = edge_pack_ref[feat + k : feat + k + 1, :feat]
    for k, ref in enumerate((c1, c2, g2, s2)):
        ref[...] = node_pack_ref[feat + k : feat + k + 1, :feat]


def struct(shape, dtype):
    return jax.ShapeDtypeStruct(shape, dtype)


def whole(shape):
    return pl.BlockSpec(shape, lambda *_: (0,) * len(shape))


def per_device(groups, peers, *arrays):
    (
        nodes, edges, send_nodes, block_tile, block_count, slot_ids,
        edge_in_weight, edge_in_bias, edge_out_weight, edge_out_bias, edge_gain, edge_shift,
        node_in_weight, node_in_bias, node_out_weight, node_out_bias, node_gain, node_shift,
        node_cot, edge_cot,
    ) = arrays
    feat = nodes.shape[1]
    node_total = nodes.shape[0]
    edge_total = edges.shape[0]
    block_total = block_tile.shape[0]
    blocks = block_total // peers
    per_peer = edge_total // peers
    rows = edge_total // LANES

    def swap(value, mask):
        if mask == 0:
            return value
        return lax.ppermute(value, "peer", [(i, i ^ mask) for i in range(peers)])

    def spread_out(value):
        return [swap(value, mask) for mask in range(peers)]

    def add_up(value):
        for axis, size in (("peer", peers), ("grp", groups)):
            mask = 1
            while mask < size:
                value = value + lax.ppermute(value, axis, [(i, i ^ mask) for i in range(size)])
                mask *= 2
        return value

    node_t = nodes.T
    edge_t = edges.T
    node_cot_t = node_cot.T
    edge_cot_t = edge_cot.T
    in_t = edge_in_weight.T
    send = send_nodes.reshape(rows, LANES)
    me = lax.axis_index("peer").astype(jnp.int32)

    shards = spread_out(node_t)

    live = jnp.arange(LANES, dtype=jnp.int32)[None, :] < block_count[:, None]
    code = slot_ids.reshape(block_total, LANES) + jnp.where(live, 0, LANES) + 2 * LANES * block_tile[:, None]
    code = lax.all_to_all(code, "peer", 0, 0, tiled=True)
    meta = jnp.concatenate([me[None], code[:, 0] // (2 * LANES)])
    code = (code & (2 * LANES - 1)).reshape(peers, blocks, LANES)

    vec = jnp.broadcast_to(
        jnp.stack([edge_in_bias, edge_out_bias, edge_gain, edge_shift, node_in_bias, node_out_bias, node_gain, node_shift])[:, :, None],
        (8, feat, LANES),
    )
    se_weight = jnp.concatenate([in_t[:, :feat], in_t[:, 2 * feat :]], axis=1)

    wide = 1024
    pick, base = pl.pallas_call(
        functools.partial(sender_kernel, 512),
        grid=(edge_total // wide,),
        in_specs=[
            whole((feat, node_total)),
            pl.BlockSpec((wide // LANES, LANES), lambda i: (i, 0)),
            pl.BlockSpec((feat, wide), lambda i: (0, i)),
            whole((feat, 2 * feat)),
            whole((8, feat, LANES)),
        ],
        out_specs=[
            pl.BlockSpec((feat, wide), lambda i: (0, i)),
            pl.BlockSpec((feat, wide), lambda i: (0, i)),
        ],
        out_shape=[struct((feat, edge_total), bf16), struct((feat, edge_total), f32)],
        compiler_params=params(),
        name="sender",
    )(node_t, send, edge_t, se_weight, vec)

    wide = min(1024, per_peer)
    chunks = per_peer // wide
    sub = wide // LANES

    def at(i, j, meta_ref):
        return (0, (meta_ref[0] ^ i) * chunks + j)

    def row_at(i, j, meta_ref):
        return ((meta_ref[0] ^ i) * chunks + j, 0)

    def code_at(i, j, meta_ref):
        return (meta_ref[0] ^ i, j, 0)

    slab = pl.BlockSpec((feat, wide), at)
    code_spec = pl.BlockSpec((1, sub, LANES), code_at)
    inv_spec = pl.BlockSpec((sub, LANES), row_at)
    shard_spec = whole((feat, node_total))
    part_spec = pl.BlockSpec((1, feat, node_total), lambda i, j, meta_ref: (i, 0, 0))
    edge_result, act, slope, normed, inv, part = pl.pallas_call(
        functools.partial(forward_kernel, peers, blocks, 512),
        grid_spec=pltpu.PrefetchScalarGridSpec(
            num_scalar_prefetch=1,
            grid=(peers, chunks),
            in_specs=[code_spec, slab, slab, whole((feat, feat)), whole((feat, feat)), whole((8, feat, LANES))]
            + [shard_spec] * peers,
            out_specs=[slab, slab, slab, slab, inv_spec, part_spec],
            scratch_shapes=[pltpu.VMEM((feat, node_total), f32), pltpu.VMEM((feat, node_total), f32)],
        ),
        out_shape=[
            struct((feat, edge_total), bf16),
            struct((feat, edge_total), bf16),
            struct((feat, edge_total), bf16),
            struct((feat, edge_total), bf16),
            struct((rows, LANES), f32),
            struct((peers, feat, node_total), bf16),
        ],
        compiler_params=params(),
        name="forward",
    )(meta, code, base, edge_t, in_t[:, feat : 2 * feat], edge_out_weight.T, vec, *shards)

    parts = [swap(part[mask], mask) for mask in range(peers)]
    node_result, node_base, back, node_pack = pl.pallas_call(
        functools.partial(node_kernel, peers),
        out_shape=[
            struct((feat, node_total), bf16),
            struct((feat, node_total), f32),
            struct((feat, node_total), bf16),
            struct((feat + 8, 4 * feat), f32),
        ],
        compiler_params=params(),
        name="node",
    )(node_t, node_cot_t, node_in_weight.T, node_in_weight, node_out_weight.T, node_out_weight, vec, *parts)

    backs = spread_out(back)
    node_pack = add_up(node_pack)

    edge_grad, first_grad, part, edge_pack = pl.pallas_call(
        functools.partial(backward_kernel, peers, blocks, 512),
        grid_spec=pltpu.PrefetchScalarGridSpec(
            num_scalar_prefetch=1,
            grid=(peers, chunks),
            in_specs=[code_spec, slab, slab, slab, slab, inv_spec, slab, slab, whole((feat, feat)), whole((feat, feat)), whole((8, feat, LANES))]
            + [shard_spec] * (2 * peers),
            out_specs=[slab, slab, part_spec, whole((feat + 8, 4 * feat))],
            scratch_shapes=[
                pltpu.VMEM((feat, node_total), f32),
                pltpu.VMEM((feat, node_total), f32),
                pltpu.VMEM((feat, 2 * feat), f32),
                pltpu.VMEM((feat, feat), f32),
                pltpu.VMEM((feat, feat), f32),
                pltpu.VMEM((4, feat, LANES), f32),
            ],
        ),
        out_shape=[
            struct((feat, edge_total), f32),
            struct((feat, edge_total), bf16),
            struct((peers, feat, node_total), bf16),
            struct((feat + 8, 4 * feat), f32),
        ],
        compiler_params=params(),
        name="backward",
    )(meta, code, edge_cot_t, normed, act, slope, inv, edge_t, pick, edge_out_weight, edge_in_weight[2 * feat :], vec, *backs, *shards)

    parts = [swap(part[mask], mask) for mask in range(peers)]
    edge_pack = add_up(edge_pack)

    wide = 2048
    send_sum = pl.pallas_call(
        sender_sum_kernel,
        grid=(edge_total // wide,),
        in_specs=[
            pl.BlockSpec((feat, wide), lambda i: (0, i)),
            pl.BlockSpec((wide // LANES, LANES), lambda i: (i, 0)),
        ],
        out_specs=whole((feat, node_total)),
        out_shape=struct((feat, node_total), f32),
        scratch_shapes=[pltpu.VMEM((node_total // WIDE * feat, WIDE), f32)],
        compiler_params=params(),
        name="sender_sum",
    )(first_grad, send)

    vec_out = struct((1, feat), f32)
    sr_weight = jnp.concatenate([edge_in_weight[:feat], edge_in_weight[feat : 2 * feat]], axis=1).astype(f32)
    node_grad, e1, b1, e2, b2, g1, s1, n1, c1, n2, c2, g2, s2 = pl.pallas_call(
        functools.partial(finish_kernel, peers),
        out_shape=[
            struct((feat, node_total), f32),
            struct((feat, 3 * feat), f32), vec_out, struct((feat, feat), f32), vec_out, vec_out, vec_out,
            struct((feat, 2 * feat), f32), vec_out, struct((feat, feat), f32), vec_out, vec_out, vec_out,
        ],
        compiler_params=params(),
        name="finish",
    )(node_base, send_sum, sr_weight, node_pack, edge_pack, *parts)

    def flat(row):
        return row.reshape(feat)

    return (
        node_result.T, edge_result.T, node_grad.T, edge_grad.T,
        e1.T, flat(b1), e2, flat(b2), flat(g1), flat(s1),
        n1.T, flat(c1), n2, flat(c2), flat(g2), flat(s2),
    )


def solution(mesh):
    split = P(("grp", "peer"), None)
    line = P(("grp", "peer"))
    one = P()
    return jax.shard_map(
        functools.partial(per_device, mesh.shape["grp"], mesh.shape["peer"]),
        mesh=mesh,
        in_specs=(split, split, line, line, line, line) + (one,) * 12 + (split, split),
        out_specs=(split, split, split, split) + (one,) * 12,
        check_vma=False,
    )
```

time: 820 us -> 323 us (0.39); the launches traced: 807 us -> 320 us
  matrix products: 359 us -> 0 us
  local copies, waits for them, and re-layouts: 182 us -> 15.7 us
  Pallas kernels: 0 us -> 133 us
  blocking collectives: 96.8 us -> 0 us
  starting transfers between devices: 16.7 us -> 96.4 us
  waiting for transfers between devices: 98.2 us -> 66.2 us
  other arithmetic: 38.7 us -> 7.33 us
  between operations: 15 us -> 1.01 us
    dot_general x84 -> x0, matrix products: 359 us -> none  [the longest x32 143 us: add_group(): lax.dot_general(onehot, grad_group, (((0,), (0,)), ((), ())), precision=h...]
    pallas_call x0 -> x6, Pallas kernels: none -> 133 us  [the longest x1 44.1 us: per_device(): pl.pallas_call(functools.partial(backward_kernel, peers, blocks, 512), gr...]
    all_to_all x3 -> x1, waiting for transfers between devices: 98.2 us -> 0.82 us  [per_device(): code = lax.all_to_all(code, 'peer', 0, 0, tiled=True)]
    all_to_all x1 -> x0, blocking collectives: 96.8 us -> none  [per_device(): lax.all_to_all(message_low, 'peer', split_axis=0, concat_axis=0, tiled=True)]
    ppermute x0 -> x38, starting transfers between devices: none -> 92.2 us  [the longest x28 83.2 us: swap(): return lax.ppermute(value, 'peer', [(i, i ^ mask) for i in range(peers)])]
    ppermute x0 -> x38, waiting for transfers between devices: none -> 65.3 us  [the longest x28 38.7 us: swap(): return lax.ppermute(value, 'peer', [(i, i ^ mask) for i in range(peers)])]
    convert_element_type x7 -> x0, local copies, waits for them, and re-layouts: 34.2 us -> none  [the longest x3 18.4 us: per_device(): from_tiles_wide(aggregate_grad, tile_pick, slot_wide).astype(jnp.bfloat16)]
    all_to_all x7 -> x0, local copies, waits for them, and re-layouts: 30.2 us -> none  [the longest x3 16.4 us: per_device(): lax.all_to_all(outgoing, 'peer', split_axis=0, concat_axis=0, tiled=True)]
  transfers between devices with their start and end apart: 4 -> 39, of which waited for: 2 -> 19; matrix products, arithmetic and copies ran while one was open for 39% -> 5% of each run, Pallas kernels for 0% -> 28%
where the time goes in v1:
time: 323 us; the launch traced here: 320 us
  Pallas kernels  133 us (41%)
  starting transfers between devices  96.4 us (30%)
  waiting for transfers between devices  66.2 us (20%)
  local copies, waits for them, and re-layouts  15.7 us (5%)
  other arithmetic  7.33 us (2%)
    ppermute x28, starting transfers between devices, swap(): return lax.ppermute(value, 'peer', [(i, i ^ mask) for i in range(peers)])  83.2 us
    pallas_call x1, Pallas kernels, per_device(): pl.pallas_call(functools.partial(backward_kernel, peers, blocks, 512), gr...  44.1 us
    ppermute x28, waiting for transfers between devices, swap(): return lax.ppermute(value, 'peer', [(i, i ^ mask) for i in range(peers)])  38.7 us
    pallas_call x1, Pallas kernels, per_device(): pl.pallas_call(functools.partial(forward_kernel, peers, blocks, 512), gri...  35.6 us
    pallas_call x1, Pallas kernels, per_device(): pl.pallas_call(functools.partial(sender_kernel, 512), grid=(edge_total //...  30.6 us
    ppermute x10, waiting for transfers between devices, add_up(): lax.ppermute(value, axis, [(i, i ^ mask) for i in range(size)])  26.6 us
    pallas_call x1, Pallas kernels, per_device(): pl.pallas_call(sender_sum_kernel, grid=(edge_total // wide,), in_specs=[p...  15.5 us
    ppermute x10, starting transfers between devices, add_up(): lax.ppermute(value, axis, [(i, i ^ mask) for i in range(size)])  8.98 us
  transfers between devices with their start and end apart: 39, of which 19 were waited for; matrix products, arithmetic and copies ran while one was open for 5% of the time, Pallas kernels for 28%

profile of v1, /device:TPU:0, one launch (start us, length us, event | category | flops | bytes accessed | tf_op | source)
XLA Modules:
  0.0 320.1 jit_solution(12414311885210794321)
XLA Ops:
  0.7 6.1 %collective-permute-start.6 = (bf16[64,2048]{1,0:T(8,128)(2,1)}, bf16[64,2048]{1,0:T(8,128)(2,1)S(1)}, u32[]{:S(2)}, u32[]{:S(2)}) collective-permute-start(bf16[64,2048]{1,0:T(8,128)(2,1)} %bitcast.71), channel_id=1, source_target_pairs={{0,7},{1,6},{2,5},{3,4},{4,3},{5,2},{6,1},{7,0},{8,15},{9,14},{10,... | collective-permute-start | bytes 786440 | tf_op jit(solution)/shard_map/ppermute | solution.py:357
  9.7 2.3 collective-permute-start.2
  15.2 4.2 %all-to-all-start = ((s32[8,32,128]{2,1,0:T(8,128)}), s32[8,32,128]{2,1,0:T(8,128)S(1)}, u32[]{:S(2)}, u32[]{:S(2)}) async-start(s32[8,32,128]{2,1,0:T(8,128)} %add_add_fusion), calls=%async_computation | async-start | bytes 262144 | tf_op jit(solution)/shard_map/all_to_all | solution.py:382
  24.6 30.6 %sender.1 = (bf16[64,32768]{1,0:T(8,128)(2,1)}, f32[64,32768]{1,0:T(8,128)}) custom-call(bf16[64,2048]{1,0:T(8,128)(2,1)} %bitcast.76, s32[256,128]{1,0:T(8,128)} %bitcast.84, bf16[64,32768]{1,0:T(8,128)(2,1)} %bitcast.68, bf16[64,128]{1,0:T(8,128)(2,1)} %pad_maximum_fusion.weight_ref, f32[8,64,128]{2,1,0:T(8,128)} %broadcast_in_dim.20.vec_ref), custom_call_target="tpu_custom_call" | custom-call | tf_op jit(solution)/shard_map/sender/pallas_call | solution.py:393
  60.2 3.4 %collective-permute-done.1.rest_2_.rest_10_ = bf16[64,2048]{1,0:T(8,128)(2,1)S(1)} collective-permute-done((bf16[64,2048]{1,0:T(8,128)(2,1)S(1)}, bf16[64,2048]{1,0:T(8,128)(2,1)S(1)}, u32[]{:S(2)}, u32[]{:S(2)}) %collective-permute-start.1) | collective-permute-done | bytes 262176 | tf_op jit(solution)/shard_map/ppermute | solution.py:357
  64.5 35.6 %forward.1 = (bf16[64,32768]{1,0:T(8,128)(2,1)}, bf16[64,32768]{1,0:T(8,128)(2,1)}, bf16[64,32768]{1,0:T(8,128)(2,1)}, bf16[64,32768]{1,0:T(8,128)(2,1)}, f32[25...) custom-call(s32[257]{0:T(512)} %pad_add_fusion.meta_ref, s32[8,32,128]{2,1,0:T(8,128)} %broadcast_and_fusion.code_ref, ...), custom_call_target="tpu_custom_call" | custom-call | tf_op jit(solution)/shard_map/forward/pallas_call | solution.py:430
  100.1 2.4 slice_bitcast_fusion.8
  102.5 3.3 %collective-permute-start.13 = (bf16[64,2048]{1,0:T(8,128)(2,1)S(1)}, bf16[64,2048]{1,0:T(8,128)(2,1)S(1)}, u32[]{:S(2)}, u32[]{:S(2)}) collective-permute-start(bf16[64,2048]{1,0:T(8,128)(2,1)S(1)} %get-tuple-element.82), channel_id=1, source_target_pairs={{0,7},{1,6},{2,5},{3,4},{4,3},{5,2},{6,1},{7,0},{8,15},{9,14},{10,... | collective-permute-start | bytes 786440 | tf_op jit(solution)/shard_map/ppermute | solution.py:357
  107.8 2.3 collective-permute-start.10
  111.0 3.5 %collective-permute-done.13.rest_7_ = bf16[64,2048]{1,0:T(8,128)(2,1)S(1)} collective-permute-done((bf16[64,2048]{1,0:T(8,128)(2,1)S(1)}, bf16[64,2048]{1,0:T(8,128)(2,1)S(1)}, u32[]{:S(2)}, u32[]{:S(2)}) %collective-permute-start.13) | collective-permute-done | bytes 262176 | tf_op jit(solution)/shard_map/ppermute | solution.py:357
  114.5 21.4 %collective-permute-start.8 = (bf16[64,2048]{1,0:T(8,128)(2,1)S(1)}, bf16[64,2048]{1,0:T(8,128)(2,1)S(1)}, u32[]{:S(2)}, u32[]{:S(2)}) collective-permute-start(bf16[64,2048]{1,0:T(8,128)(2,1)S(1)} %get-tuple-element.87), channel_id=1, source_target_pairs={{0,2},{1,3},{2,0},{3,1},{4,6},{5,7},{6,4},{7,5},{8,10},{9,11},{10,... | collective-permute-start | bytes 786440 | tf_op jit(solution)/shard_map/ppermute | solution.py:357
  137.8 8.3 %collective-permute-done.11.rest_5_ = bf16[64,2048]{1,0:T(8,128)(2,1)S(1)} collective-permute-done((bf16[64,2048]{1,0:T(8,128)(2,1)S(1)}, bf16[64,2048]{1,0:T(8,128)(2,1)S(1)}, u32[]{:S(2)}, u32[]{:S(2)}) %collective-permute-start.11) | collective-permute-done | bytes 262176 | tf_op jit(solution)/shard_map/ppermute | solution.py:357
  146.0 3.2 %collective-permute-done.10.rest_4_ = bf16[64,2048]{1,0:T(8,128)(2,1)S(1)} collective-permute-done((bf16[64,2048]{1,0:T(8,128)(2,1)S(1)}, bf16[64,2048]{1,0:T(8,128)(2,1)S(1)}, u32[]{:S(2)}, u32[]{:S(2)}) %collective-permute-start.10) | collective-permute-done | bytes 262176 | tf_op jit(solution)/shard_map/ppermute | solution.py:357
  149.3 2.2 collective-permute-done.8.rest_2_
  152.3 4.2 %node.1 = (bf16[64,2048]{1,0:T(8,128)(2,1)}, f32[64,2048]{1,0:T(8,128)}, bf16[64,2048]{1,0:T(8,128)(2,1)}, f32[72,256]{1,0:T(8,128)}) custom-call(bf16[64,2048]{1,0:T(8,128)(2,1)} %bitcast.78, bf16[64,2048]{1,0:T(8,128)(2,1)} %bitcast.87, bf16[64,128]{1,0:T(8,128)(2,1)} %bitcast.89, bf16[128,64]{1,0:T(8,128)(2,1)} %copy.45.in_ref, bf16[64,64]{1,0:T(8,128)(2,1)} %bitcast.90, ...), custom_call_target="tpu_custom_call" | custom-call | tf_op jit(solution)/shard_map/node/pallas_call | solution.py:453
  156.5 3.3 %collective-permute-start.20 = (bf16[64,2048]{1,0:T(8,128)(2,1)}, bf16[64,2048]{1,0:T(8,128)(2,1)S(1)}, u32[]{:S(2)}, u32[]{:S(2)}) collective-permute-start(bf16[64,2048]{1,0:T(8,128)(2,1)} %get-tuple-element.55.rest_0_), channel_id=1, source_target_pairs={{0,7},{1,6},{2,5},{3,4},{4,3},{5,2},{6,1},{7,0},{8,15},{9,14},{10,... | collective-permute-start | bytes 786440 | tf_op jit(solution)/shard_map/ppermute | solution.py:357
  160.2 3.9 %collective-permute-start.17 = (bf16[64,2048]{1,0:T(8,128)(2,1)}, bf16[64,2048]{1,0:T(8,128)(2,1)S(1)}, u32[]{:S(2)}, u32[]{:S(2)}) collective-permute-start(bf16[64,2048]{1,0:T(8,128)(2,1)} %get-tuple-element.55.rest_0_), channel_id=1, source_target_pairs={{0,4},{1,5},{2,6},{3,7},{4,0},{5,1},{6,2},{7,3},{8,12},{9,13},{10,... | collective-permute-start | bytes 786440 | tf_op jit(solution)/shard_map/ppermute | solution.py:357
  165.1 3.5 %collective-permute-done.20.rest_7_ = bf16[64,2048]{1,0:T(8,128)(2,1)S(1)} collective-permute-done((bf16[64,2048]{1,0:T(8,128)(2,1)}, bf16[64,2048]{1,0:T(8,128)(2,1)S(1)}, u32[]{:S(2)}, u32[]{:S(2)}) %collective-permute-start.20) | collective-permute-done | bytes 262176 | tf_op jit(solution)/shard_map/ppermute | solution.py:357
  168.6 20.2 %collective-permute-start.15 = (bf16[64,2048]{1,0:T(8,128)(2,1)}, bf16[64,2048]{1,0:T(8,128)(2,1)S(1)}, u32[]{:S(2)}, u32[]{:S(2)}) collective-permute-start(bf16[64,2048]{1,0:T(8,128)(2,1)} %get-tuple-element.55.rest_0_), channel_id=1, source_target_pairs={{0,2},{1,3},{2,0},{3,1},{4,6},{5,7},{6,4},{7,5},{8,10},{9,11},{10,... | collective-permute-start | bytes 786440 | tf_op jit(solution)/shard_map/ppermute | solution.py:357
  190.3 8.5 %collective-permute-done.18.rest_5_ = bf16[64,2048]{1,0:T(8,128)(2,1)S(1)} collective-permute-done((bf16[64,2048]{1,0:T(8,128)(2,1)}, bf16[64,2048]{1,0:T(8,128)(2,1)S(1)}, u32[]{:S(2)}, u32[]{:S(2)}) %collective-permute-start.18) | collective-permute-done | bytes 262176 | tf_op jit(solution)/shard_map/ppermute | solution.py:357
  203.4 44.1 %backward.1 = (f32[64,32768]{1,0:T(8,128)}, bf16[64,32768]{1,0:T(8,128)(2,1)}, bf16[8,64,2048]{2,1,0:T(8,128)(2,1)}, f32[72,256]{1,0:T(8,128)}) custom-call(s32[257]{0:T(512)} %pad_add_fusion.meta_ref, s32[8,32,128]{2,1,0:T(8,128)} %broadcast_and_fusion.code_ref, bf16[64,32768]{1,0:T(8,128)(2,1)} %bitcast.82, ...), custom_call_target="tpu_custom_call" | custom-call | tf_op jit(solution)/shard_map/backward/pallas_call | solution.py:468
  249.6 2.6 collective-permute-done.26
  253.2 2.5 slice_bitcast_fusion
  255.6 2.7 collective-permute-start.37
  258.3 2.5 collective-permute-start.36
  261.0 3.9 %collective-permute-start.28 = (f32[72,256]{1,0:T(8,128)S(1)}, f32[72,256]{1,0:T(8,128)S(1)}, u32[]{:S(2)}, u32[]{:S(2)}) collective-permute-start(f32[72,256]{1,0:T(8,128)S(1)} %add.56), channel_id=1, source_target_pairs={{0,4},{1,5},{2,6},{3,7},{4,0},{5,1},{6,2},{7,3},{8,12},{9,13},{10,... | collective-permute-start | bytes 221192 | tf_op jit(solution)/shard_map/ppermute | solution.py:366
  264.9 19.4 %collective-permute-done.23 = f32[72,256]{1,0:T(8,128)S(1)} collective-permute-done((f32[72,256]{1,0:T(8,128)S(1)}, f32[72,256]{1,0:T(8,128)S(1)}, u32[]{:S(2)}, u32[]{:S(2)}) %collective-permute-start.23) | collective-permute-done | bytes 73760 | tf_op jit(solution)/shard_map/ppermute | solution.py:366
  287.8 3.0 collective-permute-done.25
  290.9 3.4 %collective-permute-start.33 = (bf16[64,2048]{1,0:T(8,128)(2,1)S(1)}, bf16[64,2048]{1,0:T(8,128)(2,1)S(1)}, u32[]{:S(2)}, u32[]{:S(2)}) collective-permute-start(bf16[64,2048]{1,0:T(8,128)(2,1)S(1)} %get-tuple-element.78), channel_id=1, source_target_pairs={{0,3},{1,2},{2,1},{3,0},{4,7},{5,6},{6,5},{7,4},{8,11},{9,10},{10,... | collective-permute-start | bytes 786440 | tf_op jit(solution)/shard_map/ppermute | solution.py:357
  295.8 15.5 %sender_sum.1.sum_ref = f32[64,2048]{1,0:T(8,128)} custom-call(bf16[64,32768]{1,0:T(8,128)(2,1)} %get-tuple-element.56.grad_ref, s32[256,128]{1,0:T(8,128)} %bitcast.85), custom_call_target="tpu_custom_call" | custom-call | tf_op jit(solution)/shard_map/sender_sum/pallas_call | solution.py:499
  313.0 2.7 collective-permute-done.32.rest_2_
  316.5 3.5 %finish.1 = (f32[64,2048]{1,0:T(8,128)}, f32[64,192]{1,0:T(8,128)}, f32[1,64]{1,0:T(1,128)}, f32[64,64]{1,0:T(8,128)}, f32[1,64]{1,0:T(1,128)}, /*index=5*/f32[1...) custom-call(f32[64,2048]{1,0:T(8,128)} %get-tuple-element.49.base_re, ...), custom_call_target="tpu_custom_call" | custom-call | tf_op jit(solution)/shard_map/finish/pallas_call | solution.py:515
  (150 shorter events, 41.0 us)
Async XLA Ops:
  0.7 55.4 %collective-permute-start.6 = (bf16[64,2048]{1,0:T(8,128)(2,1)}, bf16[64,2048]{1,0:T(8,128)(2,1)S(1)}, u32[]{:S(2)}, u32[]{:S(2)}) collective-permute-start(bf16[64,2048]{1,0:T(8,128)(2,1)} %bitcast.71), channel_id=1, source_target_pairs={{0,7},{1,6},{2,5},{3,4},{4,3},{5,2},{6,1},{7,0},{8,15},{9,14},{10,... | collective-permute-start | bytes 786440 | tf_op jit(solution)/shard_map/ppermute | solution.py:357
  6.7 50.7 %collective-permute-start.5 = (bf16[64,2048]{1,0:T(8,128)(2,1)}, bf16[64,2048]{1,0:T(8,128)(2,1)S(1)}, u32[]{:S(2)}, u32[]{:S(2)}) collective-permute-start(bf16[64,2048]{1,0:T(8,128)(2,1)} %bitcast.72), channel_id=1, source_target_pairs={{0,6},{1,7},{2,4},{3,5},{4,2},{5,3},{6,0},{7,1},{8,14},{9,15},{10,... | collective-permute-start | bytes 786440 | tf_op jit(solution)/shard_map/ppermute | solution.py:357
  7.0 53.2 %collective-permute-start.4 = (bf16[64,2048]{1,0:T(8,128)(2,1)}, bf16[64,2048]{1,0:T(8,128)(2,1)S(1)}, u32[]{:S(2)}, u32[]{:S(2)}) collective-permute-start(bf16[64,2048]{1,0:T(8,128)(2,1)} %bitcast.73), channel_id=1, source_target_pairs={{0,5},{1,4},{2,7},{3,6},{4,1},{5,0},{6,3},{7,2},{8,13},{9,12},{10,... | collective-permute-start | bytes 786440 | tf_op jit(solution)/shard_map/ppermute | solution.py:357
  7.7 52.5 %collective-permute-start.3 = (bf16[64,2048]{1,0:T(8,128)(2,1)}, bf16[64,2048]{1,0:T(8,128)(2,1)S(1)}, u32[]{:S(2)}, u32[]{:S(2)}) collective-permute-start(bf16[64,2048]{1,0:T(8,128)(2,1)} %bitcast.74), channel_id=1, source_target_pairs={{0,4},{1,5},{2,6},{3,7},{4,0},{5,1},{6,2},{7,3},{8,12},{9,13},{10,... | collective-permute-start | bytes 786440 | tf_op jit(solution)/shard_map/ppermute | solution.py:357
  9.7 50.5 %collective-permute-start.2 = (bf16[64,2048]{1,0:T(8,128)(2,1)}, bf16[64,2048]{1,0:T(8,128)(2,1)S(1)}, u32[]{:S(2)}, u32[]{:S(2)}) collective-permute-start(bf16[64,2048]{1,0:T(8,128)(2,1)} %bitcast.75), channel_id=1, source_target_pairs={{0,3},{1,2},{2,1},{3,0},{4,7},{5,6},{6,5},{7,4},{8,11},{9,10},{10,... | collective-permute-start | bytes 786440 | tf_op jit(solution)/shard_map/ppermute | solution.py:357
  15.2 40.8 %all-to-all-start = ((s32[8,32,128]{2,1,0:T(8,128)}), s32[8,32,128]{2,1,0:T(8,128)S(1)}, u32[]{:S(2)}, u32[]{:S(2)}) async-start(s32[8,32,128]{2,1,0:T(8,128)} %add_add_fusion), calls=%async_computation | async-start | bytes 262144 | tf_op jit(solution)/shard_map/all_to_all | solution.py:382
  102.5 12.0 %collective-permute-start.13 = (bf16[64,2048]{1,0:T(8,128)(2,1)S(1)}, bf16[64,2048]{1,0:T(8,128)(2,1)S(1)}, u32[]{:S(2)}, u32[]{:S(2)}) collective-permute-start(bf16[64,2048]{1,0:T(8,128)(2,1)S(1)} %get-tuple-element.82), channel_id=1, source_target_pairs={{0,7},{1,6},{2,5},{3,4},{4,3},{5,2},{6,1},{7,0},{8,15},{9,14},{10,... | collective-permute-start | bytes 786440 | tf_op jit(solution)/shard_map/ppermute | solution.py:357
  105.7 30.1 %collective-permute-start.12 = (bf16[64,2048]{1,0:T(8,128)(2,1)S(1)}, bf16[64,2048]{1,0:T(8,128)(2,1)S(1)}, u32[]{:S(2)}, u32[]{:S(2)}) collective-permute-start(bf16[64,2048]{1,0:T(8,128)(2,1)S(1)} %get-tuple-element.83), channel_id=1, source_target_pairs={{0,6},{1,7},{2,4},{3,5},{4,2},{5,3},{6,0},{7,1},{8,14},{9,15},{10,... | collective-permute-start | bytes 786440 | tf_op jit(solution)/shard_map/ppermute | solution.py:357
  107.2 38.8 %collective-permute-start.11 = (bf16[64,2048]{1,0:T(8,128)(2,1)S(1)}, bf16[64,2048]{1,0:T(8,128)(2,1)S(1)}, u32[]{:S(2)}, u32[]{:S(2)}) collective-permute-start(bf16[64,2048]{1,0:T(8,128)(2,1)S(1)} %get-tuple-element.84), channel_id=1, source_target_pairs={{0,5},{1,4},{2,7},{3,6},{4,1},{5,0},{6,3},{7,2},{8,13},{9,12},{10,... | collective-permute-start | bytes 786440 | tf_op jit(solution)/shard_map/ppermute | solution.py:357
  107.8 41.5 %collective-permute-start.10 = (bf16[64,2048]{1,0:T(8,128)(2,1)S(1)}, bf16[64,2048]{1,0:T(8,128)(2,1)S(1)}, u32[]{:S(2)}, u32[]{:S(2)}) collective-permute-start(bf16[64,2048]{1,0:T(8,128)(2,1)S(1)} %get-tuple-element.85), channel_id=1, source_target_pairs={{0,4},{1,5},{2,6},{3,7},{4,0},{5,1},{6,2},{7,3},{8,12},{9,13},{10,... | collective-permute-start | bytes 786440 | tf_op jit(solution)/shard_map/ppermute | solution.py:357
  110.1 39.1 %collective-permute-start.9 = (bf16[64,2048]{1,0:T(8,128)(2,1)S(1)}, bf16[64,2048]{1,0:T(8,128)(2,1)S(1)}, u32[]{:S(2)}, u32[]{:S(2)}) collective-permute-start(bf16[64,2048]{1,0:T(8,128)(2,1)S(1)} %get-tuple-element.86), channel_id=1, source_target_pairs={{0,3},{1,2},{2,1},{3,0},{4,7},{5,6},{6,5},{7,4},{8,11},{9,10},{10,... | collective-permute-start | bytes 786440 | tf_op jit(solution)/shard_map/ppermute | solution.py:357
  114.5 37.0 %collective-permute-start.8 = (bf16[64,2048]{1,0:T(8,128)(2,1)S(1)}, bf16[64,2048]{1,0:T(8,128)(2,1)S(1)}, u32[]{:S(2)}, u32[]{:S(2)}) collective-permute-start(bf16[64,2048]{1,0:T(8,128)(2,1)S(1)} %get-tuple-element.87), channel_id=1, source_target_pairs={{0,2},{1,3},{2,0},{3,1},{4,6},{5,7},{6,4},{7,5},{8,10},{9,11},{10,... | collective-permute-start | bytes 786440 | tf_op jit(solution)/shard_map/ppermute | solution.py:357
  135.9 15.6 %collective-permute-start.7 = (bf16[64,2048]{1,0:T(8,128)(2,1)S(1)}, bf16[64,2048]{1,0:T(8,128)(2,1)S(1)}, u32[]{:S(2)}, u32[]{:S(2)}) collective-permute-start(bf16[64,2048]{1,0:T(8,128)(2,1)S(1)} %get-tuple-element.88), channel_id=1, source_target_pairs={{0,1},{1,0},{2,3},{3,2},{4,5},{5,4},{6,7},{7,6},{8,9},{9,8},{10,11... | collective-permute-start | bytes 786440 | tf_op jit(solution)/shard_map/ppermute | solution.py:357
  156.5 12.1 %collective-permute-start.20 = (bf16[64,2048]{1,0:T(8,128)(2,1)}, bf16[64,2048]{1,0:T(8,128)(2,1)S(1)}, u32[]{:S(2)}, u32[]{:S(2)}) collective-permute-start(bf16[64,2048]{1,0:T(8,128)(2,1)} %get-tuple-element.55.rest_0_), channel_id=1, source_target_pairs={{0,7},{1,6},{2,5},{3,4},{4,3},{5,2},{6,1},{7,0},{8,15},{9,14},{10,... | collective-permute-start | bytes 786440 | tf_op jit(solution)/shard_map/ppermute | solution.py:357
  159.8 29.0 %collective-permute-start.19 = (bf16[64,2048]{1,0:T(8,128)(2,1)}, bf16[64,2048]{1,0:T(8,128)(2,1)S(1)}, u32[]{:S(2)}, u32[]{:S(2)}) collective-permute-start(bf16[64,2048]{1,0:T(8,128)(2,1)} %get-tuple-element.55.rest_0_), channel_id=1, source_target_pairs={{0,6},{1,7},{2,4},{3,5},{4,2},{5,3},{6,0},{7,1},{8,14},{9,15},{10,... | collective-permute-start | bytes 786440 | tf_op jit(solution)/shard_map/ppermute | solution.py:357
  160.2 38.6 %collective-permute-start.18 = (bf16[64,2048]{1,0:T(8,128)(2,1)}, bf16[64,2048]{1,0:T(8,128)(2,1)S(1)}, u32[]{:S(2)}, u32[]{:S(2)}) collective-permute-start(bf16[64,2048]{1,0:T(8,128)(2,1)} %get-tuple-element.55.rest_0_), channel_id=1, source_target_pairs={{0,5},{1,4},{2,7},{3,6},{4,1},{5,0},{6,3},{7,2},{8,13},{9,12},{10,... | collective-permute-start | bytes 786440 | tf_op jit(solution)/shard_map/ppermute | solution.py:357
  160.2 40.8 %collective-permute-start.17 = (bf16[64,2048]{1,0:T(8,128)(2,1)}, bf16[64,2048]{1,0:T(8,128)(2,1)S(1)}, u32[]{:S(2)}, u32[]{:S(2)}) collective-permute-start(bf16[64,2048]{1,0:T(8,128)(2,1)} %get-tuple-element.55.rest_0_), channel_id=1, source_target_pairs={{0,4},{1,5},{2,6},{3,7},{4,0},{5,1},{6,2},{7,3},{8,12},{9,13},{10,... | collective-permute-start | bytes 786440 | tf_op jit(solution)/shard_map/ppermute | solution.py:357
  164.2 36.9 %collective-permute-start.16 = (bf16[64,2048]{1,0:T(8,128)(2,1)}, bf16[64,2048]{1,0:T(8,128)(2,1)S(1)}, u32[]{:S(2)}, u32[]{:S(2)}) collective-permute-start(bf16[64,2048]{1,0:T(8,128)(2,1)} %get-tuple-element.55.rest_0_), channel_id=1, source_target_pairs={{0,3},{1,2},{2,1},{3,0},{4,7},{5,6},{6,5},{7,4},{8,11},{9,10},{10,... | collective-permute-start | bytes 786440 | tf_op jit(solution)/shard_map/ppermute | solution.py:357
  168.6 34.0 %collective-permute-start.15 = (bf16[64,2048]{1,0:T(8,128)(2,1)}, bf16[64,2048]{1,0:T(8,128)(2,1)S(1)}, u32[]{:S(2)}, u32[]{:S(2)}) collective-permute-start(bf16[64,2048]{1,0:T(8,128)(2,1)} %get-tuple-element.55.rest_0_), channel_id=1, source_target_pairs={{0,2},{1,3},{2,0},{3,1},{4,6},{5,7},{6,4},{7,5},{8,10},{9,11},{10,... | collective-permute-start | bytes 786440 | tf_op jit(solution)/shard_map/ppermute | solution.py:357
  188.8 13.8 %collective-permute-start.14 = (bf16[64,2048]{1,0:T(8,128)(2,1)}, bf16[64,2048]{1,0:T(8,128)(2,1)S(1)}, u32[]{:S(2)}, u32[]{:S(2)}) collective-permute-start(bf16[64,2048]{1,0:T(8,128)(2,1)} %get-tuple-element.55.rest_0_), channel_id=1, source_target_pairs={{0,1},{1,0},{2,3},{3,2},{4,5},{5,4},{6,7},{7,6},{8,9},{9,8},{10,11... | collective-permute-start | bytes 786440 | tf_op jit(solution)/shard_map/ppermute | solution.py:357
  198.8 50.7 %collective-permute-start.21 = (f32[72,256]{1,0:T(8,128)}, f32[72,256]{1,0:T(8,128)S(1)}, u32[]{:S(2)}, u32[]{:S(2)}) collective-permute-start(f32[72,256]{1,0:T(8,128)} %get-tuple-element.57), channel_id=1, source_target_pairs={{0,1},{1,0},{2,3},{3,2},{4,5},{5,4},{6,7},{7,6},{8,9},{9,8},{10,11... | collective-permute-start | bytes 221192 | tf_op jit(solution)/shard_map/ppermute | solution.py:366
  249.6 11.3 %collective-permute-start.22 = (f32[72,256]{1,0:T(8,128)S(1)}, f32[72,256]{1,0:T(8,128)S(1)}, u32[]{:S(2)}, u32[]{:S(2)}) collective-permute-start(f32[72,256]{1,0:T(8,128)S(1)} %add.50), channel_id=1, source_target_pairs={{0,2},{1,3},{2,0},{3,1},{4,6},{5,7},{6,4},{7,5},{8,10},{9,11},{10,... | collective-permute-start | bytes 221192 | tf_op jit(solution)/shard_map/ppermute | solution.py:366
  253.1 7.9 %collective-permute-start.27 = (f32[72,256]{1,0:T(8,128)S(1)}, f32[72,256]{1,0:T(8,128)S(1)}, u32[]{:S(2)}, u32[]{:S(2)}) collective-permute-start(f32[72,256]{1,0:T(8,128)S(1)} %add.55), channel_id=1, source_target_pairs={{0,2},{1,3},{2,0},{3,1},{4,6},{5,7},{6,4},{7,5},{8,10},{9,11},{10,... | collective-permute-start | bytes 221192 | tf_op jit(solution)/shard_map/ppermute | solution.py:366
  255.6 35.2 %collective-permute-start.37 = (bf16[64,2048]{1,0:T(8,128)(2,1)S(1)}, bf16[64,2048]{1,0:T(8,128)(2,1)S(1)}, u32[]{:S(2)}, u32[]{:S(2)}) collective-permute-start(bf16[64,2048]{1,0:T(8,128)(2,1)S(1)} %get-tuple-element.74), channel_id=1, source_target_pairs={{0,7},{1,6},{2,5},{3,4},{4,3},{5,2},{6,1},{7,0},{8,15},{9,14},{10,... | collective-permute-start | bytes 786440 | tf_op jit(solution)/shard_map/ppermute | solution.py:357
  258.3 35.9 %collective-permute-start.36 = (bf16[64,2048]{1,0:T(8,128)(2,1)S(1)}, bf16[64,2048]{1,0:T(8,128)(2,1)S(1)}, u32[]{:S(2)}, u32[]{:S(2)}) collective-permute-start(bf16[64,2048]{1,0:T(8,128)(2,1)S(1)} %get-tuple-element.75), channel_id=1, source_target_pairs={{0,6},{1,7},{2,4},{3,5},{4,2},{5,3},{6,0},{7,1},{8,14},{9,15},{10,... | collective-permute-start | bytes 786440 | tf_op jit(solution)/shard_map/ppermute | solution.py:357
  260.8 23.5 %collective-permute-start.23 = (f32[72,256]{1,0:T(8,128)S(1)}, f32[72,256]{1,0:T(8,128)S(1)}, u32[]{:S(2)}, u32[]{:S(2)}) collective-permute-start(f32[72,256]{1,0:T(8,128)S(1)} %add.51), channel_id=1, source_target_pairs={{0,4},{1,5},{2,6},{3,7},{4,0},{5,1},{6,2},{7,3},{8,12},{9,13},{10,... | collective-permute-start | bytes 221192 | tf_op jit(solution)/shard_map/ppermute | solution.py:366
  261.0 24.1 %collective-permute-start.28 = (f32[72,256]{1,0:T(8,128)S(1)}, f32[72,256]{1,0:T(8,128)S(1)}, u32[]{:S(2)}, u32[]{:S(2)}) collective-permute-start(f32[72,256]{1,0:T(8,128)S(1)} %add.56), channel_id=1, source_target_pairs={{0,4},{1,5},{2,6},{3,7},{4,0},{5,1},{6,2},{7,3},{8,12},{9,13},{10,... | collective-permute-start | bytes 221192 | tf_op jit(solution)/shard_map/ppermute | solution.py:366
  287.8 24.7 %collective-permute-start.35 = (bf16[64,2048]{1,0:T(8,128)(2,1)S(1)}, bf16[64,2048]{1,0:T(8,128)(2,1)S(1)}, u32[]{:S(2)}, u32[]{:S(2)}) collective-permute-start(bf16[64,2048]{1,0:T(8,128)(2,1)S(1)} %get-tuple-element.76), channel_id=1, source_target_pairs={{0,5},{1,4},{2,7},{3,6},{4,1},{5,0},{6,3},{7,2},{8,13},{9,12},{10,... | collective-permute-start | bytes 786440 | tf_op jit(solution)/shard_map/ppermute | solution.py:357
  290.8 22.1 %collective-permute-start.34 = (bf16[64,2048]{1,0:T(8,128)(2,1)S(1)}, bf16[64,2048]{1,0:T(8,128)(2,1)S(1)}, u32[]{:S(2)}, u32[]{:S(2)}) collective-permute-start(bf16[64,2048]{1,0:T(8,128)(2,1)S(1)} %get-tuple-element.77), channel_id=1, source_target_pairs={{0,4},{1,5},{2,6},{3,7},{4,0},{5,1},{6,2},{7,3},{8,12},{9,13},{10,... | collective-permute-start | bytes 786440 | tf_op jit(solution)/shard_map/ppermute | solution.py:357
  290.9 22.1 %collective-permute-start.33 = (bf16[64,2048]{1,0:T(8,128)(2,1)S(1)}, bf16[64,2048]{1,0:T(8,128)(2,1)S(1)}, u32[]{:S(2)}, u32[]{:S(2)}) collective-permute-start(bf16[64,2048]{1,0:T(8,128)(2,1)S(1)} %get-tuple-element.78), channel_id=1, source_target_pairs={{0,3},{1,2},{2,1},{3,0},{4,7},{5,6},{6,5},{7,4},{8,11},{9,10},{10,... | collective-permute-start | bytes 786440 | tf_op jit(solution)/shard_map/ppermute | solution.py:357
  294.3 21.4 %collective-permute-start.32 = (bf16[64,2048]{1,0:T(8,128)(2,1)S(1)}, bf16[64,2048]{1,0:T(8,128)(2,1)S(1)}, u32[]{:S(2)}, u32[]{:S(2)}) collective-permute-start(bf16[64,2048]{1,0:T(8,128)(2,1)S(1)} %get-tuple-element.79), channel_id=1, source_target_pairs={{0,2},{1,3},{2,0},{3,1},{4,6},{5,7},{6,4},{7,5},{8,10},{9,11},{10,... | collective-permute-start | bytes 786440 | tf_op jit(solution)/shard_map/ppermute | solution.py:357
  294.3 21.4 %collective-permute-start.31 = (bf16[64,2048]{1,0:T(8,128)(2,1)S(1)}, bf16[64,2048]{1,0:T(8,128)(2,1)S(1)}, u32[]{:S(2)}, u32[]{:S(2)}) collective-permute-start(bf16[64,2048]{1,0:T(8,128)(2,1)S(1)} %get-tuple-element.80), channel_id=1, source_target_pairs={{0,1},{1,0},{2,3},{3,2},{4,5},{5,4},{6,7},{7,6},{8,9},{9,8},{10,11... | collective-permute-start | bytes 786440 | tf_op jit(solution)/shard_map/ppermute | solution.py:357
  (40 other events, 501.8 us)

commit v2 on v1

v2 whole, which is shorter than its diff:
```python
import functools

import jax
import jax.numpy as jnp
from jax import lax
from jax.experimental import pallas as pl
from jax.experimental.pallas import tpu as pltpu
from jax.sharding import PartitionSpec as P

epsilon = 1e-05
bf16 = jnp.bfloat16
f32 = jnp.float32
LANES = 128
WIDE = 256


def dot(left, right):
    return jnp.dot(left, right, preferred_element_type=f32)


def dot_nt(left, right):
    return lax.dot_general(left, right, (((1,), (1,)), ((), ())), preferred_element_type=f32)


def dot_exact(left, right):
    return jnp.dot(left, right, preferred_element_type=f32, precision=lax.Precision.HIGHEST)


def dot_nt_exact(left, right):
    return lax.dot_general(
        left,
        right,
        (((1,), (1,)), ((), ())),
        preferred_element_type=f32,
        precision=lax.Precision.HIGHEST,
    )


def params(limit=56):
    return pltpu.CompilerParams(vmem_limit_bytes=limit * 1024 * 1024)


def spread(column, width):
    return jnp.concatenate([column] * (width // LANES), axis=1)


def fold(values):
    total = values[:, :LANES]
    for start in range(LANES, values.shape[1], LANES):
        total = total + values[:, start : start + LANES]
    return total


def row_join(ref, first, count):
    return jnp.concatenate([ref[first + k : first + k + 1, :] for k in range(count)], axis=1)


def sigmoid(values):
    return 0.5 * jnp.tanh(0.5 * values) + 0.5


def onehot_rows(row, rows):
    width = row.shape[1]
    place = lax.broadcasted_iota(jnp.int32, (rows, width), 0)
    return jnp.where(place == row, 1.0, 0.0).astype(bf16)


def onehot_low(row, place):
    spots = jnp.broadcast_to(row.astype(bf16), place.shape)
    return jnp.where(place == spots, jnp.ones((), bf16), jnp.zeros((), bf16))


def place_low():
    return lax.broadcasted_iota(jnp.int32, (LANES, LANES), 0).astype(bf16)


def node_groups(node_ref):
    total = node_ref.shape[1]
    return jnp.concatenate(
        [node_ref[:, start : start + WIDE] for start in range(0, total, WIDE)], axis=0
    )


def sender_kernel(piece, me_ref, node_ref, send_ref, edge_ref, weight_ref, vec_ref, pick_ref, base_ref):
    width = edge_ref.shape[1]
    feat = edge_ref.shape[0]
    groups = node_ref.shape[1] // WIDE
    table = node_groups(node_ref)
    bias = spread(vec_ref[0], piece)
    for start in range(0, width, piece):
        ids = row_join(send_ref, start // LANES, piece // LANES)
        onehot = onehot_rows(ids & (WIDE - 1), WIDE)
        group = lax.shift_right_logical(ids, 8)
        found = dot(table, onehot)
        rows = found[:feat]
        for g in range(1, groups):
            rows = jnp.where(
                jnp.broadcast_to(group == g, (feat, piece)), found[g * feat : (g + 1) * feat], rows
            )
        low = rows.astype(bf16)
        pick_ref[:, start : start + piece] = low
        both = jnp.concatenate([low, edge_ref[:, start : start + piece]], axis=0)
        base_ref[:, start : start + piece] = dot(weight_ref[...], both) + bias


def gather_blocks(meta_ref, first, code_ref, start, count, source_ref):
    feat = source_ref.shape[0]
    parts = []
    for k in range(count):
        tile = meta_ref[first + start + k]
        code = code_ref[0, start + k : start + k + 1, :]
        index = jnp.broadcast_to(code & (LANES - 1), (feat, LANES))
        rows = source_ref[:, pl.ds(pl.multiple_of(tile * LANES, LANES), LANES)]
        taken = jnp.take_along_axis(rows, index, axis=1)
        parts.append(jnp.where(jnp.broadcast_to(code < LANES, (feat, LANES)), taken, 0.0))
    return jnp.concatenate(parts, axis=1)


def scatter_blocks(meta_ref, first, code_ref, start, count, values, total_ref, place):
    for k in range(count):
        tile = meta_ref[first + start + k]
        onehot = onehot_low(code_ref[0, start + k : start + k + 1, :], place)
        term = dot_nt(values[:, k * LANES : (k + 1) * LANES], onehot)
        where_to = pl.ds(pl.multiple_of(tile * LANES, LANES), LANES)
        total_ref[:, where_to] = total_ref[:, where_to] + term


def forward_kernel(masks, blocks, piece, extra, meta_ref, code_ref, base_ref, edge_ref, in_ref, out_ref, vec_ref, *rest):
    count = len(masks)
    shard_refs = rest[:count]
    result_ref, act_ref, slope_ref, normed_ref, inv_ref, part_ref, proj_ref, total_ref = rest[count + extra :]
    step = pl.program_id(0)
    for k in range(count):

        @pl.when(step == k)
        def _():
            proj_ref[...] = dot(in_ref[...], shard_refs[k][...])

    total_ref[...] = jnp.zeros_like(total_ref)
    width = edge_ref.shape[1]
    first = 1 + owner(masks, step, meta_ref) * blocks
    per = piece // LANES
    place = place_low()
    for start in range(0, width, piece):
        lanes = slice(start, start + piece)
        block = start // LANES
        half = base_ref[:, lanes] + gather_blocks(meta_ref, first, code_ref, block, per, proj_ref)
        up = jnp.tanh(half) + 1.0
        act = half * up
        slope_ref[:, lanes] = (up + act * (2.0 - up)).astype(bf16)
        act_low = act.astype(bf16)
        act_ref[:, lanes] = act_low
        second = dot(out_ref[...], act_low) + spread(vec_ref[1], piece)
        centered = second - jnp.mean(second, axis=0, keepdims=True)
        inv = lax.rsqrt(jnp.mean(centered * centered, axis=0, keepdims=True) + epsilon)
        normed = centered * inv
        normed_ref[:, lanes] = normed.astype(bf16)
        for k in range(per):
            inv_ref[block + k : block + k + 1, :] = inv[:, k * LANES : (k + 1) * LANES]
        message = (normed * spread(vec_ref[2], piece) + spread(vec_ref[3], piece)).astype(bf16)
        result_ref[:, lanes] = edge_ref[:, lanes] + message
        scatter_blocks(meta_ref, first, code_ref, block, per, message, total_ref, place)
    part_ref[0] = total_ref[...].astype(bf16)


def node_kernel(peers, node_ref, cot_ref, in_t_ref, in_ref, out_t_ref, out_ref, vec_ref, *rest):
    part_refs = rest[:peers]
    result_ref, base_ref, back_ref, pack_ref = rest[peers:]
    feat, total = node_ref.shape
    aggregate = part_refs[0][...].astype(f32)
    for k in range(1, peers):
        aggregate = aggregate + part_refs[k][...].astype(f32)
    node_inputs = jnp.concatenate([node_ref[...], aggregate.astype(bf16)], axis=0)
    pre = dot(in_t_ref[...], node_inputs) + spread(vec_ref[4], total)
    sig = sigmoid(pre)
    act = pre * sig
    slope = sig + act * (1.0 - sig)
    act_low = act.astype(bf16)
    second = dot(out_t_ref[...], act_low) + spread(vec_ref[5], total)
    centered = second - jnp.mean(second, axis=0, keepdims=True)
    inv = lax.rsqrt(jnp.mean(centered * centered, axis=0, keepdims=True) + epsilon)
    normed = centered * inv
    gain = spread(vec_ref[6], total)
    update = normed * gain + spread(vec_ref[7], total)
    result_ref[...] = (node_ref[...].astype(f32) + update).astype(bf16)
    upstream = cot_ref[...].astype(f32)
    scaled = upstream * gain
    inner = (
        scaled
        - jnp.mean(scaled, axis=0, keepdims=True)
        - normed * jnp.mean(scaled * normed, axis=0, keepdims=True)
    )
    grad = (inner * inv).astype(bf16)
    third = (dot(out_ref[...], grad) * slope).astype(bf16)
    input_grad = dot(in_ref[...], third)
    base_ref[...] = upstream + input_grad[:feat]
    back_ref[...] = input_grad[feat:].astype(bf16)
    pack_ref[...] = jnp.zeros_like(pack_ref)
    pack_ref[:feat, : 2 * feat] = dot_nt(third, node_inputs)
    pack_ref[:feat, 2 * feat : 3 * feat] = dot_nt(act_low, grad)
    ones = jnp.ones((8, LANES), f32)
    sums = (
        fold(third.astype(f32)),
        fold(grad.astype(f32)),
        fold(upstream * normed),
        fold(upstream),
    )
    for k in range(4):
        pack_ref[feat + k : feat + k + 1, :feat] = dot_nt_exact(ones, sums[k])[:1]


def backward_kernel(masks, blocks, piece, extra, meta_ref, code_ref, cot_ref, normed_ref, act_ref, slope_ref, inv_ref, edge_ref, pick_ref, out_ref, in_ref, vec_ref, *rest):
    count = len(masks)
    back_refs = rest[:count]
    shard_refs = rest[count : 2 * count]
    prior_refs = rest[2 * count : 2 * count + extra]
    grad_ref, first_ref, part_ref, pack_ref, pull_ref, total_ref, w1_ref, wr_ref, w2_ref, sum_ref = rest[2 * count + extra :]
    step = pl.program_id(0)
    feat, width = edge_ref.shape

    @pl.when(step == 0)
    def _():
        w1_ref[...] = jnp.zeros_like(w1_ref)
        wr_ref[...] = jnp.zeros_like(wr_ref)
        w2_ref[...] = jnp.zeros_like(w2_ref)
        sum_ref[...] = jnp.zeros_like(sum_ref)

    for k in range(count):

        @pl.when(step == k)
        def _():
            pull_ref[...] = back_refs[k][...].astype(f32)

    total_ref[...] = jnp.zeros_like(total_ref)
    first = 1 + owner(masks, step, meta_ref) * blocks
    per = piece // LANES
    place = place_low()
    for start in range(0, width, piece):
        lanes = slice(start, start + piece)
        block = start // LANES
        cot = cot_ref[:, lanes].astype(f32)
        upstream = cot + gather_blocks(meta_ref, first, code_ref, block, per, pull_ref)
        normed = normed_ref[:, lanes].astype(f32)
        scaled = upstream * spread(vec_ref[2], piece)
        inner_grad = (
            scaled
            - jnp.mean(scaled, axis=0, keepdims=True)
            - normed * jnp.mean(scaled * normed, axis=0, keepdims=True)
        )
        second = (inner_grad * row_join(inv_ref, block, per)).astype(bf16)
        sum_ref[2] += fold(upstream * normed)
        sum_ref[3] += fold(upstream)
        sum_ref[1] += fold(second.astype(f32))
        w2_ref[...] += dot_nt(act_ref[:, lanes], second)
        grad = (dot(out_ref[...], second) * slope_ref[:, lanes].astype(f32)).astype(bf16)
        first_ref[:, lanes] = grad
        sum_ref[0] += fold(grad.astype(f32))
        grad_ref[:, lanes] = cot + dot(in_ref[...], grad)
        both = jnp.concatenate([pick_ref[:, lanes], edge_ref[:, lanes]], axis=0)
        w1_ref[...] += dot_nt(grad, both)
        scatter_blocks(meta_ref, first, code_ref, block, per, grad, total_ref, place)
    low = total_ref[...].astype(bf16)
    part_ref[0] = low
    for k in range(count):

        @pl.when(step == k)
        def _():
            wr_ref[...] += dot_nt(low, shard_refs[k][...])

    @pl.when(step == pl.num_programs(0) - 1)
    def _():
        pack_ref[...] = jnp.zeros_like(pack_ref)
        pack_ref[:feat, :feat] = w1_ref[:, :feat]
        pack_ref[:feat, feat : 2 * feat] = wr_ref[...]
        pack_ref[:feat, 2 * feat : 3 * feat] = w1_ref[:, feat:]
        pack_ref[:feat, 3 * feat : 4 * feat] = w2_ref[...]
        ones = jnp.ones((8, LANES), f32)
        for k in range(4):
            pack_ref[feat + k : feat + k + 1, :feat] = dot_nt_exact(ones, sum_ref[k])[:1]
        if extra:
            pack_ref[...] += prior_refs[1][...]


def sender_sum_kernel(me_ref, grad_ref, send_ref, sum_ref, total_ref):
    feat, width = grad_ref.shape
    groups = sum_ref.shape[1] // WIDE

    @pl.when(pl.program_id(0) == 0)
    def _():
        total_ref[...] = jnp.zeros_like(total_ref)

    piece = min(2048, width)
    for start in range(0, width, piece):
        ids = row_join(send_ref, start // LANES, piece // LANES)
        onehot = onehot_rows(ids & (WIDE - 1), WIDE)
        group = jnp.broadcast_to(lax.shift_right_logical(ids, 8).astype(bf16), (feat, piece))
        values = grad_ref[:, start : start + piece]
        zero = jnp.zeros((), bf16)
        masked = jnp.concatenate(
            [jnp.where(group == jnp.asarray(g, bf16), values, zero) for g in range(groups)], axis=0
        )
        total_ref[...] += dot_nt(masked, onehot)

    @pl.when(pl.program_id(0) == pl.num_programs(0) - 1)
    def _():
        for g in range(groups):
            sum_ref[:, g * WIDE : (g + 1) * WIDE] = total_ref[g * feat : (g + 1) * feat, :]


def finish_kernel(sums, peers, base_ref, weight_ref, node_pack_ref, edge_pack_ref, *rest):
    sum_refs = rest[:sums]
    part_refs = rest[sums : sums + peers]
    grad_ref, e1, b1, e2, b2, g1, s1, n1, c1, n2, c2, g2, s2 = rest[sums + peers :]
    sent = sum_refs[0][...]
    for k in range(1, sums):
        sent = sent + sum_refs[k][...]
    total = part_refs[0][...].astype(f32)
    for k in range(1, peers):
        total = total + part_refs[k][...].astype(f32)
    both = jnp.concatenate([sent, total], axis=0)
    grad_ref[...] = base_ref[...] + dot_exact(weight_ref[...], both)
    feat = base_ref.shape[0]
    e1[...] = edge_pack_ref[:feat, : 3 * feat]
    e2[...] = edge_pack_ref[:feat, 3 * feat : 4 * feat]
    n1[...] = node_pack_ref[:feat, : 2 * feat]
    n2[...] = node_pack_ref[:feat, 2 * feat : 3 * feat]
    for k, ref in enumerate((b1, b2, g1, s1)):
        ref[...] = edge_pack_ref[feat + k : feat + k + 1, :feat]
    for k, ref in enumerate((c1, c2, g2, s2)):
        ref[...] = node_pack_ref[feat + k : feat + k + 1, :feat]


def owner(masks, step, meta_ref):
    stride = masks[1] - masks[0] if len(masks) > 1 else 0
    return meta_ref[0] ^ (masks[0] + stride * step)


def struct(shape, dtype):
    return jax.ShapeDtypeStruct(shape, dtype)


def whole(shape):
    return pl.BlockSpec(shape, lambda *_: (0,) * len(shape))


def per_device(groups, peers, *arrays):
    (
        nodes, edges, send_nodes, block_tile, block_count, slot_ids,
        edge_in_weight, edge_in_bias, edge_out_weight, edge_out_bias, edge_gain, edge_shift,
        node_in_weight, node_in_bias, node_out_weight, node_out_bias, node_gain, node_shift,
        node_cot, edge_cot,
    ) = arrays
    feat = nodes.shape[1]
    node_total = nodes.shape[0]
    edge_total = edges.shape[0]
    block_total = block_tile.shape[0]
    blocks = block_total // peers
    per_peer = edge_total // peers
    rows = edge_total // LANES

    def swap(value, mask):
        if mask == 0:
            return value
        return lax.ppermute(value, "peer", [(i, i ^ mask) for i in range(peers)])

    near = [m for m in range(0, peers, 2)]
    routed = [m for m in (4, 6, 2) if m < peers] + [m for m in range(8, peers, 2)]

    def gather_all(value):
        found = {0: value, 1: swap(value, 1)}
        for m in routed:
            found[m] = swap(value, m)
        for m in routed:
            found[m | 1] = swap(found[m], 1)
        return found

    def sum_out(parts):
        got = {m: swap(parts[m | 1], 1) for m in routed + [0]}
        sums = [parts[0], got[0]]
        for m in routed:
            both = (parts[m].astype(f32) + got[m].astype(f32)).astype(bf16)
            sums.append(swap(both, m))
        return sums

    def add_up(value):
        for axis, size in (("grp", groups), ("peer", peers)):
            mask = 1
            while mask < size:
                value = value + lax.ppermute(value, axis, [(i, i ^ mask) for i in range(size)])
                mask *= 2
        return value

    teams = [tuple(range(0, peers, 2)), tuple(range(1, peers, 2))]

    node_t = nodes.T
    edge_t = edges.T
    node_cot_t = node_cot.T
    edge_cot_t = edge_cot.T
    in_t = edge_in_weight.T
    send = send_nodes.reshape(rows, LANES)
    me = lax.axis_index("peer").astype(jnp.int32)[None]

    shards = gather_all(node_t)

    live = jnp.arange(LANES, dtype=jnp.int32)[None, :] < block_count[:, None]
    code = slot_ids.reshape(block_total, LANES) + jnp.where(live, 0, LANES) + 2 * LANES * block_tile[:, None]
    code = lax.all_to_all(code, "peer", 0, 0, tiled=True)
    meta = jnp.concatenate([me, code[:, 0] // (2 * LANES)])
    code = (code & (2 * LANES - 1)).reshape(peers, blocks, LANES)

    vec = jnp.broadcast_to(
        jnp.stack([0.5 * edge_in_bias, edge_out_bias, edge_gain, edge_shift, node_in_bias, node_out_bias, node_gain, node_shift])[:, :, None],
        (8, feat, LANES),
    )
    half = jnp.asarray(0.5, bf16)
    se_weight = jnp.concatenate([in_t[:, :feat], in_t[:, 2 * feat :]], axis=1) * half
    re_weight = in_t[:, feat : 2 * feat] * half
    back_weight = edge_out_weight * half

    wide = per_peer
    sub = wide // LANES

    def slab_of(masks):
        return pl.BlockSpec((feat, wide), lambda i, ref: (0, owner(masks, i, ref)))

    def rows_of(masks):
        return pl.BlockSpec((sub, LANES), lambda i, ref: (owner(masks, i, ref), 0))

    def code_of(masks):
        return pl.BlockSpec((1, sub, LANES), lambda i, ref: (owner(masks, i, ref), 0, 0))

    own_slab = pl.BlockSpec((feat, wide), lambda i, ref: (0, i))
    own_rows = pl.BlockSpec((sub, LANES), lambda i, ref: (i, 0))
    part_spec = pl.BlockSpec((1, feat, node_total), lambda i, ref: (i, 0, 0))
    shard_spec = whole((feat, node_total))
    keep_spec = pl.BlockSpec(memory_space=pl.ANY)

    picks, bases = [], []
    for masks in teams:
        count = len(masks)
        pick, base = pl.pallas_call(
            functools.partial(sender_kernel, 512),
            grid_spec=pltpu.PrefetchScalarGridSpec(
                num_scalar_prefetch=1,
                grid=(count,),
                in_specs=[shard_spec, rows_of(masks), slab_of(masks), whole((feat, 2 * feat)), whole((8, feat, LANES))],
                out_specs=[own_slab, own_slab],
            ),
            out_shape=[struct((feat, count * wide), bf16), struct((feat, count * wide), f32)],
            compiler_params=params(),
            name="sender",
        )(me, node_t, send, edge_t, se_weight, vec)
        picks.append(pick)
        bases.append(base)

    saved = []
    parts = {}
    result = None
    for t, masks in enumerate(teams):
        count = len(masks)
        extra = 0 if result is None else 1
        result, act, slope, normed, inv, part = pl.pallas_call(
            functools.partial(forward_kernel, masks, blocks, 1024, extra),
            grid_spec=pltpu.PrefetchScalarGridSpec(
                num_scalar_prefetch=1,
                grid=(count,),
                in_specs=[code_of(masks), own_slab, slab_of(masks), whole((feat, feat)), whole((feat, feat)), whole((8, feat, LANES))]
                + [shard_spec] * count
                + [keep_spec] * extra,
                out_specs=[slab_of(masks), own_slab, own_slab, own_slab, own_rows, part_spec],
                scratch_shapes=[pltpu.VMEM((feat, node_total), f32), pltpu.VMEM((feat, node_total), f32)],
            ),
            out_shape=[
                struct((feat, edge_total), bf16),
                struct((feat, count * wide), bf16),
                struct((feat, count * wide), bf16),
                struct((feat, count * wide), bf16),
                struct((count * sub, LANES), f32),
                struct((count, feat, node_total), bf16),
            ],
            input_output_aliases={7 + count: 0} if extra else {},
            compiler_params=params(),
            name="forward",
        )(meta, code, bases[t], edge_t, re_weight, edge_out_weight.T, vec, *[shards[m] for m in masks], *([result] * extra))
        saved.append((normed, act, slope, inv))
        for k, m in enumerate(masks):
            parts[m] = part[k]
    edge_result = result

    sums = sum_out(parts)
    node_result, node_base, back, node_pack = pl.pallas_call(
        functools.partial(node_kernel, len(sums)),
        out_shape=[
            struct((feat, node_total), bf16),
            struct((feat, node_total), f32),
            struct((feat, node_total), bf16),
            struct((feat + 8, 4 * feat), f32),
        ],
        compiler_params=params(),
        name="node",
    )(node_t, node_cot_t, node_in_weight.T, node_in_weight, node_out_weight.T, node_out_weight, vec, *sums)

    backs = gather_all(back)
    node_pack = add_up(node_pack)

    parts = {}
    firsts = []
    edge_grad = edge_pack = None
    for t, masks in enumerate(teams):
        count = len(masks)
        prior = [] if edge_grad is None else [edge_grad, edge_pack]
        extra = len(prior)
        normed, act, slope, inv = saved[t]
        edge_grad, first_grad, part, edge_pack = pl.pallas_call(
            functools.partial(backward_kernel, masks, blocks, 1024, extra),
            grid_spec=pltpu.PrefetchScalarGridSpec(
                num_scalar_prefetch=1,
                grid=(count,),
                in_specs=[code_of(masks), slab_of(masks), own_slab, own_slab, own_slab, own_rows, slab_of(masks), own_slab, whole((feat, feat)), whole((feat, feat)), whole((8, feat, LANES))]
                + [shard_spec] * (2 * count)
                + ([keep_spec, whole((feat + 8, 4 * feat))] if extra else []),
                out_specs=[slab_of(masks), own_slab, part_spec, whole((feat + 8, 4 * feat))],
                scratch_shapes=[
                    pltpu.VMEM((feat, node_total), f32),
                    pltpu.VMEM((feat, node_total), f32),
                    pltpu.VMEM((feat, 2 * feat), f32),
                    pltpu.VMEM((feat, feat), f32),
                    pltpu.VMEM((feat, feat), f32),
                    pltpu.VMEM((4, feat, LANES), f32),
                ],
            ),
            out_shape=[
                struct((feat, edge_total), f32),
                struct((feat, count * wide), bf16),
                struct((count, feat, node_total), bf16),
                struct((feat + 8, 4 * feat), f32),
            ],
            input_output_aliases={12 + 2 * count: 0} if extra else {},
            compiler_params=params(),
            name="backward",
        )(
            meta, code, edge_cot_t, normed, act, slope, inv, edge_t, picks[t], back_weight, edge_in_weight[2 * feat :], vec,
            *[backs[m] for m in masks], *[shards[m] for m in masks], *prior,
        )
        firsts.append(first_grad)
        for k, m in enumerate(masks):
            parts[m] = part[k]

    sums = sum_out(parts)
    edge_pack = add_up(edge_pack)

    sent = []
    for t, masks in enumerate(teams):
        sent.append(
            pl.pallas_call(
                sender_sum_kernel,
                grid_spec=pltpu.PrefetchScalarGridSpec(
                    num_scalar_prefetch=1,
                    grid=(len(masks),),
                    in_specs=[own_slab, rows_of(masks)],
                    out_specs=shard_spec,
                    scratch_shapes=[pltpu.VMEM((node_total // WIDE * feat, WIDE), f32)],
                ),
                out_shape=struct((feat, node_total), f32),
                compiler_params=params(),
                name="sender_sum",
            )(me, firsts[t], send)
        )

    vec_out = struct((1, feat), f32)
    sr_weight = jnp.concatenate([edge_in_weight[:feat], edge_in_weight[feat : 2 * feat]], axis=1).astype(f32)
    node_grad, e1, b1, e2, b2, g1, s1, n1, c1, n2, c2, g2, s2 = pl.pallas_call(
        functools.partial(finish_kernel, len(sent), len(sums)),
        out_shape=[
            struct((feat, node_total), f32),
            struct((feat, 3 * feat), f32), vec_out, struct((feat, feat), f32), vec_out, vec_out, vec_out,
            struct((feat, 2 * feat), f32), vec_out, struct((feat, feat), f32), vec_out, vec_out, vec_out,
        ],
        compiler_params=params(),
        name="finish",
    )(node_base, sr_weight, node_pack, edge_pack, *sent, *sums)

    def flat(row):
        return row.reshape(feat)

    return (
        node_result.T, edge_result.T, node_grad.T, edge_grad.T,
        e1.T, flat(b1), e2, flat(b2), flat(g1), flat(s1),
        n1.T, flat(c1), n2, flat(c2), flat(g2), flat(s2),
    )


def solution(mesh):
    split = P(("grp", "peer"), None)
    line = P(("grp", "peer"))
    one = P()
    return jax.shard_map(
        functools.partial(per_device, mesh.shape["grp"], mesh.shape["peer"]),
        mesh=mesh,
        in_specs=(split, split, line, line, line, line) + (one,) * 12 + (split, split),
        out_specs=(split, split, split, split) + (one,) * 12,
        check_vma=False,
    )
```

time: 323 us -> 248 us (0.77)
  starting transfers between devices: 96.4 us -> 51.3 us
  Pallas kernels: 133 us -> 104 us
    ppermute x28, starting transfers between devices: 83.2 us -> 38.2 us  [swap(): return lax.ppermute(value, 'peer', [(i, i ^ mask) for i in range(peers)])]
    pallas_call x6 -> x10, Pallas kernels: 133 us -> 104 us  [the longest x2 32.2 us: per_device(): pl.pallas_call(functools.partial(backward_kernel, masks, blocks, 1024, ex...]
    ppermute x28, waiting for transfers between devices: 38.7 us -> 45.9 us  [swap(): return lax.ppermute(value, 'peer', [(i, i ^ mask) for i in range(peers)])]
    ppermute x10, waiting for transfers between devices: 26.6 us -> 22.8 us  [add_up(): lax.ppermute(value, axis, [(i, i ^ mask) for i in range(size)])]
    unnamed x73 -> x67, local copies, waits for them, and re-layouts: 6.86 us -> 6.39 us
  transfers between devices with their start and end apart: 39 -> 39, of which waited for: 19 -> 14; matrix products, arithmetic and copies ran while one was open for 5% -> 7% of each run, Pallas kernels for 28% -> 34%
where the time goes in v2:
time: 248 us
  Pallas kernels  104 us (42%)
  waiting for transfers between devices  68.7 us (28%)
  starting transfers between devices  51.3 us (21%)
  local copies, waits for them, and re-layouts  13.1 us (5%)
  other arithmetic  9.68 us (4%)
    ppermute x28, waiting for transfers between devices, swap(): return lax.ppermute(value, 'peer', [(i, i ^ mask) for i in range(peers)])  45.9 us
    ppermute x28, starting transfers between devices, swap(): return lax.ppermute(value, 'peer', [(i, i ^ mask) for i in range(peers)])  38.2 us
    pallas_call x2, Pallas kernels, per_device(): pl.pallas_call(functools.partial(backward_kernel, masks, blocks, 1024, ex...  32.2 us
    pallas_call x2, Pallas kernels, per_device(): pl.pallas_call(functools.partial(sender_kernel, 512), grid_spec=pltpu.Pre...  26.2 us
    pallas_call x2, Pallas kernels, per_device(): pl.pallas_call(functools.partial(forward_kernel, masks, blocks, 1024, ext...  23.6 us
    ppermute x10, waiting for transfers between devices, add_up(): lax.ppermute(value, axis, [(i, i ^ mask) for i in range(size)])  22.8 us
    pallas_call x2, Pallas kernels, per_device(): pl.pallas_call(sender_sum_kernel, grid_spec=pltpu.PrefetchScalarGridSpec(...  14.3 us
    ppermute x10, starting transfers between devices, add_up(): lax.ppermute(value, axis, [(i, i ^ mask) for i in range(size)])  8.27 us
  transfers between devices with their start and end apart: 39, of which 14 were waited for; matrix products, arithmetic and copies ran while one was open for 7% of the time, Pallas kernels for 34%

profile of v2, /device:TPU:0, one launch (start us, length us, event | category | flops | bytes accessed | tf_op | source)
XLA Modules:
  0.0 247.6 jit_solution(14103389113782771934)
XLA Ops:
  0.6 3.0 %collective-permute-start.3 = (bf16[64,2048]{1,0:T(8,128)(2,1)}, bf16[64,2048]{1,0:T(8,128)(2,1)S(1)}, u32[]{:S(2)}, u32[]{:S(2)}) collective-permute-start(bf16[64,2048]{1,0:T(8,128)(2,1)} %bitcast.84), channel_id=1, source_target_pairs={{0,1},{1,0},{2,3},{3,2},{4,5},{5,4},{6,7},{7,6},{8,9},{9,8},{10,11... | collective-permute-start | bytes 786440 | tf_op jit(solution)/shard_map/ppermute | solution.py:364
  3.7 3.6 %collective-permute-start.2 = (bf16[64,2048]{1,0:T(8,128)(2,1)}, bf16[64,2048]{1,0:T(8,128)(2,1)S(1)}, u32[]{:S(2)}, u32[]{:S(2)}) collective-permute-start(bf16[64,2048]{1,0:T(8,128)(2,1)} %bitcast.85), channel_id=1, source_target_pairs={{0,6},{1,7},{2,4},{3,5},{4,2},{5,3},{6,0},{7,1},{8,14},{9,15},{10,... | collective-permute-start | bytes 786440 | tf_op jit(solution)/shard_map/ppermute | solution.py:364
  11.3 4.9 %all-to-all-start = ((s32[8,32,128]{2,1,0:T(8,128)}), s32[8,32,128]{2,1,0:T(8,128)S(1)}, u32[]{:S(2)}, u32[]{:S(2)}) async-start(s32[8,32,128]{2,1,0:T(8,128)} %add_add_fusion), calls=%async_computation | async-start | bytes 262144 | tf_op jit(solution)/shard_map/all_to_all | solution.py:407
  20.6 13.1 %sender.3 = (bf16[64,16384]{1,0:T(8,128)(2,1)}, f32[64,16384]{1,0:T(8,128)}) custom-call(s32[1]{0:T(128)} %bitcast.12.me_ref, bf16[64,2048]{1,0:T(8,128)(2,1)} %bitcast.88, s32[256,128]{1,0:T(8,128)} %bitcast.94, bf16[64,32768]{1,0:T(8,128)(2,1)} %bitcast.75, bf16[64,128]{1,0:T(8,128)(2,1)} %maximum_multiply_fusion.weight_ref, ...), custom_call_target="tpu_custom_call" | custom-call | tf_op jit(solution)/shard_map/sender/pallas_call | solution.py:441
  33.7 13.1 %sender.2 = (bf16[64,16384]{1,0:T(8,128)(2,1)}, f32[64,16384]{1,0:T(8,128)}) custom-call(s32[1]{0:T(128)} %bitcast.12.me_ref, bf16[64,2048]{1,0:T(8,128)(2,1)} %bitcast.89, s32[256,128]{1,0:T(8,128)} %bitcast.95, bf16[64,32768]{1,0:T(8,128)(2,1)} %bitcast.76, bf16[64,128]{1,0:T(8,128)(2,1)} %maximum_multiply_fusion.weight_ref, ...), custom_call_target="tpu_custom_call" | custom-call | tf_op jit(solution)/shard_map/sender/pallas_call | solution.py:441
  47.6 2.1 collective-permute-start.6
  49.8 1.9 collective-permute-start.4
  53.1 11.8 %forward.2 = (bf16[64,32768]{1,0:T(8,128)(2,1)}, bf16[64,16384]{1,0:T(8,128)(2,1)}, bf16[64,16384]{1,0:T(8,128)(2,1)}, bf16[64,16384]{1,0:T(8,128)(2,1)}, f32[12...) custom-call(s32[257]{0:T(512)} %pad_add_fusion.meta_ref, s32[8,32,128]{2,1,0:T(8,128)} %broadcast_and_fusion.code_ref, ...), custom_call_target="tpu_custom_call" | custom-call | tf_op jit(solution)/shard_map/forward/pallas_call | solution.py:462
  66.3 11.8 %forward.3 = (bf16[64,32768]{1,0:T(8,128)(2,1)}, bf16[64,16384]{1,0:T(8,128)(2,1)}, bf16[64,16384]{1,0:T(8,128)(2,1)}, bf16[64,16384]{1,0:T(8,128)(2,1)}, f32[12...) custom-call(s32[257]{0:T(512)} %pad_add_fusion.meta_ref, ...), custom_call_target="tpu_custom_call", output_to_operand_aliasing={{0}: (11, {})} | custom-call | tf_op jit(solution)/shard_map/forward/pallas_call | solution.py:462
  85.0 3.7 %collective-permute-done.12 = bf16[64,2048]{1,0:T(8,128)(2,1)S(1)} collective-permute-done((bf16[64,2048]{1,0:T(8,128)(2,1)S(1)}, bf16[64,2048]{1,0:T(8,128)(2,1)S(1)}, u32[]{:S(2)}, u32[]{:S(2)}) %collective-permute-start.12) | collective-permute-done | bytes 262176 | tf_op jit(solution)/shard_map/ppermute | solution.py:364
  88.7 5.6 %collective-permute-done.10 = bf16[64,2048]{1,0:T(8,128)(2,1)S(1)} collective-permute-done((bf16[64,2048]{1,0:T(8,128)(2,1)S(1)}, bf16[64,2048]{1,0:T(8,128)(2,1)S(1)}, u32[]{:S(2)}, u32[]{:S(2)}) %collective-permute-start.10) | collective-permute-done | bytes 262176 | tf_op jit(solution)/shard_map/ppermute | solution.py:364
  94.3 5.0 %collective-permute-done.8 = bf16[64,2048]{1,0:T(8,128)(2,1)S(1)} collective-permute-done((bf16[64,2048]{1,0:T(8,128)(2,1)S(1)}, bf16[64,2048]{1,0:T(8,128)(2,1)S(1)}, u32[]{:S(2)}, u32[]{:S(2)}) %collective-permute-start.8) | collective-permute-done | bytes 262176 | tf_op jit(solution)/shard_map/ppermute | solution.py:364
  101.1 2.4 collective-permute-start.11
  104.2 2.3 collective-permute-done.13.rest_4_
  106.6 5.3 %collective-permute-done.11.rest_3_ = bf16[64,2048]{1,0:T(8,128)(2,1)S(1)} collective-permute-done((bf16[64,2048]{1,0:T(8,128)(2,1)S(1)}, bf16[64,2048]{1,0:T(8,128)(2,1)S(1)}, u32[]{:S(2)}, u32[]{:S(2)}) %collective-permute-start.11) | collective-permute-done | bytes 262176 | tf_op jit(solution)/shard_map/ppermute | solution.py:364
  111.9 8.3 %collective-permute-done.9.rest_2_ = bf16[64,2048]{1,0:T(8,128)(2,1)S(1)} collective-permute-done((bf16[64,2048]{1,0:T(8,128)(2,1)S(1)}, bf16[64,2048]{1,0:T(8,128)(2,1)S(1)}, u32[]{:S(2)}, u32[]{:S(2)}) %collective-permute-start.9) | collective-permute-done | bytes 262176 | tf_op jit(solution)/shard_map/ppermute | solution.py:364
  120.9 3.9 %node.1 = (bf16[64,2048]{1,0:T(8,128)(2,1)}, f32[64,2048]{1,0:T(8,128)}, bf16[64,2048]{1,0:T(8,128)(2,1)}, f32[72,256]{1,0:T(8,128)}) custom-call(bf16[64,2048]{1,0:T(8,128)(2,1)} %bitcast.91, bf16[64,2048]{1,0:T(8,128)(2,1)} %bitcast.100, bf16[64,128]{1,0:T(8,128)(2,1)} %bitcast.104, bf16[128,64]{1,0:T(8,128)(2,1)} %copy.47.in_ref, ...), custom_call_target="tpu_custom_call" | custom-call | tf_op jit(solution)/shard_map/node/pallas_call | solution.py:491
  124.8 2.6 %collective-permute-start.24 = (bf16[64,2048]{1,0:T(8,128)(2,1)}, bf16[64,2048]{1,0:T(8,128)(2,1)S(1)}, u32[]{:S(2)}, u32[]{:S(2)}) collective-permute-start(bf16[64,2048]{1,0:T(8,128)(2,1)} %get-tuple-element.71.rest_0_), channel_id=1, source_target_pairs={{0,6},{1,7},{2,4},{3,5},{4,2},{5,3},{6,0},{7,1},{8,14},{9,15},{10,... | collective-permute-start | bytes 786440 | tf_op jit(solution)/shard_map/ppermute | solution.py:364
  130.6 5.4 %collective-permute-done.24.rest_3_ = bf16[64,2048]{1,0:T(8,128)(2,1)S(1)} collective-permute-done((bf16[64,2048]{1,0:T(8,128)(2,1)}, bf16[64,2048]{1,0:T(8,128)(2,1)S(1)}, u32[]{:S(2)}, u32[]{:S(2)}) %collective-permute-start.24) | collective-permute-done | bytes 262176 | tf_op jit(solution)/shard_map/ppermute | solution.py:364
  137.4 9.6 %collective-permute-done.22.rest_2_ = bf16[64,2048]{1,0:T(8,128)(2,1)S(1)} collective-permute-done((bf16[64,2048]{1,0:T(8,128)(2,1)}, bf16[64,2048]{1,0:T(8,128)(2,1)S(1)}, u32[]{:S(2)}, u32[]{:S(2)}) %collective-permute-start.22) | collective-permute-done | bytes 262176 | tf_op jit(solution)/shard_map/ppermute | solution.py:364
  150.5 16.3 %backward.2 = (f32[64,32768]{1,0:T(8,128)}, bf16[64,16384]{1,0:T(8,128)(2,1)}, bf16[4,64,2048]{2,1,0:T(8,128)(2,1)}, f32[72,256]{1,0:T(8,128)}) custom-call(s32[257]{0:T(512)} %pad_add_fusion.meta_ref, s32[8,32,128]{2,1,0:T(8,128)} %broadcast_and_fusion.code_ref, bf16[64,32768]{1,0:T(8,128)(2,1)} %bitcast.81, ...), custom_call_target="tpu_custom_call" | custom-call | tf_op jit(solution)/shard_map/backward/pallas_call | solution.py:514
  167.7 16.0 %backward.3 = (f32[64,32768]{1,0:T(8,128)}, bf16[64,16384]{1,0:T(8,128)(2,1)}, bf16[4,64,2048]{2,1,0:T(8,128)(2,1)}, f32[72,256]{1,0:T(8,128)}) custom-call(s32[257]{0:T(512)} %pad_add_fusion.meta_ref, s32[8,32,128]{2,1,0:T(8,128)} %broadcast_and_fusion.code_ref, bf16[64,32768]{1,0:T(8,128)(2,1)} %bitcast.82, ...), custom_call_target="tpu_custom_call", output_to_operand_aliasing={{0}: (20, {})} | custom-call | tf_op jit(solution)/shard_map/backward/pallas_call | solution.py:514
  190.2 2.8 %collective-permute-done.15 = f32[72,256]{1,0:T(8,128)S(1)} collective-permute-done((f32[72,256]{1,0:T(8,128)S(1)}, f32[72,256]{1,0:T(8,128)S(1)}, u32[]{:S(2)}, u32[]{:S(2)}) %collective-permute-start.15) | collective-permute-done | bytes 73760 | tf_op jit(solution)/shard_map/ppermute | solution.py:389
  195.4 11.3 %collective-permute-done.16 = f32[72,256]{1,0:T(8,128)S(1)} collective-permute-done((f32[72,256]{1,0:T(8,128)S(1)}, f32[72,256]{1,0:T(8,128)S(1)}, u32[]{:S(2)}, u32[]{:S(2)}) %collective-permute-start.16) | collective-permute-done | bytes 73760 | tf_op jit(solution)/shard_map/ppermute | solution.py:389
  208.9 2.3 collective-permute-done.17
  212.7 2.1 collective-permute-start.29
  215.2 2.2 collective-permute-start.35
  218.4 2.3 collective-permute-start.33
  222.1 7.2 %sender_sum.2.rest_0_ = f32[64,2048]{1,0:T(8,128)} custom-call(s32[1]{0:T(128)} %bitcast.12.me_ref, bf16[64,16384]{1,0:T(8,128)(2,1)} %get-tuple-element.80.grad_ref, s32[256,128]{1,0:T(8,128)} %bitcast.96), custom_call_target="tpu_custom_call" | custom-call | tf_op jit(solution)/shard_map/sender_sum/pallas_call | solution.py:555
  229.9 7.1 %sender_sum.3.rest_1_ = f32[64,2048]{1,0:T(8,128)} custom-call(s32[1]{0:T(128)} %bitcast.12.me_ref, bf16[64,16384]{1,0:T(8,128)(2,1)} %get-tuple-element.81.grad_ref, s32[256,128]{1,0:T(8,128)} %bitcast.97), custom_call_target="tpu_custom_call" | custom-call | tf_op jit(solution)/shard_map/sender_sum/pallas_call | solution.py:555
  237.1 5.4 %collective-permute-done.30 = f32[72,256]{1,0:T(8,128)S(1)} collective-permute-done((f32[72,256]{1,0:T(8,128)S(1)}, f32[72,256]{1,0:T(8,128)S(1)}, u32[]{:S(2)}, u32[]{:S(2)}) %collective-permute-start.30) | collective-permute-done | bytes 73760 | tf_op jit(solution)/shard_map/ppermute | solution.py:389
  244.1 3.3 %finish.1 = (f32[64,2048]{1,0:T(8,128)}, f32[64,192]{1,0:T(8,128)}, f32[1,64]{1,0:T(1,128)}, f32[64,64]{1,0:T(8,128)}, f32[1,64]{1,0:T(1,128)}, /*index=5*/f32[1...) custom-call(f32[64,2048]{1,0:T(8,128)} %get-tuple-element.64.base_re, ...), custom_call_target="tpu_custom_call" | custom-call | tf_op jit(solution)/shard_map/finish/pallas_call | solution.py:572
  (154 shorter events, 48.7 us)
Async XLA Ops:
  0.6 64.3 %collective-permute-start.3 = (bf16[64,2048]{1,0:T(8,128)(2,1)}, bf16[64,2048]{1,0:T(8,128)(2,1)S(1)}, u32[]{:S(2)}, u32[]{:S(2)}) collective-permute-start(bf16[64,2048]{1,0:T(8,128)(2,1)} %bitcast.84), channel_id=1, source_target_pairs={{0,1},{1,0},{2,3},{3,2},{4,5},{5,4},{6,7},{7,6},{8,9},{9,8},{10,11... | collective-permute-start | bytes 786440 | tf_op jit(solution)/shard_map/ppermute | solution.py:364
  3.7 43.9 %collective-permute-start.2 = (bf16[64,2048]{1,0:T(8,128)(2,1)}, bf16[64,2048]{1,0:T(8,128)(2,1)S(1)}, u32[]{:S(2)}, u32[]{:S(2)}) collective-permute-start(bf16[64,2048]{1,0:T(8,128)(2,1)} %bitcast.85), channel_id=1, source_target_pairs={{0,6},{1,7},{2,4},{3,5},{4,2},{5,3},{6,0},{7,1},{8,14},{9,15},{10,... | collective-permute-start | bytes 786440 | tf_op jit(solution)/shard_map/ppermute | solution.py:364
  7.3 42.4 %collective-permute-start.1 = (bf16[64,2048]{1,0:T(8,128)(2,1)}, bf16[64,2048]{1,0:T(8,128)(2,1)S(1)}, u32[]{:S(2)}, u32[]{:S(2)}) collective-permute-start(bf16[64,2048]{1,0:T(8,128)(2,1)} %bitcast.86), channel_id=1, source_target_pairs={{0,4},{1,5},{2,6},{3,7},{4,0},{5,1},{6,2},{7,3},{8,12},{9,13},{10,... | collective-permute-start | bytes 786440 | tf_op jit(solution)/shard_map/ppermute | solution.py:364
  7.3 42.5 %collective-permute-start = (bf16[64,2048]{1,0:T(8,128)(2,1)}, bf16[64,2048]{1,0:T(8,128)(2,1)S(1)}, u32[]{:S(2)}, u32[]{:S(2)}) collective-permute-start(bf16[64,2048]{1,0:T(8,128)(2,1)} %bitcast.87), channel_id=1, source_target_pairs={{0,2},{1,3},{2,0},{3,1},{4,6},{5,7},{6,4},{7,5},{8,10},{9,11},{10,... | collective-permute-start | bytes 786440 | tf_op jit(solution)/shard_map/ppermute | solution.py:364
  11.3 36.2 %all-to-all-start = ((s32[8,32,128]{2,1,0:T(8,128)}), s32[8,32,128]{2,1,0:T(8,128)S(1)}, u32[]{:S(2)}, u32[]{:S(2)}) async-start(s32[8,32,128]{2,1,0:T(8,128)} %add_add_fusion), calls=%async_computation | async-start | bytes 262144 | tf_op jit(solution)/shard_map/all_to_all | solution.py:407
  47.6 17.3 %collective-permute-start.6 = (bf16[64,2048]{1,0:T(8,128)(2,1)S(1)}, bf16[64,2048]{1,0:T(8,128)(2,1)S(1)}, u32[]{:S(2)}, u32[]{:S(2)}) collective-permute-start(bf16[64,2048]{1,0:T(8,128)(2,1)S(1)} %collective-permute-done.2.rest_3_.rest_7_), channel_id=1, source_target_pairs={{0,1},{1,0},{2,3},{3,2},{4,5},{5,4},{6,7},{7,6},{8,9},{9,8},{10,11... | collective-permute-start | bytes 786440 | tf_op jit(solution)/shard_map/ppermute | solution.py:364
  49.7 15.2 %collective-permute-start.5 = (bf16[64,2048]{1,0:T(8,128)(2,1)S(1)}, bf16[64,2048]{1,0:T(8,128)(2,1)S(1)}, u32[]{:S(2)}, u32[]{:S(2)}) collective-permute-start(bf16[64,2048]{1,0:T(8,128)(2,1)S(1)} %collective-permute-done.1.rest_2_.rest_6_), channel_id=1, source_target_pairs={{0,1},{1,0},{2,3},{3,2},{4,5},{5,4},{6,7},{7,6},{8,9},{9,8},{10,11... | collective-permute-start | bytes 786440 | tf_op jit(solution)/shard_map/ppermute | solution.py:364
  49.8 15.8 %collective-permute-start.4 = (bf16[64,2048]{1,0:T(8,128)(2,1)S(1)}, bf16[64,2048]{1,0:T(8,128)(2,1)S(1)}, u32[]{:S(2)}, u32[]{:S(2)}) collective-permute-start(bf16[64,2048]{1,0:T(8,128)(2,1)S(1)} %collective-permute-done.rest_1_.rest_5_), channel_id=1, source_target_pairs={{0,1},{1,0},{2,3},{3,2},{4,5},{5,4},{6,7},{7,6},{8,9},{9,8},{10,11... | collective-permute-start | bytes 786440 | tf_op jit(solution)/shard_map/ppermute | solution.py:364
  81.2 13.1 %collective-permute-start.10 = (bf16[64,2048]{1,0:T(8,128)(2,1)S(1)}, bf16[64,2048]{1,0:T(8,128)(2,1)S(1)}, u32[]{:S(2)}, u32[]{:S(2)}) collective-permute-start(bf16[64,2048]{1,0:T(8,128)(2,1)S(1)} %get-tuple-element.109), channel_id=1, source_target_pairs={{0,1},{1,0},{2,3},{3,2},{4,5},{5,4},{6,7},{7,6},{8,9},{9,8},{10,11... | collective-permute-start | bytes 786440 | tf_op jit(solution)/shard_map/ppermute | solution.py:364
  81.5 17.8 %collective-permute-start.8 = (bf16[64,2048]{1,0:T(8,128)(2,1)S(1)}, bf16[64,2048]{1,0:T(8,128)(2,1)S(1)}, u32[]{:S(2)}, u32[]{:S(2)}) collective-permute-start(bf16[64,2048]{1,0:T(8,128)(2,1)S(1)} %get-tuple-element.110), channel_id=1, source_target_pairs={{0,1},{1,0},{2,3},{3,2},{4,5},{5,4},{6,7},{7,6},{8,9},{9,8},{10,11... | collective-permute-start | bytes 786440 | tf_op jit(solution)/shard_map/ppermute | solution.py:364
  84.7 19.6 %collective-permute-start.7 = (bf16[64,2048]{1,0:T(8,128)(2,1)S(1)}, bf16[64,2048]{1,0:T(8,128)(2,1)S(1)}, u32[]{:S(2)}, u32[]{:S(2)}) collective-permute-start(bf16[64,2048]{1,0:T(8,128)(2,1)S(1)} %get-tuple-element.111), channel_id=1, source_target_pairs={{0,1},{1,0},{2,3},{3,2},{4,5},{5,4},{6,7},{7,6},{8,9},{9,8},{10,11... | collective-permute-start | bytes 786440 | tf_op jit(solution)/shard_map/ppermute | solution.py:364
  101.1 10.8 %collective-permute-start.11 = (bf16[64,2048]{1,0:T(8,128)(2,1)S(1)}, bf16[64,2048]{1,0:T(8,128)(2,1)S(1)}, u32[]{:S(2)}, u32[]{:S(2)}) collective-permute-start(bf16[64,2048]{1,0:T(8,128)(2,1)S(1)} %get-tuple-element.106), channel_id=1, source_target_pairs={{0,6},{1,7},{2,4},{3,5},{4,2},{5,3},{6,0},{7,1},{8,14},{9,15},{10,... | collective-permute-start | bytes 786440 | tf_op jit(solution)/shard_map/ppermute | solution.py:364
  103.5 16.7 %collective-permute-start.9 = (bf16[64,2048]{1,0:T(8,128)(2,1)S(1)}, bf16[64,2048]{1,0:T(8,128)(2,1)S(1)}, u32[]{:S(2)}, u32[]{:S(2)}) collective-permute-start(bf16[64,2048]{1,0:T(8,128)(2,1)S(1)} %get-tuple-element.107), channel_id=1, source_target_pairs={{0,4},{1,5},{2,6},{3,7},{4,0},{5,1},{6,2},{7,3},{8,12},{9,13},{10,... | collective-permute-start | bytes 786440 | tf_op jit(solution)/shard_map/ppermute | solution.py:364
  124.8 11.2 %collective-permute-start.24 = (bf16[64,2048]{1,0:T(8,128)(2,1)}, bf16[64,2048]{1,0:T(8,128)(2,1)S(1)}, u32[]{:S(2)}, u32[]{:S(2)}) collective-permute-start(bf16[64,2048]{1,0:T(8,128)(2,1)} %get-tuple-element.71.rest_0_), channel_id=1, source_target_pairs={{0,6},{1,7},{2,4},{3,5},{4,2},{5,3},{6,0},{7,1},{8,14},{9,15},{10,... | collective-permute-start | bytes 786440 | tf_op jit(solution)/shard_map/ppermute | solution.py:364
  127.4 19.6 %collective-permute-start.22 = (bf16[64,2048]{1,0:T(8,128)(2,1)}, bf16[64,2048]{1,0:T(8,128)(2,1)S(1)}, u32[]{:S(2)}, u32[]{:S(2)}) collective-permute-start(bf16[64,2048]{1,0:T(8,128)(2,1)} %get-tuple-element.71.rest_0_), channel_id=1, source_target_pairs={{0,4},{1,5},{2,6},{3,7},{4,0},{5,1},{6,2},{7,3},{8,12},{9,13},{10,... | collective-permute-start | bytes 786440 | tf_op jit(solution)/shard_map/ppermute | solution.py:364
  127.4 21.0 %collective-permute-start.20 = (bf16[64,2048]{1,0:T(8,128)(2,1)}, bf16[64,2048]{1,0:T(8,128)(2,1)S(1)}, u32[]{:S(2)}, u32[]{:S(2)}) collective-permute-start(bf16[64,2048]{1,0:T(8,128)(2,1)} %get-tuple-element.71.rest_0_), channel_id=1, source_target_pairs={{0,2},{1,3},{2,0},{3,1},{4,6},{5,7},{6,4},{7,5},{8,10},{9,11},{10,... | collective-permute-start | bytes 786440 | tf_op jit(solution)/shard_map/ppermute | solution.py:364
  129.2 37.6 %collective-permute-start.19 = (bf16[64,2048]{1,0:T(8,128)(2,1)}, bf16[64,2048]{1,0:T(8,128)(2,1)S(1)}, u32[]{:S(2)}, u32[]{:S(2)}) collective-permute-start(bf16[64,2048]{1,0:T(8,128)(2,1)} %get-tuple-element.71.rest_0_), channel_id=1, source_target_pairs={{0,1},{1,0},{2,3},{3,2},{4,5},{5,4},{6,7},{7,6},{8,9},{9,8},{10,11... | collective-permute-start | bytes 786440 | tf_op jit(solution)/shard_map/ppermute | solution.py:364
  136.0 30.8 %collective-permute-start.25 = (bf16[64,2048]{1,0:T(8,128)(2,1)S(1)}, bf16[64,2048]{1,0:T(8,128)(2,1)S(1)}, u32[]{:S(2)}, u32[]{:S(2)}) collective-permute-start(bf16[64,2048]{1,0:T(8,128)(2,1)S(1)} %collective-permute-done.24.rest_3_), channel_id=1, source_target_pairs={{0,1},{1,0},{2,3},{3,2},{4,5},{5,4},{6,7},{7,6},{8,9},{9,8},{10,11... | collective-permute-start | bytes 786440 | tf_op jit(solution)/shard_map/ppermute | solution.py:364
  147.0 19.7 %collective-permute-start.23 = (bf16[64,2048]{1,0:T(8,128)(2,1)S(1)}, bf16[64,2048]{1,0:T(8,128)(2,1)S(1)}, u32[]{:S(2)}, u32[]{:S(2)}) collective-permute-start(bf16[64,2048]{1,0:T(8,128)(2,1)S(1)} %collective-permute-done.22.rest_2_), channel_id=1, source_target_pairs={{0,1},{1,0},{2,3},{3,2},{4,5},{5,4},{6,7},{7,6},{8,9},{9,8},{10,11... | collective-permute-start | bytes 786440 | tf_op jit(solution)/shard_map/ppermute | solution.py:364
  148.4 18.4 %collective-permute-start.21 = (bf16[64,2048]{1,0:T(8,128)(2,1)S(1)}, bf16[64,2048]{1,0:T(8,128)(2,1)S(1)}, u32[]{:S(2)}, u32[]{:S(2)}) collective-permute-start(bf16[64,2048]{1,0:T(8,128)(2,1)S(1)} %collective-permute-done.20.rest_1_), channel_id=1, source_target_pairs={{0,1},{1,0},{2,3},{3,2},{4,5},{5,4},{6,7},{7,6},{8,9},{9,8},{10,11... | collective-permute-start | bytes 786440 | tf_op jit(solution)/shard_map/ppermute | solution.py:364
  150.5 38.0 %collective-permute-start.14 = (f32[72,256]{1,0:T(8,128)}, f32[72,256]{1,0:T(8,128)S(1)}, u32[]{:S(2)}, u32[]{:S(2)}) collective-permute-start(f32[72,256]{1,0:T(8,128)} %get-tuple-element.65), channel_id=1, source_target_pairs={{0,8},{8,0},{16,24},{24,16},{1,9},{9,1},{17,25},{25,17},{2,10},{10... | collective-permute-start | bytes 221192 | tf_op jit(solution)/shard_map/ppermute | solution.py:389
  185.1 27.6 %collective-permute-start.36 = (bf16[64,2048]{1,0:T(8,128)(2,1)S(1)}, bf16[64,2048]{1,0:T(8,128)(2,1)S(1)}, u32[]{:S(2)}, u32[]{:S(2)}) collective-permute-start(bf16[64,2048]{1,0:T(8,128)(2,1)S(1)} %get-tuple-element.101), channel_id=1, source_target_pairs={{0,1},{1,0},{2,3},{3,2},{4,5},{5,4},{6,7},{7,6},{8,9},{9,8},{10,11... | collective-permute-start | bytes 786440 | tf_op jit(solution)/shard_map/ppermute | solution.py:364
  186.5 28.4 %collective-permute-start.34 = (bf16[64,2048]{1,0:T(8,128)(2,1)S(1)}, bf16[64,2048]{1,0:T(8,128)(2,1)S(1)}, u32[]{:S(2)}, u32[]{:S(2)}) collective-permute-start(bf16[64,2048]{1,0:T(8,128)(2,1)S(1)} %get-tuple-element.102), channel_id=1, source_target_pairs={{0,1},{1,0},{2,3},{3,2},{4,5},{5,4},{6,7},{7,6},{8,9},{9,8},{10,11... | collective-permute-start | bytes 786440 | tf_op jit(solution)/shard_map/ppermute | solution.py:364
  187.2 27.6 %collective-permute-start.32 = (bf16[64,2048]{1,0:T(8,128)(2,1)S(1)}, bf16[64,2048]{1,0:T(8,128)(2,1)S(1)}, u32[]{:S(2)}, u32[]{:S(2)}) collective-permute-start(bf16[64,2048]{1,0:T(8,128)(2,1)S(1)} %get-tuple-element.103), channel_id=1, source_target_pairs={{0,1},{1,0},{2,3},{3,2},{4,5},{5,4},{6,7},{7,6},{8,9},{9,8},{10,11... | collective-permute-start | bytes 786440 | tf_op jit(solution)/shard_map/ppermute | solution.py:364
  192.9 13.8 %collective-permute-start.16 = (f32[72,256]{1,0:T(8,128)S(1)}, f32[72,256]{1,0:T(8,128)S(1)}, u32[]{:S(2)}, u32[]{:S(2)}) collective-permute-start(f32[72,256]{1,0:T(8,128)S(1)} %add.72), channel_id=1, source_target_pairs={{0,1},{1,0},{2,3},{3,2},{4,5},{5,4},{6,7},{7,6},{8,9},{9,8},{10,11... | collective-permute-start | bytes 221192 | tf_op jit(solution)/shard_map/ppermute | solution.py:389
  193.8 13.0 %collective-permute-start.27 = (f32[72,256]{1,0:T(8,128)S(1)}, f32[72,256]{1,0:T(8,128)S(1)}, u32[]{:S(2)}, u32[]{:S(2)}) collective-permute-start(f32[72,256]{1,0:T(8,128)S(1)} %add.76), channel_id=1, source_target_pairs={{0,16},{8,24},{16,0},{24,8},{1,17},{9,25},{17,1},{25,9},{2,18},{10... | collective-permute-start | bytes 221192 | tf_op jit(solution)/shard_map/ppermute | solution.py:389
  211.2 9.5 %collective-permute-start.18 = (f32[72,256]{1,0:T(8,128)S(1)}, f32[72,256]{1,0:T(8,128)S(1)}, u32[]{:S(2)}, u32[]{:S(2)}) collective-permute-start(f32[72,256]{1,0:T(8,128)S(1)} %add.74), channel_id=1, source_target_pairs={{0,4},{1,5},{2,6},{3,7},{4,0},{5,1},{6,2},{7,3},{8,12},{9,13},{10,... | collective-permute-start | bytes 221192 | tf_op jit(solution)/shard_map/ppermute | solution.py:389
  211.3 31.8 %collective-permute-start.31 = (bf16[64,2048]{1,0:T(8,128)(2,1)S(1)}, bf16[64,2048]{1,0:T(8,128)(2,1)S(1)}, u32[]{:S(2)}, u32[]{:S(2)}) collective-permute-start(bf16[64,2048]{1,0:T(8,128)(2,1)S(1)} %get-tuple-element.104), channel_id=1, source_target_pairs={{0,1},{1,0},{2,3},{3,2},{4,5},{5,4},{6,7},{7,6},{8,9},{9,8},{10,11... | collective-permute-start | bytes 786440 | tf_op jit(solution)/shard_map/ppermute | solution.py:364
  215.1 28.0 %collective-permute-start.37 = (bf16[64,2048]{1,0:T(8,128)(2,1)S(1)}, bf16[64,2048]{1,0:T(8,128)(2,1)S(1)}, u32[]{:S(2)}, u32[]{:S(2)}) collective-permute-start(bf16[64,2048]{1,0:T(8,128)(2,1)S(1)} %get-tuple-element.98), channel_id=1, source_target_pairs={{0,2},{1,3},{2,0},{3,1},{4,6},{5,7},{6,4},{7,5},{8,10},{9,11},{10,... | collective-permute-start | bytes 786440 | tf_op jit(solution)/shard_map/ppermute | solution.py:364
  215.2 27.9 %collective-permute-start.35 = (bf16[64,2048]{1,0:T(8,128)(2,1)S(1)}, bf16[64,2048]{1,0:T(8,128)(2,1)S(1)}, u32[]{:S(2)}, u32[]{:S(2)}) collective-permute-start(bf16[64,2048]{1,0:T(8,128)(2,1)S(1)} %get-tuple-element.99), channel_id=1, source_target_pairs={{0,6},{1,7},{2,4},{3,5},{4,2},{5,3},{6,0},{7,1},{8,14},{9,15},{10,... | collective-permute-start | bytes 786440 | tf_op jit(solution)/shard_map/ppermute | solution.py:364
  218.4 24.8 %collective-permute-start.33 = (bf16[64,2048]{1,0:T(8,128)(2,1)S(1)}, bf16[64,2048]{1,0:T(8,128)(2,1)S(1)}, u32[]{:S(2)}, u32[]{:S(2)}) collective-permute-start(bf16[64,2048]{1,0:T(8,128)(2,1)S(1)} %get-tuple-element.100), channel_id=1, source_target_pairs={{0,4},{1,5},{2,6},{3,7},{4,0},{5,1},{6,2},{7,3},{8,12},{9,13},{10,... | collective-permute-start | bytes 786440 | tf_op jit(solution)/shard_map/ppermute | solution.py:364
  220.7 21.8 %collective-permute-start.30 = (f32[72,256]{1,0:T(8,128)S(1)}, f32[72,256]{1,0:T(8,128)S(1)}, u32[]{:S(2)}, u32[]{:S(2)}) collective-permute-start(f32[72,256]{1,0:T(8,128)S(1)} %add.79), channel_id=1, source_target_pairs={{0,4},{1,5},{2,6},{3,7},{4,0},{5,1},{6,2},{7,3},{8,12},{9,13},{10,... | collective-permute-start | bytes 221192 | tf_op jit(solution)/shard_map/ppermute | solution.py:389
  (37 other events, 256.6 us)

commit v3 on v2

--- a/solution.py
+++ b/solution.py
@@ -36,7 +36,7 @@
     )
 
 
-def params(limit=56):
+def params(limit=48):
     return pltpu.CompilerParams(vmem_limit_bytes=limit * 1024 * 1024)
 
 
@@ -81,7 +81,9 @@
     )
 
 
-def sender_kernel(piece, me_ref, node_ref, send_ref, edge_ref, weight_ref, vec_ref, pick_ref, base_ref):
+def sender_kernel(piece, extra, me_ref, node_ref, send_ref, edge_ref, weight_ref, vec_ref, *rest):
+    pick_ref, base_ref, token_ref = rest[extra:]
+    token_ref[...] = jnp.zeros_like(token_ref)
     width = edge_ref.shape[1]
     feat = edge_ref.shape[0]
     groups = node_ref.shape[1] // WIDE
@@ -128,17 +130,25 @@
 def forward_kernel(masks, blocks, piece, extra, meta_ref, code_ref, base_ref, edge_ref, in_ref, out_ref, vec_ref, *rest):
     count = len(masks)
     shard_refs = rest[:count]
-    result_ref, act_ref, slope_ref, normed_ref, inv_ref, part_ref, proj_ref, total_ref = rest[count + extra :]
+    result_ref, act_ref, slope_ref, normed_ref, inv_ref, token_ref = rest[count + extra : count + extra + 6]
+    part_refs = rest[count + extra + 6 : -2]
+    proj_ref, total_ref = rest[-2:]
+    token_ref[...] = jnp.zeros_like(token_ref)
     step = pl.program_id(0)
-    for k in range(count):
-
-        @pl.when(step == k)
-        def _():
-            proj_ref[...] = dot(in_ref[...], shard_refs[k][...])
-
-    total_ref[...] = jnp.zeros_like(total_ref)
+    inner = pl.program_id(1)
+
+    @pl.when(inner == 0)
+    def _():
+        for k in range(count):
+
+            @pl.when(step == k)
+            def _():
+                proj_ref[...] = dot(in_ref[...], shard_refs[k][...])
+
+        total_ref[...] = jnp.zeros_like(total_ref)
+
     width = edge_ref.shape[1]
-    first = 1 + owner(masks, step, meta_ref) * blocks
+    first = 1 + owner(masks, step, meta_ref) * blocks + inner * (width // LANES)
     per = piece // LANES
     place = place_low()
     for start in range(0, width, piece):
@@ -160,7 +170,15 @@
         message = (normed * spread(vec_ref[2], piece) + spread(vec_ref[3], piece)).astype(bf16)
         result_ref[:, lanes] = edge_ref[:, lanes] + message
         scatter_blocks(meta_ref, first, code_ref, block, per, message, total_ref, place)
-    part_ref[0] = total_ref[...].astype(bf16)
+
+    @pl.when(inner == pl.num_programs(1) - 1)
+    def _():
+        low = total_ref[...].astype(bf16)
+        for k in range(count):
+
+            @pl.when(step == k)
+            def _():
+                part_refs[k][...] = low
 
 
 def node_kernel(peers, node_ref, cot_ref, in_t_ref, in_ref, out_t_ref, out_ref, vec_ref, *rest):
@@ -214,25 +232,32 @@
     back_refs = rest[:count]
     shard_refs = rest[count : 2 * count]
     prior_refs = rest[2 * count : 2 * count + extra]
-    grad_ref, first_ref, part_ref, pack_ref, pull_ref, total_ref, w1_ref, wr_ref, w2_ref, sum_ref = rest[2 * count + extra :]
+    grad_ref, first_ref, pack_ref, token_ref = rest[2 * count + extra : 2 * count + extra + 4]
+    part_refs = rest[2 * count + extra + 4 : -6]
+    pull_ref, total_ref, w1_ref, wr_ref, w2_ref, sum_ref = rest[-6:]
     step = pl.program_id(0)
+    inner = pl.program_id(1)
     feat, width = edge_ref.shape
-
-    @pl.when(step == 0)
+    token_ref[...] = jnp.zeros_like(token_ref)
+
+    @pl.when((step == 0) & (inner == 0))
     def _():
         w1_ref[...] = jnp.zeros_like(w1_ref)
         wr_ref[...] = jnp.zeros_like(wr_ref)
         w2_ref[...] = jnp.zeros_like(w2_ref)
         sum_ref[...] = jnp.zeros_like(sum_ref)
 
-    for k in range(count):
-
-        @pl.when(step == k)
-        def _():
-            pull_ref[...] = back_refs[k][...].astype(f32)
-
-    total_ref[...] = jnp.zeros_like(total_ref)
-    first = 1 + owner(masks, step, meta_ref) * blocks
+    @pl.when(inner == 0)
+    def _():
+        for k in range(count):
+
+            @pl.when(step == k)
+            def _():
+                pull_ref[...] = back_refs[k][...].astype(f32)
+
+        total_ref[...] = jnp.zeros_like(total_ref)
+
+    first = 1 + owner(masks, step, meta_ref) * blocks + inner * (width // LANES)
     per = piece // LANES
     place = place_low()
     for start in range(0, width, piece):
@@ -259,15 +284,19 @@
         both = jnp.concatenate([pick_ref[:, lanes], edge_ref[:, lanes]], axis=0)
         w1_ref[...] += dot_nt(grad, both)
         scatter_blocks(meta_ref, first, code_ref, block, per, grad, total_ref, place)
-    low = total_ref[...].astype(bf16)
-    part_ref[0] = low
-    for k in range(count):
-
-        @pl.when(step == k)
-        def _():
-            wr_ref[...] += dot_nt(low, shard_refs[k][...])
-
-    @pl.when(step == pl.num_programs(0) - 1)
+    last = inner == pl.num_programs(1) - 1
+
+    @pl.when(last)
+    def _():
+        low = total_ref[...].astype(bf16)
+        for k in range(count):
+
+            @pl.when(step == k)
+            def _():
+                part_refs[k][...] = low
+                wr_ref[...] += dot_nt(low, shard_refs[k][...])
+
+    @pl.when(last & (step == pl.num_programs(0) - 1))
     def _():
         pack_ref[...] = jnp.zeros_like(pack_ref)
         pack_ref[:feat, :feat] = w1_ref[:, :feat]
@@ -278,36 +307,36 @@
         for k in range(4):
             pack_ref[feat + k : feat + k + 1, :feat] = dot_nt_exact(ones, sum_ref[k])[:1]
         if extra:
-            pack_ref[...] += prior_refs[1][...]
-
-
-def sender_sum_kernel(me_ref, grad_ref, send_ref, sum_ref, total_ref):
+            pack_ref[...] += prior_refs[2][...]
+
+
+def sender_sum_kernel(grad_ref, send_ref, sum_ref, token_ref, total_ref):
     feat, width = grad_ref.shape
     groups = sum_ref.shape[1] // WIDE
-
-    @pl.when(pl.program_id(0) == 0)
+    step = pl.program_id(0)
+    token_ref[...] = jnp.zeros_like(token_ref)
+
+    @pl.when(step == 0)
     def _():
         total_ref[...] = jnp.zeros_like(total_ref)
 
-    piece = min(2048, width)
-    for start in range(0, width, piece):
-        ids = row_join(send_ref, start // LANES, piece // LANES)
-        onehot = onehot_rows(ids & (WIDE - 1), WIDE)
-        group = jnp.broadcast_to(lax.shift_right_logical(ids, 8).astype(bf16), (feat, piece))
-        values = grad_ref[:, start : start + piece]
-        zero = jnp.zeros((), bf16)
-        masked = jnp.concatenate(
-            [jnp.where(group == jnp.asarray(g, bf16), values, zero) for g in range(groups)], axis=0
-        )
-        total_ref[...] += dot_nt(masked, onehot)
-
-    @pl.when(pl.program_id(0) == pl.num_programs(0) - 1)
+    ids = row_join(send_ref, 0, width // LANES)
+    onehot = onehot_rows(ids & (WIDE - 1), WIDE)
+    group = jnp.broadcast_to(lax.shift_right_logical(ids, 8).astype(bf16), (feat, width))
+    values = grad_ref[...]
+    zero = jnp.zeros((), bf16)
+    masked = jnp.concatenate(
+        [jnp.where(group == jnp.asarray(g, bf16), values, zero) for g in range(groups)], axis=0
+    )
+    total_ref[...] += dot_nt(masked, onehot)
+
+    @pl.when(step == pl.num_programs(0) - 1)
     def _():
         for g in range(groups):
             sum_ref[:, g * WIDE : (g + 1) * WIDE] = total_ref[g * feat : (g + 1) * feat, :]
 
 
-def finish_kernel(sums, peers, base_ref, weight_ref, node_pack_ref, edge_pack_ref, *rest):
+def finish_kernel(sums, peers, base_ref, weight_ref, pack_ref, *rest):
     sum_refs = rest[:sums]
     part_refs = rest[sums : sums + peers]
     grad_ref, e1, b1, e2, b2, g1, s1, n1, c1, n2, c2, g2, s2 = rest[sums + peers :]
@@ -320,19 +349,52 @@
     both = jnp.concatenate([sent, total], axis=0)
     grad_ref[...] = base_ref[...] + dot_exact(weight_ref[...], both)
     feat = base_ref.shape[0]
-    e1[...] = edge_pack_ref[:feat, : 3 * feat]
-    e2[...] = edge_pack_ref[:feat, 3 * feat : 4 * feat]
-    n1[...] = node_pack_ref[:feat, : 2 * feat]
-    n2[...] = node_pack_ref[:feat, 2 * feat : 3 * feat]
+    e1[...] = pack_ref[:feat, : 3 * feat]
+    e2[...] = pack_ref[:feat, 3 * feat : 4 * feat]
+    n1[...] = pack_ref[:feat, 4 * feat : 6 * feat]
+    n2[...] = pack_ref[:feat, 6 * feat : 7 * feat]
     for k, ref in enumerate((b1, b2, g1, s1)):
-        ref[...] = edge_pack_ref[feat + k : feat + k + 1, :feat]
+        ref[...] = pack_ref[feat + k : feat + k + 1, :feat]
     for k, ref in enumerate((c1, c2, g2, s2)):
-        ref[...] = node_pack_ref[feat + k : feat + k + 1, :feat]
+        ref[...] = pack_ref[feat + k : feat + k + 1, 4 * feat : 5 * feat]
 
 
 def owner(masks, step, meta_ref):
     stride = masks[1] - masks[0] if len(masks) > 1 else 0
     return meta_ref[0] ^ (masks[0] + stride * step)
+
+
+def flip(value):
+    size = value.shape[1]
+    rows = lax.broadcasted_iota(jnp.int32, (size, size), 0)
+    cols = lax.broadcasted_iota(jnp.int32, (size, size), 1)
+    eye = jnp.where(rows == cols, 1.0, 0.0).astype(bf16)
+    return dot_nt(eye, value).astype(value.dtype)
+
+
+def prepare_kernel(in_ref, out_ref, node_in_ref, node_out_ref, *rest):
+    row_refs = rest[:8]
+    vec_ref, se_ref, re_ref, out_t_ref, back_ref, edge_back_ref, node_back_ref, node_out_t_ref, sr_ref = rest[8:]
+    feat = out_ref.shape[0]
+    rows = lax.broadcasted_iota(jnp.int32, (feat, feat), 0)
+    cols = lax.broadcasted_iota(jnp.int32, (feat, feat), 1)
+    for k in range(8):
+        spot = jnp.where(rows == cols, jnp.broadcast_to(row_refs[k][...], (feat, feat)), 0.0)
+        column = jnp.sum(spot, axis=1, keepdims=True)
+        vec_ref[k] = jnp.broadcast_to(column * 0.5 if k == 0 else column, (feat, LANES))
+    half = jnp.asarray(0.5, bf16)
+    sent = in_ref[:, :feat]
+    received = in_ref[:, feat : 2 * feat]
+    edge = in_ref[:, 2 * feat :]
+    se_ref[...] = jnp.concatenate([sent, edge], axis=1) * half
+    re_ref[...] = received * half
+    out_t_ref[...] = flip(out_ref[...])
+    back_ref[...] = out_ref[...] * half
+    edge_back_ref[...] = flip(edge)
+    node_back_ref[:feat] = flip(node_in_ref[:, :feat])
+    node_back_ref[feat:] = flip(node_in_ref[:, feat:])
+    node_out_t_ref[...] = flip(node_out_ref[...])
+    sr_ref[...] = jnp.concatenate([flip(sent), flip(received)], axis=1).astype(f32)
 
 
 def struct(shape, dtype):
@@ -366,31 +428,54 @@
     near = [m for m in range(0, peers, 2)]
     routed = [m for m in (4, 6, 2) if m < peers] + [m for m in range(8, peers, 2)]
 
-    def gather_all(value):
-        found = {0: value, 1: swap(value, 1)}
+    def tie(value, *others):
+        return lax.optimization_barrier((value,) + others)[0]
+
+    def gather_first(value):
+        return {m: swap(value, m) for m in [0, 1] + routed}
+
+    def gather_rest(found, gate):
         for m in routed:
-            found[m] = swap(value, m)
-        for m in routed:
-            found[m | 1] = swap(found[m], 1)
+            found[m | 1] = swap(tie(found[m], gate), 1)
         return found
 
-    def sum_out(parts):
-        got = {m: swap(parts[m | 1], 1) for m in routed + [0]}
+    def swap_near(parts):
+        return {m: swap(parts[m | 1], 1) for m in routed + [0]}
+
+    def sum_out(parts, got):
         sums = [parts[0], got[0]]
         for m in routed:
             both = (parts[m].astype(f32) + got[m].astype(f32)).astype(bf16)
-            sums.append(swap(both, m))
-        return sums
-
-    def add_up(value):
-        for axis, size in (("grp", groups), ("peer", peers)):
+            sums.append(both)
+        return sums[:2] + [swap(both, m) for both, m in zip(sums[2:], routed)], sums[-1]
+
+    def add_groups(value):
+        if groups > 4:
             mask = 1
-            while mask < size:
-                value = value + lax.ppermute(value, axis, [(i, i ^ mask) for i in range(size)])
+            while mask < groups:
+                value = value + lax.ppermute(value, "grp", [(i, i ^ mask) for i in range(groups)])
                 mask *= 2
-        return value
-
-    teams = [tuple(range(0, peers, 2)), tuple(range(1, peers, 2))]
+            return value
+        others = [lax.ppermute(value, "grp", [(i, i ^ mask) for i in range(groups)]) for mask in range(1, groups)]
+        return sum(others, value)
+
+    def add_far(value):
+        if peers > 8:
+            mask = 2
+            while mask < peers:
+                value = value + swap(value, mask)
+                mask *= 2
+            return value
+        return sum([swap(value, m) for m in routed], value)
+
+    halves = [tuple(range(0, peers, 2)), tuple(range(1, peers, 2))]
+    send_teams = halves
+    quarter = (peers + 3) // 4
+    teams = [halves[0][:quarter], halves[1], halves[0][quarter:]]
+    teams = [masks for masks in teams if masks]
+    back_teams = [(0, 1), (2, 3)][: (peers + 3) // 4]
+    for m in range(4, peers, 4):
+        back_teams += [(m, m + 2), (m + 1, m + 3)]
 
     node_t = nodes.T
     edge_t = edges.T
@@ -400,94 +485,101 @@
     send = send_nodes.reshape(rows, LANES)
     me = lax.axis_index("peer").astype(jnp.int32)[None]
 
-    shards = gather_all(node_t)
-
-    live = jnp.arange(LANES, dtype=jnp.int32)[None, :] < block_count[:, None]
-    code = slot_ids.reshape(block_total, LANES) + jnp.where(live, 0, LANES) + 2 * LANES * block_tile[:, None]
-    code = lax.all_to_all(code, "peer", 0, 0, tiled=True)
-    meta = jnp.concatenate([me, code[:, 0] // (2 * LANES)])
-    code = (code & (2 * LANES - 1)).reshape(peers, blocks, LANES)
-
-    vec = jnp.broadcast_to(
-        jnp.stack([0.5 * edge_in_bias, edge_out_bias, edge_gain, edge_shift, node_in_bias, node_out_bias, node_gain, node_shift])[:, :, None],
-        (8, feat, LANES),
+    shards = gather_first(node_t)
+
+    square = struct((feat, feat), bf16)
+    vec, se_weight, re_weight, out_t, back_weight, edge_back, node_back, node_out_t, sr_weight = pl.pallas_call(
+        prepare_kernel,
+        out_shape=[
+            struct((8, feat, LANES), f32), struct((feat, 2 * feat), bf16), square, square, square, square,
+            struct((2 * feat, feat), bf16), square, struct((feat, 2 * feat), f32),
+        ],
+        name="prepare",
+    )(
+        in_t, edge_out_weight, node_in_weight.T, node_out_weight,
+        *[v[None] for v in (edge_in_bias, edge_out_bias, edge_gain, edge_shift, node_in_bias, node_out_bias, node_gain, node_shift)],
     )
-    half = jnp.asarray(0.5, bf16)
-    se_weight = jnp.concatenate([in_t[:, :feat], in_t[:, 2 * feat :]], axis=1) * half
-    re_weight = in_t[:, feat : 2 * feat] * half
-    back_weight = edge_out_weight * half
-
-    wide = per_peer
+
+    wide = min(4096, per_peer)
+    chunks = per_peer // wide
     sub = wide // LANES
+    piece = min(1024, wide)
 
     def slab_of(masks):
-        return pl.BlockSpec((feat, wide), lambda i, ref: (0, owner(masks, i, ref)))
+        return pl.BlockSpec((feat, wide), lambda i, j, ref: (0, owner(masks, i, ref) * chunks + j))
 
     def rows_of(masks):
-        return pl.BlockSpec((sub, LANES), lambda i, ref: (owner(masks, i, ref), 0))
+        return pl.BlockSpec((sub, LANES), lambda i, j, ref: (owner(masks, i, ref) * chunks + j, 0))
 
     def code_of(masks):
-        return pl.BlockSpec((1, sub, LANES), lambda i, ref: (owner(masks, i, ref), 0, 0))
-
-    own_slab = pl.BlockSpec((feat, wide), lambda i, ref: (0, i))
-    own_rows = pl.BlockSpec((sub, LANES), lambda i, ref: (i, 0))
-    part_spec = pl.BlockSpec((1, feat, node_total), lambda i, ref: (i, 0, 0))
+        return pl.BlockSpec((1, sub, LANES), lambda i, j, ref: (owner(masks, i, ref), j, 0))
+
+    def kept_slab(place):
+        return pl.BlockSpec((feat, wide), lambda i, j, ref: (0, (place + i) * chunks + j))
+
+    own_slab = kept_slab(0)
+    own_rows = pl.BlockSpec((sub, LANES), lambda i, j, ref: (i * chunks + j, 0))
     shard_spec = whole((feat, node_total))
     keep_spec = pl.BlockSpec(memory_space=pl.ANY)
 
-    picks, bases = [], []
+    token = struct((8, LANES), f32)
+    token_spec = whole((8, LANES))
+    slab_shape = struct((feat, edge_total), bf16)
+    shard_shape = struct((feat, node_total), bf16)
+    chain = []
+    for masks in send_teams:
+        count = len(masks)
+        extra = len(chain)
+        pick, base, gate = pl.pallas_call(
+            functools.partial(sender_kernel, min(512, wide), extra),
+            grid_spec=pltpu.PrefetchScalarGridSpec(
+                num_scalar_prefetch=1,
+                grid=(count, chunks),
+                in_specs=[shard_spec, rows_of(masks), slab_of(masks), whole((feat, 2 * feat)), whole((8, feat, LANES))] + [keep_spec] * extra,
+                out_specs=[slab_of(masks), slab_of(masks), token_spec],
+            ),
+            out_shape=[slab_shape, struct((feat, edge_total), f32), token],
+            input_output_aliases={6 + k: k for k in range(extra)},
+            compiler_params=params(),
+            name="sender",
+        )(me, node_t, send, edge_t, se_weight, vec, *chain)
+        if not chain:
+            shards = gather_rest(shards, gate)
+            send = tie(send, *[shards[m] for m in routed])
+            live = jnp.arange(LANES, dtype=jnp.int32)[None, :] < tie(block_count, gate, *[shards[m] for m in routed])[:, None]
+            code = slot_ids.reshape(block_total, LANES) + jnp.where(live, 0, LANES) + 2 * LANES * block_tile[:, None]
+            code = lax.all_to_all(code, "peer", 0, 0, tiled=True)
+            meta = jnp.concatenate([me, code[:, 0] // (2 * LANES)])
+            code = (code & (2 * LANES - 1)).reshape(peers, blocks, LANES)
+        chain = [pick, base]
+
+    parts = {}
+    chain = []
     for masks in teams:
         count = len(masks)
-        pick, base = pl.pallas_call(
-            functools.partial(sender_kernel, 512),
+        extra = len(chain)
+        *outs, = pl.pallas_call(
+            functools.partial(forward_kernel, masks, blocks, piece, extra),
             grid_spec=pltpu.PrefetchScalarGridSpec(
                 num_scalar_prefetch=1,
-                grid=(count,),
-                in_specs=[shard_spec, rows_of(masks), slab_of(masks), whole((feat, 2 * feat)), whole((8, feat, LANES))],
-                out_specs=[own_slab, own_slab],
-            ),
-            out_shape=[struct((feat, count * wide), bf16), struct((feat, count * wide), f32)],
-            compiler_params=params(),
-            name="sender",
-        )(me, node_t, send, edge_t, se_weight, vec)
-        picks.append(pick)
-        bases.append(base)
-
-    saved = []
-    parts = {}
-    result = None
-    for t, masks in enumerate(teams):
-        count = len(masks)
-        extra = 0 if result is None else 1
-        result, act, slope, normed, inv, part = pl.pallas_call(
-            functools.partial(forward_kernel, masks, blocks, 1024, extra),
-            grid_spec=pltpu.PrefetchScalarGridSpec(
-                num_scalar_prefetch=1,
-                grid=(count,),
-                in_specs=[code_of(masks), own_slab, slab_of(masks), whole((feat, feat)), whole((feat, feat)), whole((8, feat, LANES))]
+                grid=(count, chunks),
+                in_specs=[code_of(masks), slab_of(masks), slab_of(masks), whole((feat, feat)), whole((feat, feat)), whole((8, feat, LANES))]
                 + [shard_spec] * count
                 + [keep_spec] * extra,
-                out_specs=[slab_of(masks), own_slab, own_slab, own_slab, own_rows, part_spec],
+                out_specs=[slab_of(masks)] * 4 + [rows_of(masks), token_spec] + [shard_spec] * count,
                 scratch_shapes=[pltpu.VMEM((feat, node_total), f32), pltpu.VMEM((feat, node_total), f32)],
             ),
-            out_shape=[
-                struct((feat, edge_total), bf16),
-                struct((feat, count * wide), bf16),
-                struct((feat, count * wide), bf16),
-                struct((feat, count * wide), bf16),
-                struct((count * sub, LANES), f32),
-                struct((count, feat, node_total), bf16),
-            ],
-            input_output_aliases={7 + count: 0} if extra else {},
+            out_shape=[slab_shape] * 4 + [struct((rows, LANES), f32), token] + [shard_shape] * count,
+            input_output_aliases={7 + count + k: k for k in range(extra)},
             compiler_params=params(),
             name="forward",
-        )(meta, code, bases[t], edge_t, re_weight, edge_out_weight.T, vec, *[shards[m] for m in masks], *([result] * extra))
-        saved.append((normed, act, slope, inv))
-        for k, m in enumerate(masks):
-            parts[m] = part[k]
+        )(meta, code, base, edge_t, re_weight, out_t, vec, *[shards[m] for m in masks], *chain)
+        chain = outs[:5]
+        parts.update(zip(masks, outs[6:]))
+    result, act, slope, normed, inv = chain
     edge_result = result
 
-    sums = sum_out(parts)
+    sums, _ = sum_out(parts, swap_near(parts))
     node_result, node_base, back, node_pack = pl.pallas_call(
         functools.partial(node_kernel, len(sums)),
         out_shape=[
@@ -498,28 +590,28 @@
         ],
         compiler_params=params(),
         name="node",
-    )(node_t, node_cot_t, node_in_weight.T, node_in_weight, node_out_weight.T, node_out_weight, vec, *sums)
-
-    backs = gather_all(back)
-    node_pack = add_up(node_pack)
+    )(node_t, node_cot_t, node_in_weight.T, node_back, node_out_t, node_out_weight, vec, *sums)
+
+    near_pack = swap(node_pack, 1)
+    backs = gather_first(back)
 
     parts = {}
-    firsts = []
-    edge_grad = edge_pack = None
-    for t, masks in enumerate(teams):
+    chain = []
+    for masks in back_teams:
         count = len(masks)
-        prior = [] if edge_grad is None else [edge_grad, edge_pack]
-        extra = len(prior)
-        normed, act, slope, inv = saved[t]
-        edge_grad, first_grad, part, edge_pack = pl.pallas_call(
-            functools.partial(backward_kernel, masks, blocks, 1024, extra),
+        extra = len(chain)
+        if masks == back_teams[-1] and extra:
+            chain[2] = tie(chain[2], node_sum)
+        *outs, = pl.pallas_call(
+            functools.partial(backward_kernel, masks, blocks, piece, extra),
             grid_spec=pltpu.PrefetchScalarGridSpec(
                 num_scalar_prefetch=1,
-                grid=(count,),
-                in_specs=[code_of(masks), slab_of(masks), own_slab, own_slab, own_slab, own_rows, slab_of(masks), own_slab, whole((feat, feat)), whole((feat, feat)), whole((8, feat, LANES))]
+                grid=(count, chunks),
+                in_specs=[code_of(masks)] + [slab_of(masks)] * 4 + [rows_of(masks)] + [slab_of(masks)] * 2
+                + [whole((feat, feat)), whole((feat, feat)), whole((8, feat, LANES))]
                 + [shard_spec] * (2 * count)
-                + ([keep_spec, whole((feat + 8, 4 * feat))] if extra else []),
-                out_specs=[slab_of(masks), own_slab, part_spec, whole((feat + 8, 4 * feat))],
+                + ([keep_spec] * 2 + [whole((feat + 8, 4 * feat))] if extra else []),
+                out_specs=[slab_of(masks), slab_of(masks), whole((feat + 8, 4 * feat)), token_spec] + [shard_spec] * count,
                 scratch_shapes=[
                     pltpu.VMEM((feat, node_total), f32),
                     pltpu.VMEM((feat, node_total), f32),
@@ -531,44 +623,57 @@
             ),
             out_shape=[
                 struct((feat, edge_total), f32),
-                struct((feat, count * wide), bf16),
-                struct((count, feat, node_total), bf16),
+                slab_shape,
                 struct((feat + 8, 4 * feat), f32),
-            ],
-            input_output_aliases={12 + 2 * count: 0} if extra else {},
+                token,
+            ]
+            + [shard_shape] * count,
+            input_output_aliases={12 + 2 * count + k: k for k in range(2 if extra else 0)},
             compiler_params=params(),
             name="backward",
         )(
-            meta, code, edge_cot_t, normed, act, slope, inv, edge_t, picks[t], back_weight, edge_in_weight[2 * feat :], vec,
-            *[backs[m] for m in masks], *[shards[m] for m in masks], *prior,
+            meta, code, edge_cot_t, normed, act, slope, inv, edge_t, pick, back_weight, edge_back, vec,
+            *[backs[m] for m in masks], *[shards[m] for m in masks], *chain,
         )
-        firsts.append(first_grad)
-        for k, m in enumerate(masks):
-            parts[m] = part[k]
-
-    sums = sum_out(parts)
-    edge_pack = add_up(edge_pack)
-
-    sent = []
-    for t, masks in enumerate(teams):
-        sent.append(
-            pl.pallas_call(
-                sender_sum_kernel,
-                grid_spec=pltpu.PrefetchScalarGridSpec(
-                    num_scalar_prefetch=1,
-                    grid=(len(masks),),
-                    in_specs=[own_slab, rows_of(masks)],
-                    out_specs=shard_spec,
-                    scratch_shapes=[pltpu.VMEM((node_total // WIDE * feat, WIDE), f32)],
-                ),
-                out_shape=struct((feat, node_total), f32),
-                compiler_params=params(),
-                name="sender_sum",
-            )(me, firsts[t], send)
-        )
-
+        chain, gate = outs[:3], outs[3]
+        parts.update(zip(masks, outs[4:]))
+        if not extra:
+            backs = gather_rest(backs, gate)
+            node_sum = node_pack + near_pack
+        elif masks == back_teams[1]:
+            node_sum = add_far(tie(node_sum, gate))
+    edge_grad, first_grad, edge_pack = chain
+
+    near_pack = swap(edge_pack, 1)
+    got = swap_near(parts)
+
+    sent, gates = [], []
+    sum_wide = min(2048, per_peer)
+    steps = edge_total // sum_wide // 2
+    for start in (0, steps):
+        if gates:
+            got = {m: tie(value, gates[0]) for m, value in got.items()}
+            sums, mark = sum_out(parts, got)
+            edge_pack = add_far(tie(edge_pack + tie(near_pack, gates[0]), mark))
+            first_grad = tie(first_grad, mark)
+        total, gate = pl.pallas_call(
+            sender_sum_kernel,
+            grid=(steps,),
+            in_specs=[
+                pl.BlockSpec((feat, sum_wide), lambda i, start=start: (0, start + i)),
+                pl.BlockSpec((sum_wide // LANES, LANES), lambda i, start=start: (start + i, 0)),
+            ],
+            out_specs=[shard_spec, token_spec],
+            out_shape=[struct((feat, node_total), f32), token],
+            scratch_shapes=[pltpu.VMEM((node_total // WIDE * feat, WIDE), f32)],
+            compiler_params=params(),
+            name="sender_sum",
+        )(first_grad, send)
+        sent.append(total)
+        gates.append(gate)
+
+    both_packs = add_groups(jnp.concatenate([tie(edge_pack, gates[1]), node_sum], axis=1))
     vec_out = struct((1, feat), f32)
-    sr_weight = jnp.concatenate([edge_in_weight[:feat], edge_in_weight[feat : 2 * feat]], axis=1).astype(f32)
     node_grad, e1, b1, e2, b2, g1, s1, n1, c1, n2, c2, g2, s2 = pl.pallas_call(
         functools.partial(finish_kernel, len(sent), len(sums)),
         out_shape=[
@@ -578,7 +683,7 @@
         ],
         compiler_params=params(),
         name="finish",
-    )(node_base, sr_weight, node_pack, edge_pack, *sent, *sums)
+    )(node_base, sr_weight, both_packs, *sent, *sums)
 
     def flat(row):
         return row.reshape(feat)

time: 248 us -> 221 us (0.89)
  waiting for transfers between devices: 68.7 us -> 36 us
  other arithmetic: 9.68 us -> 2.1 us
  local copies, waits for them, and re-layouts: 13.1 us -> 18.4 us
  starting transfers between devices: 51.3 us -> 55.6 us
  Pallas kernels: 104 us -> 107 us
    ppermute x10 -> x3, waiting for transfers between devices: 22.8 us -> 0.01 us  [add_groups(): lax.ppermute(value, 'grp', [(i, i ^ mask) for i in range(groups)])]
    unnamed x67 -> x55, local copies, waits for them, and re-layouts: 6.39 us -> 18.2 us
    ppermute x28 -> x36, starting transfers between devices: 38.2 us -> 48.3 us  [swap(): return lax.ppermute(value, 'peer', [(i, i ^ mask) for i in range(peers)])]
    ppermute x28 -> x36, waiting for transfers between devices: 45.9 us -> 36 us  [swap(): return lax.ppermute(value, 'peer', [(i, i ^ mask) for i in range(peers)])]
    pallas_call x8 -> x12, Pallas kernels: 96.4 us -> 104 us  [the longest x4 37.5 us: per_device(): pl.pallas_call(functools.partial(backward_kernel, masks, blocks, piece, e...]
    ppermute x10 -> x3, starting transfers between devices: 8.27 us -> 1.92 us  [add_groups(): lax.ppermute(value, 'grp', [(i, i ^ mask) for i in range(groups)])]
    squeeze x4 -> x0, local copies, waits for them, and re-layouts: 4.17 us -> none  [per_device(): parts[m] = part[k]]
    mul x3 -> x0, other arithmetic: 2.77 us -> none  [the longest x1 1.47 us: per_device(): re_weight = in_t[:, feat:2 * feat] * half]
  transfers between devices with their start and end apart: 39 -> 40, of which waited for: 14 -> 12; matrix products, arithmetic and copies ran while one was open for 7% -> 1% of each run, Pallas kernels for 34% -> 42%
where the time goes in v3:
time: 221 us
  Pallas kernels  107 us (48%)
  starting transfers between devices  55.6 us (25%)
  waiting for transfers between devices  36 us (16%)
  local copies, waits for them, and re-layouts  18.4 us (8%)
    ppermute x36, starting transfers between devices, swap(): return lax.ppermute(value, 'peer', [(i, i ^ mask) for i in range(peers)])  48.3 us
    pallas_call x4, Pallas kernels, per_device(): pl.pallas_call(functools.partial(backward_kernel, masks, blocks, piece, e...  37.5 us
    ppermute x36, waiting for transfers between devices, swap(): return lax.ppermute(value, 'peer', [(i, i ^ mask) for i in range(peers)])  36 us
    pallas_call x2, Pallas kernels, per_device(): pl.pallas_call(functools.partial(sender_kernel, min(512, wide), extra), g...  26.2 us
    pallas_call x3, Pallas kernels, per_device(): pl.pallas_call(functools.partial(forward_kernel, masks, blocks, piece, ex...  24.9 us
    unnamed x55, local copies, waits for them, and re-layouts  18.2 us
    pallas_call x2, Pallas kernels, per_device(): pl.pallas_call(sender_sum_kernel, grid=(steps,), in_specs=[pl.BlockSpec((...  13.8 us
    all_to_all x1, starting transfers between devices, per_device(): code = lax.all_to_all(code, 'peer', 0, 0, tiled=True)  5.42 us
  transfers between devices with their start and end apart: 40, of which 12 were waited for; matrix products, arithmetic and copies ran while one was open for 1% of the time, Pallas kernels for 42%

profile of v3, /device:TPU:0, one launch (start us, length us, event | category | flops | bytes accessed | tf_op | source)
XLA Modules:
  0.0 220.6 jit_solution(3415793481982484774)
XLA Ops:
  0.7 4.1 %collective-permute-start = (bf16[64,2048]{1,0:T(8,128)(2,1)}, bf16[64,2048]{1,0:T(8,128)(2,1)S(1)}, u32[]{:S(2)}, u32[]{:S(2)}) collective-permute-start(bf16[64,2048]{1,0:T(8,128)(2,1)} %bitcast.34), channel_id=1, source_target_pairs={{0,4},{1,5},{2,6},{3,7},{4,0},{5,1},{6,2},{7,3},{8,12},{9,13},{10,... | collective-permute-start | bytes 786440 | tf_op jit(solution)/shard_map/ppermute | solution.py:426
  12.5 13.1 %sender.2 = (bf16[64,32768]{1,0:T(8,128)(2,1)S(1)}, f32[64,32768]{1,0:T(8,128)}, f32[8,128]{1,0:T(8,128)}) custom-call(s32[1]{0:T(128)} %bitcast.12.me_ref, bf16[64,2048]{1,0:T(8,128)(2,1)S(1)} %bitcast.37, s32[256,128]{1,0:T(8,128)S(1)} %bitcast.43, bf16[64,32768]{1,0:T(8,128)(2,1)} %bitcast.50, bf16[64,128]{1,0:T(8,128)(2,1)S(1)} %copy-done.20, ...), custom_call_target="tpu_custom_call" | custom-call | tf_op jit(solution)/shard_map/sender/pallas_call | solution.py:533
  28.5 5.4 %all-to-all-start = ((s32[8,32,128]{2,1,0:T(8,128)}), s32[8,32,128]{2,1,0:T(8,128)S(1)}, u32[]{:S(2)}, u32[]{:S(2)}) async-start(s32[8,32,128]{2,1,0:T(8,128)} %add_add_fusion.1), calls=%async_computation | async-start | bytes 262144 | tf_op jit(solution)/shard_map/all_to_all | solution.py:551
  33.9 2.0 collective-permute-start.3
  38.1 2.2 copy-done.5
  40.3 13.0 %sender.3 = (bf16[64,32768]{1,0:T(8,128)(2,1)S(1)}, f32[64,32768]{1,0:T(8,128)}, f32[8,128]{1,0:T(8,128)}) custom-call(s32[1]{0:T(128)} %bitcast.12.me_ref, bf16[64,2048]{1,0:T(8,128)(2,1)S(1)} %bitcast.39, s32[256,128]{1,0:T(8,128)S(1)} %bitcast.44, bf16[64,32768]{1,0:T(8,128)(2,1)} %bitcast.51, ...), custom_call_target="tpu_custom_call", output_to_operand_aliasing={{0}: (6, {}), {1}: (7, {})} | custom-call | tf_op jit(solution)/shard_map/sender/pallas_call | solution.py:533
  55.5 6.9 %forward.3 = (bf16[64,32768]{1,0:T(8,128)(2,1)}, bf16[64,32768]{1,0:T(8,128)(2,1)S(1)}, bf16[64,32768]{1,0:T(8,128)(2,1)}, bf16[64,32768]{1,0:T(8,128)(2,1)}, f3...) custom-call(s32[257]{0:T(512)S(1)} %pad_add_fusion.meta_ref, ...), custom_call_target="tpu_custom_call" | custom-call | tf_op jit(solution)/shard_map/forward/pallas_call | solution.py:561
  62.4 2.0 copy-done
  64.5 11.1 %forward.4 = (bf16[64,32768]{1,0:T(8,128)(2,1)}, bf16[64,32768]{1,0:T(8,128)(2,1)}, bf16[64,32768]{1,0:T(8,128)(2,1)}, bf16[64,32768]{1,0:T(8,128)(2,1)}, f32[25...) custom-call(s32[257]{0:T(512)S(1)} %pad_add_fusion.meta_ref, ...), custom_call_target="tpu_custom_call", output_to_operand_aliasing={{0}: (11, {}), {1}: (12, {}), {2}: (13, {}), {3}: (14, {}),... | custom-call | tf_op jit(solution)/shard_map/forward/pallas_call | solution.py:561
  79.6 2.2 copy-done.1
  81.8 6.9 %forward.5 = (bf16[64,32768]{1,0:T(8,128)(2,1)}, bf16[64,32768]{1,0:T(8,128)(2,1)S(1)}, bf16[64,32768]{1,0:T(8,128)(2,1)}, bf16[64,32768]{1,0:T(8,128)(2,1)}, f3...) custom-call(s32[257]{0:T(512)S(1)} %pad_add_fusion.meta_ref, ...), custom_call_target="tpu_custom_call", output_to_operand_aliasing={{0}: (9, {}), {1}: (10, {}), {2}: (11, {}), {3}: (12, {}), ... | custom-call | tf_op jit(solution)/shard_map/forward/pallas_call | solution.py:561
  88.7 2.0 copy-done.2
  92.9 2.5 %collective-permute-start.11 = (bf16[64,2048]{1,0:T(8,128)(2,1)S(1)}, bf16[64,2048]{1,0:T(8,128)(2,1)S(1)}, u32[]{:S(2)}, u32[]{:S(2)}) collective-permute-start(bf16[64,2048]{1,0:T(8,128)(2,1)S(1)} %add_convert_fusion.4), channel_id=1, source_target_pairs={{0,6},{1,7},{2,4},{3,5},{4,2},{5,3},{6,0},{7,1},{8,14},{9,15},{10,... | collective-permute-start | bytes 786440 | tf_op jit(solution)/shard_map/ppermute | solution.py:426
  96.0 2.9 %collective-permute-start.9 = (bf16[64,2048]{1,0:T(8,128)(2,1)S(1)}, bf16[64,2048]{1,0:T(8,128)(2,1)S(1)}, u32[]{:S(2)}, u32[]{:S(2)}) collective-permute-start(bf16[64,2048]{1,0:T(8,128)(2,1)S(1)} %add_convert_fusion.5), channel_id=1, source_target_pairs={{0,4},{1,5},{2,6},{3,7},{4,0},{5,1},{6,2},{7,3},{8,12},{9,13},{10,... | collective-permute-start | bytes 786440 | tf_op jit(solution)/shard_map/ppermute | solution.py:426
  101.1 6.0 %collective-permute-done.11.rest_3_ = bf16[64,2048]{1,0:T(8,128)(2,1)S(1)} collective-permute-done((bf16[64,2048]{1,0:T(8,128)(2,1)S(1)}, bf16[64,2048]{1,0:T(8,128)(2,1)S(1)}, u32[]{:S(2)}, u32[]{:S(2)}) %collective-permute-start.11) | collective-permute-done | bytes 262176 | tf_op jit(solution)/shard_map/ppermute | solution.py:426
  107.0 8.5 %collective-permute-done.9.rest_2_ = bf16[64,2048]{1,0:T(8,128)(2,1)S(1)} collective-permute-done((bf16[64,2048]{1,0:T(8,128)(2,1)S(1)}, bf16[64,2048]{1,0:T(8,128)(2,1)S(1)}, u32[]{:S(2)}, u32[]{:S(2)}) %collective-permute-start.9) | collective-permute-done | bytes 262176 | tf_op jit(solution)/shard_map/ppermute | solution.py:426
  118.7 2.6 %collective-permute-start.17 = (bf16[64,2048]{1,0:T(8,128)(2,1)S(1)}, bf16[64,2048]{1,0:T(8,128)(2,1)S(1)}, u32[]{:S(2)}, u32[]{:S(2)}) collective-permute-start(bf16[64,2048]{1,0:T(8,128)(2,1)S(1)} %get-tuple-element.154.rest_0_), channel_id=1, source_target_pairs={{0,6},{1,7},{2,4},{3,5},{4,2},{5,3},{6,0},{7,1},{8,14},{9,15},{10,... | collective-permute-start | bytes 786440 | tf_op jit(solution)/shard_map/ppermute | solution.py:426
  123.7 9.5 %backward.4 = (f32[64,32768]{1,0:T(8,128)}, bf16[64,32768]{1,0:T(8,128)(2,1)}, f32[72,256]{1,0:T(8,128)S(1)}, f32[8,128]{1,0:T(8,128)}, bf16[64,2048]{1,0:T(8,128)(2,1)S(1)}, /*index=5*/bf16[64,2048]{1,0:T(8,128)(2,1)S(1)}) custom-call(s32[257]{0:T(512)S(1)} %pad_add_fusion.meta_ref, s32[8,32,128]{2,1,0:T(8,128)S(1)} %broadcast_and_fusion.code_ref, ...), custom_call_target="tpu_custom_call" | custom-call | tf_op jit(solution)/shard_map/backward/pallas_call | solution.py:605
  135.3 5.1 %collective-permute-done.21 = f32[72,256]{1,0:T(8,128)S(1)} collective-permute-done((f32[72,256]{1,0:T(8,128)S(1)}, f32[72,256]{1,0:T(8,128)S(1)}, u32[]{:S(2)}, u32[]{:S(2)}) %collective-permute-start.21) | collective-permute-done | bytes 73760 | tf_op jit(solution)/shard_map/ppermute | solution.py:426
  141.2 2.1 collective-permute-start.23
  144.0 2.5 %collective-permute-done.14.rest_0_ = bf16[64,2048]{1,0:T(8,128)(2,1)S(1)} collective-permute-done((bf16[64,2048]{1,0:T(8,128)(2,1)S(1)}, bf16[64,2048]{1,0:T(8,128)(2,1)S(1)}, u32[]{:S(2)}, u32[]{:S(2)}) %collective-permute-start.14) | collective-permute-done | bytes 262176 | tf_op jit(solution)/shard_map/ppermute | solution.py:426
  148.5 9.3 %backward.5 = (f32[64,32768]{1,0:T(8,128)}, bf16[64,32768]{1,0:T(8,128)(2,1)}, f32[72,256]{1,0:T(8,128)S(1)}, f32[8,128]{1,0:T(8,128)}, bf16[64,2048]{1,0:T(8,128)(2,1)S(1)}, /*index=5*/bf16[64,2048]{1,0:T(8,128)(2,1)S(1)}) custom-call(s32[257]{0:T(512)S(1)} %pad_add_fusion.meta_ref, ...), custom_call_target="tpu_custom_call", output_to_operand_aliasing={{0}: (16, {}), {1}: (17, {})} | custom-call | tf_op jit(solution)/shard_map/backward/pallas_call | solution.py:605
  158.5 9.3 %backward.6 = (f32[64,32768]{1,0:T(8,128)}, bf16[64,32768]{1,0:T(8,128)(2,1)}, f32[72,256]{1,0:T(8,128)S(1)}, f32[8,128]{1,0:T(8,128)}, bf16[64,2048]{1,0:T(8,128)(2,1)S(1)}, /*index=5*/bf16[64,2048]{1,0:T(8,128)(2,1)S(1)}) custom-call(s32[257]{0:T(512)S(1)} %pad_add_fusion.meta_ref, ...), custom_call_target="tpu_custom_call", output_to_operand_aliasing={{0}: (16, {}), {1}: (17, {})} | custom-call | tf_op jit(solution)/shard_map/backward/pallas_call | solution.py:605
  167.8 9.3 %backward.7 = (f32[64,32768]{1,0:T(8,128)}, bf16[64,32768]{1,0:T(8,128)(2,1)}, f32[72,256]{1,0:T(8,128)S(1)}, f32[8,128]{1,0:T(8,128)}, bf16[64,2048]{1,0:T(8,128)(2,1)S(1)}, /*index=5*/bf16[64,2048]{1,0:T(8,128)(2,1)S(1)}) custom-call(s32[257]{0:T(512)S(1)} %pad_add_fusion.meta_ref, ...), custom_call_target="tpu_custom_call", output_to_operand_aliasing={{0}: (16, {}), {1}: (17, {})} | custom-call | tf_op jit(solution)/shard_map/backward/pallas_call | solution.py:605
  179.2 2.2 copy-done.3
  181.4 6.9 %sender_sum.2 = (f32[64,2048]{1,0:T(8,128)S(1)}, f32[8,128]{1,0:T(8,128)}) custom-call(bf16[64,32768]{1,0:T(8,128)(2,1)S(1)} %copy-done.3, s32[256,128]{1,0:T(8,128)S(1)} %bitcast.45), custom_call_target="tpu_custom_call" | custom-call | tf_op jit(solution)/shard_map/sender_sum/pallas_call | solution.py:659
  190.5 3.1 %collective-permute-start.28 = (f32[72,256]{1,0:T(8,128)S(1)}, f32[72,256]{1,0:T(8,128)S(1)}, u32[]{:S(2)}, u32[]{:S(2)}) collective-permute-start(f32[72,256]{1,0:T(8,128)S(1)} %add.78), channel_id=1, source_target_pairs={{0,6},{1,7},{2,4},{3,5},{4,2},{5,3},{6,0},{7,1},{8,14},{9,15},{10,... | collective-permute-start | bytes 221192 | tf_op jit(solution)/shard_map/ppermute | solution.py:426
  195.0 2.5 %collective-permute-done.34 = bf16[64,2048]{1,0:T(8,128)(2,1)S(1)} collective-permute-done((bf16[64,2048]{1,0:T(8,128)(2,1)S(1)}, bf16[64,2048]{1,0:T(8,128)(2,1)S(1)}, u32[]{:S(2)}, u32[]{:S(2)}) %collective-permute-start.34) | collective-permute-done | bytes 262176 | tf_op jit(solution)/shard_map/ppermute | solution.py:426
  197.5 3.0 %collective-permute-start.37 = (bf16[64,2048]{1,0:T(8,128)(2,1)S(1)}, bf16[64,2048]{1,0:T(8,128)(2,1)S(1)}, u32[]{:S(2)}, u32[]{:S(2)}) collective-permute-start(bf16[64,2048]{1,0:T(8,128)(2,1)S(1)} %add_convert_fusion), channel_id=1, source_target_pairs={{0,6},{1,7},{2,4},{3,5},{4,2},{5,3},{6,0},{7,1},{8,14},{9,15},{10,... | collective-permute-start | bytes 786440 | tf_op jit(solution)/shard_map/ppermute | solution.py:426
  202.9 2.1 collective-permute-start.35
  206.2 6.9 %sender_sum.3 = (f32[64,2048]{1,0:T(8,128)S(1)}, f32[8,128]{1,0:T(8,128)}) custom-call(bf16[64,32768]{1,0:T(8,128)(2,1)S(1)} %copy-done.3, s32[256,128]{1,0:T(8,128)S(1)} %bitcast.46), custom_call_target="tpu_custom_call" | custom-call | tf_op jit(solution)/shard_map/sender_sum/pallas_call | solution.py:659
  213.2 5.7 %collective-permute-done.35.rest_4_ = bf16[64,2048]{1,0:T(8,128)(2,1)S(1)} collective-permute-done((bf16[64,2048]{1,0:T(8,128)(2,1)S(1)}, bf16[64,2048]{1,0:T(8,128)(2,1)S(1)}, u32[]{:S(2)}, u32[]{:S(2)}) %collective-permute-start.35) | collective-permute-done | bytes 262176 | tf_op jit(solution)/shard_map/ppermute | solution.py:426
  (136 shorter events, 46.4 us)
Async XLA Ops:
  0.7 27.0 %collective-permute-start = (bf16[64,2048]{1,0:T(8,128)(2,1)}, bf16[64,2048]{1,0:T(8,128)(2,1)S(1)}, u32[]{:S(2)}, u32[]{:S(2)}) collective-permute-start(bf16[64,2048]{1,0:T(8,128)(2,1)} %bitcast.34), channel_id=1, source_target_pairs={{0,4},{1,5},{2,6},{3,7},{4,0},{5,1},{6,2},{7,3},{8,12},{9,13},{10,... | collective-permute-start | bytes 786440 | tf_op jit(solution)/shard_map/ppermute | solution.py:426
  4.8 22.8 %collective-permute-start.1 = (bf16[64,2048]{1,0:T(8,128)(2,1)}, bf16[64,2048]{1,0:T(8,128)(2,1)S(1)}, u32[]{:S(2)}, u32[]{:S(2)}) collective-permute-start(bf16[64,2048]{1,0:T(8,128)(2,1)} %bitcast.35), channel_id=1, source_target_pairs={{0,6},{1,7},{2,4},{3,5},{4,2},{5,3},{6,0},{7,1},{8,14},{9,15},{10,... | collective-permute-start | bytes 786440 | tf_op jit(solution)/shard_map/ppermute | solution.py:426
  6.1 21.5 %collective-permute-start.2 = (bf16[64,2048]{1,0:T(8,128)(2,1)}, bf16[64,2048]{1,0:T(8,128)(2,1)S(1)}, u32[]{:S(2)}, u32[]{:S(2)}) collective-permute-start(bf16[64,2048]{1,0:T(8,128)(2,1)} %bitcast.36), channel_id=1, source_target_pairs={{0,2},{1,3},{2,0},{3,1},{4,6},{5,7},{6,4},{7,5},{8,10},{9,11},{10,... | collective-permute-start | bytes 786440 | tf_op jit(solution)/shard_map/ppermute | solution.py:426
  28.5 26.8 %all-to-all-start = ((s32[8,32,128]{2,1,0:T(8,128)}), s32[8,32,128]{2,1,0:T(8,128)S(1)}, u32[]{:S(2)}, u32[]{:S(2)}) async-start(s32[8,32,128]{2,1,0:T(8,128)} %add_add_fusion.1), calls=%async_computation | async-start | bytes 262144 | tf_op jit(solution)/shard_map/all_to_all | solution.py:551
  33.9 30.5 %collective-permute-start.3 = (bf16[64,2048]{1,0:T(8,128)(2,1)S(1)}, bf16[64,2048]{1,0:T(8,128)(2,1)S(1)}, u32[]{:S(2)}, u32[]{:S(2)}) collective-permute-start(bf16[64,2048]{1,0:T(8,128)(2,1)S(1)} %bitcast.38), channel_id=1, source_target_pairs={{0,1},{1,0},{2,3},{3,2},{4,5},{5,4},{6,7},{7,6},{8,9},{9,8},{10,11... | collective-permute-start | bytes 786440 | tf_op jit(solution)/shard_map/ppermute | solution.py:426
  35.9 28.5 %collective-permute-start.4 = (bf16[64,2048]{1,0:T(8,128)(2,1)S(1)}, bf16[64,2048]{1,0:T(8,128)(2,1)S(1)}, u32[]{:S(2)}, u32[]{:S(2)}) collective-permute-start(bf16[64,2048]{1,0:T(8,128)(2,1)S(1)} %collective-permute-done.2.rest_1_.rest_2_), channel_id=1, source_target_pairs={{0,1},{1,0},{2,3},{3,2},{4,5},{5,4},{6,7},{7,6},{8,9},{9,8},{10,11... | collective-permute-start | bytes 786440 | tf_op jit(solution)/shard_map/ppermute | solution.py:426
  36.0 28.4 %collective-permute-start.5 = (bf16[64,2048]{1,0:T(8,128)(2,1)S(1)}, bf16[64,2048]{1,0:T(8,128)(2,1)S(1)}, u32[]{:S(2)}, u32[]{:S(2)}) collective-permute-start(bf16[64,2048]{1,0:T(8,128)(2,1)S(1)} %collective-permute-done.rest_0_.rest_2_), channel_id=1, source_target_pairs={{0,1},{1,0},{2,3},{3,2},{4,5},{5,4},{6,7},{7,6},{8,9},{9,8},{10,11... | collective-permute-start | bytes 786440 | tf_op jit(solution)/shard_map/ppermute | solution.py:426
  38.0 26.5 %collective-permute-start.6 = (bf16[64,2048]{1,0:T(8,128)(2,1)S(1)}, bf16[64,2048]{1,0:T(8,128)(2,1)S(1)}, u32[]{:S(2)}, u32[]{:S(2)}) collective-permute-start(bf16[64,2048]{1,0:T(8,128)(2,1)S(1)} %collective-permute-done.1.rest_1_.rest_3_), channel_id=1, source_target_pairs={{0,1},{1,0},{2,3},{3,2},{4,5},{5,4},{6,7},{7,6},{8,9},{9,8},{10,11... | collective-permute-start | bytes 786440 | tf_op jit(solution)/shard_map/ppermute | solution.py:426
  75.5 15.2 %collective-permute-start.12 = (bf16[64,2048]{1,0:T(8,128)(2,1)S(1)}, bf16[64,2048]{1,0:T(8,128)(2,1)S(1)}, u32[]{:S(2)}, u32[]{:S(2)}) collective-permute-start(bf16[64,2048]{1,0:T(8,128)(2,1)S(1)} %get-tuple-element.142), channel_id=1, source_target_pairs={{0,1},{1,0},{2,3},{3,2},{4,5},{5,4},{6,7},{7,6},{8,9},{9,8},{10,11... | collective-permute-start | bytes 786440 | tf_op jit(solution)/shard_map/ppermute | solution.py:426
  77.4 15.4 %collective-permute-start.10 = (bf16[64,2048]{1,0:T(8,128)(2,1)S(1)}, bf16[64,2048]{1,0:T(8,128)(2,1)S(1)}, u32[]{:S(2)}, u32[]{:S(2)}) collective-permute-start(bf16[64,2048]{1,0:T(8,128)(2,1)S(1)} %get-tuple-element.140), channel_id=1, source_target_pairs={{0,1},{1,0},{2,3},{3,2},{4,5},{5,4},{6,7},{7,6},{8,9},{9,8},{10,11... | collective-permute-start | bytes 786440 | tf_op jit(solution)/shard_map/ppermute | solution.py:426
  77.6 18.4 %collective-permute-start.8 = (bf16[64,2048]{1,0:T(8,128)(2,1)S(1)}, bf16[64,2048]{1,0:T(8,128)(2,1)S(1)}, u32[]{:S(2)}, u32[]{:S(2)}) collective-permute-start(bf16[64,2048]{1,0:T(8,128)(2,1)S(1)} %get-tuple-element.138), channel_id=1, source_target_pairs={{0,1},{1,0},{2,3},{3,2},{4,5},{5,4},{6,7},{7,6},{8,9},{9,8},{10,11... | collective-permute-start | bytes 786440 | tf_op jit(solution)/shard_map/ppermute | solution.py:426
  79.5 19.8 %collective-permute-start.7 = (bf16[64,2048]{1,0:T(8,128)(2,1)S(1)}, bf16[64,2048]{1,0:T(8,128)(2,1)S(1)}, u32[]{:S(2)}, u32[]{:S(2)}) collective-permute-start(bf16[64,2048]{1,0:T(8,128)(2,1)S(1)} %get-tuple-element.131), channel_id=1, source_target_pairs={{0,1},{1,0},{2,3},{3,2},{4,5},{5,4},{6,7},{7,6},{8,9},{9,8},{10,11... | collective-permute-start | bytes 786440 | tf_op jit(solution)/shard_map/ppermute | solution.py:426
  92.9 14.2 %collective-permute-start.11 = (bf16[64,2048]{1,0:T(8,128)(2,1)S(1)}, bf16[64,2048]{1,0:T(8,128)(2,1)S(1)}, u32[]{:S(2)}, u32[]{:S(2)}) collective-permute-start(bf16[64,2048]{1,0:T(8,128)(2,1)S(1)} %add_convert_fusion.4), channel_id=1, source_target_pairs={{0,6},{1,7},{2,4},{3,5},{4,2},{5,3},{6,0},{7,1},{8,14},{9,15},{10,... | collective-permute-start | bytes 786440 | tf_op jit(solution)/shard_map/ppermute | solution.py:426
  96.0 19.5 %collective-permute-start.9 = (bf16[64,2048]{1,0:T(8,128)(2,1)S(1)}, bf16[64,2048]{1,0:T(8,128)(2,1)S(1)}, u32[]{:S(2)}, u32[]{:S(2)}) collective-permute-start(bf16[64,2048]{1,0:T(8,128)(2,1)S(1)} %add_convert_fusion.5), channel_id=1, source_target_pairs={{0,4},{1,5},{2,6},{3,7},{4,0},{5,1},{6,2},{7,3},{8,12},{9,13},{10,... | collective-permute-start | bytes 786440 | tf_op jit(solution)/shard_map/ppermute | solution.py:426
  118.7 14.5 %collective-permute-start.19 = (bf16[64,2048]{1,0:T(8,128)(2,1)S(1)}, bf16[64,2048]{1,0:T(8,128)(2,1)S(1)}, u32[]{:S(2)}, u32[]{:S(2)}) collective-permute-start(bf16[64,2048]{1,0:T(8,128)(2,1)S(1)} %get-tuple-element.154.rest_0_), channel_id=1, source_target_pairs={{0,2},{1,3},{2,0},{3,1},{4,6},{5,7},{6,4},{7,5},{8,10},{9,11},{10,... | collective-permute-start | bytes 786440 | tf_op jit(solution)/shard_map/ppermute | solution.py:426
  118.7 24.5 %collective-permute-start.17 = (bf16[64,2048]{1,0:T(8,128)(2,1)S(1)}, bf16[64,2048]{1,0:T(8,128)(2,1)S(1)}, u32[]{:S(2)}, u32[]{:S(2)}) collective-permute-start(bf16[64,2048]{1,0:T(8,128)(2,1)S(1)} %get-tuple-element.154.rest_0_), channel_id=1, source_target_pairs={{0,6},{1,7},{2,4},{3,5},{4,2},{5,3},{6,0},{7,1},{8,14},{9,15},{10,... | collective-permute-start | bytes 786440 | tf_op jit(solution)/shard_map/ppermute | solution.py:426
  121.4 25.1 %collective-permute-start.14 = (bf16[64,2048]{1,0:T(8,128)(2,1)S(1)}, bf16[64,2048]{1,0:T(8,128)(2,1)S(1)}, u32[]{:S(2)}, u32[]{:S(2)}) collective-permute-start(bf16[64,2048]{1,0:T(8,128)(2,1)S(1)} %get-tuple-element.154.rest_0_), channel_id=1, source_target_pairs={{0,4},{1,5},{2,6},{3,7},{4,0},{5,1},{6,2},{7,3},{8,12},{9,13},{10,... | collective-permute-start | bytes 786440 | tf_op jit(solution)/shard_map/ppermute | solution.py:426
  133.2 13.8 %collective-permute-start.20 = (bf16[64,2048]{1,0:T(8,128)(2,1)S(1)}, bf16[64,2048]{1,0:T(8,128)(2,1)S(1)}, u32[]{:S(2)}, u32[]{:S(2)}) collective-permute-start(bf16[64,2048]{1,0:T(8,128)(2,1)S(1)} %collective-permute-done.19.rest_0_), channel_id=1, source_target_pairs={{0,1},{1,0},{2,3},{3,2},{4,5},{5,4},{6,7},{7,6},{8,9},{9,8},{10,11... | collective-permute-start | bytes 786440 | tf_op jit(solution)/shard_map/ppermute | solution.py:426
  140.5 17.3 %collective-permute-start.22 = (f32[72,256]{1,0:T(8,128)S(1)}, f32[72,256]{1,0:T(8,128)S(1)}, u32[]{:S(2)}, u32[]{:S(2)}) collective-permute-start(f32[72,256]{1,0:T(8,128)S(1)} %add.74), channel_id=1, source_target_pairs={{0,4},{1,5},{2,6},{3,7},{4,0},{5,1},{6,2},{7,3},{8,12},{9,13},{10,... | collective-permute-start | bytes 221192 | tf_op jit(solution)/shard_map/ppermute | solution.py:426
  141.2 17.3 %collective-permute-start.23 = (f32[72,256]{1,0:T(8,128)S(1)}, f32[72,256]{1,0:T(8,128)S(1)}, u32[]{:S(2)}, u32[]{:S(2)}) collective-permute-start(f32[72,256]{1,0:T(8,128)S(1)} %add.74), channel_id=1, source_target_pairs={{0,6},{1,7},{2,4},{3,5},{4,2},{5,3},{6,0},{7,1},{8,14},{9,15},{10,... | collective-permute-start | bytes 221192 | tf_op jit(solution)/shard_map/ppermute | solution.py:426
  143.2 15.2 %collective-permute-start.24 = (f32[72,256]{1,0:T(8,128)S(1)}, f32[72,256]{1,0:T(8,128)S(1)}, u32[]{:S(2)}, u32[]{:S(2)}) collective-permute-start(f32[72,256]{1,0:T(8,128)S(1)} %add.74), channel_id=1, source_target_pairs={{0,2},{1,3},{2,0},{3,1},{4,6},{5,7},{6,4},{7,5},{8,10},{9,11},{10,... | collective-permute-start | bytes 221192 | tf_op jit(solution)/shard_map/ppermute | solution.py:426
  146.5 21.3 %collective-permute-start.18 = (bf16[64,2048]{1,0:T(8,128)(2,1)S(1)}, bf16[64,2048]{1,0:T(8,128)(2,1)S(1)}, u32[]{:S(2)}, u32[]{:S(2)}) collective-permute-start(bf16[64,2048]{1,0:T(8,128)(2,1)S(1)} %collective-permute-done.17.rest_1_), channel_id=1, source_target_pairs={{0,1},{1,0},{2,3},{3,2},{4,5},{5,4},{6,7},{7,6},{8,9},{9,8},{10,11... | collective-permute-start | bytes 786440 | tf_op jit(solution)/shard_map/ppermute | solution.py:426
  147.0 20.7 %collective-permute-start.16 = (bf16[64,2048]{1,0:T(8,128)(2,1)S(1)}, bf16[64,2048]{1,0:T(8,128)(2,1)S(1)}, u32[]{:S(2)}, u32[]{:S(2)}) collective-permute-start(bf16[64,2048]{1,0:T(8,128)(2,1)S(1)} %collective-permute-done.14.rest_0_), channel_id=1, source_target_pairs={{0,1},{1,0},{2,3},{3,2},{4,5},{5,4},{6,7},{7,6},{8,9},{9,8},{10,11... | collective-permute-start | bytes 786440 | tf_op jit(solution)/shard_map/ppermute | solution.py:426
  157.8 32.5 %collective-permute-start.26 = (bf16[64,2048]{1,0:T(8,128)(2,1)S(1)}, bf16[64,2048]{1,0:T(8,128)(2,1)S(1)}, u32[]{:S(2)}, u32[]{:S(2)}) collective-permute-start(bf16[64,2048]{1,0:T(8,128)(2,1)S(1)} %get-tuple-element.175), channel_id=1, source_target_pairs={{0,1},{1,0},{2,3},{3,2},{4,5},{5,4},{6,7},{7,6},{8,9},{9,8},{10,11... | collective-permute-start | bytes 786440 | tf_op jit(solution)/shard_map/ppermute | solution.py:426
  177.1 13.2 %collective-permute-start.25 = (f32[72,256]{1,0:T(8,128)S(1)}, f32[72,256]{1,0:T(8,128)S(1)}, u32[]{:S(2)}, u32[]{:S(2)}) collective-permute-start(f32[72,256]{1,0:T(8,128)S(1)} %get-tuple-element.170), channel_id=1, source_target_pairs={{0,1},{1,0},{2,3},{3,2},{4,5},{5,4},{6,7},{7,6},{8,9},{9,8},{10,11... | collective-permute-start | bytes 221192 | tf_op jit(solution)/shard_map/ppermute | solution.py:426
  178.6 24.3 %collective-permute-start.33 = (bf16[64,2048]{1,0:T(8,128)(2,1)S(1)}, bf16[64,2048]{1,0:T(8,128)(2,1)S(1)}, u32[]{:S(2)}, u32[]{:S(2)}) collective-permute-start(bf16[64,2048]{1,0:T(8,128)(2,1)S(1)} %get-tuple-element.182), channel_id=1, source_target_pairs={{0,1},{1,0},{2,3},{3,2},{4,5},{5,4},{6,7},{7,6},{8,9},{9,8},{10,11... | collective-permute-start | bytes 786440 | tf_op jit(solution)/shard_map/ppermute | solution.py:426
  190.4 10.5 %collective-permute-start.27 = (f32[72,256]{1,0:T(8,128)S(1)}, f32[72,256]{1,0:T(8,128)S(1)}, u32[]{:S(2)}, u32[]{:S(2)}) collective-permute-start(f32[72,256]{1,0:T(8,128)S(1)} %add.78), channel_id=1, source_target_pairs={{0,4},{1,5},{2,6},{3,7},{4,0},{5,1},{6,2},{7,3},{8,12},{9,13},{10,... | collective-permute-start | bytes 221192 | tf_op jit(solution)/shard_map/ppermute | solution.py:426
  197.5 15.7 %collective-permute-start.37 = (bf16[64,2048]{1,0:T(8,128)(2,1)S(1)}, bf16[64,2048]{1,0:T(8,128)(2,1)S(1)}, u32[]{:S(2)}, u32[]{:S(2)}) collective-permute-start(bf16[64,2048]{1,0:T(8,128)(2,1)S(1)} %add_convert_fusion), channel_id=1, source_target_pairs={{0,6},{1,7},{2,4},{3,5},{4,2},{5,3},{6,0},{7,1},{8,14},{9,15},{10,... | collective-permute-start | bytes 786440 | tf_op jit(solution)/shard_map/ppermute | solution.py:426
  201.0 12.1 %collective-permute-start.31 = (f32[72,512]{1,0:T(8,128)S(1)}, f32[72,512]{1,0:T(8,128)S(1)}, u32[]{:S(2)}, u32[]{:S(2)}) collective-permute-start(f32[72,512]{1,0:T(8,128)S(1)} %pad_maximum_fusion), channel_id=1, source_target_pairs={{0,16},{8,24},{16,0},{24,8},{1,17},{9,25},{17,1},{25,9},{2,18},{10... | collective-permute-start | bytes 442376 | tf_op jit(solution)/shard_map/ppermute | solution.py:459
  202.6 10.5 %collective-permute-start.32 = (f32[72,512]{1,0:T(8,128)S(1)}, f32[72,512]{1,0:T(8,128)S(1)}, u32[]{:S(2)}, u32[]{:S(2)}) collective-permute-start(f32[72,512]{1,0:T(8,128)S(1)} %pad_maximum_fusion), channel_id=1, source_target_pairs={{0,24},{8,16},{16,8},{24,0},{1,25},{9,17},{17,9},{25,1},{2,26},{10... | collective-permute-start | bytes 442376 | tf_op jit(solution)/shard_map/ppermute | solution.py:459
  202.9 15.9 %collective-permute-start.35 = (bf16[64,2048]{1,0:T(8,128)(2,1)S(1)}, bf16[64,2048]{1,0:T(8,128)(2,1)S(1)}, u32[]{:S(2)}, u32[]{:S(2)}) collective-permute-start(bf16[64,2048]{1,0:T(8,128)(2,1)S(1)} %add_convert_fusion.1), channel_id=1, source_target_pairs={{0,4},{1,5},{2,6},{3,7},{4,0},{5,1},{6,2},{7,3},{8,12},{9,13},{10,... | collective-permute-start | bytes 786440 | tf_op jit(solution)/shard_map/ppermute | solution.py:426
  205.1 13.8 %collective-permute-start.38 = (bf16[64,2048]{1,0:T(8,128)(2,1)S(1)}, bf16[64,2048]{1,0:T(8,128)(2,1)S(1)}, u32[]{:S(2)}, u32[]{:S(2)}) collective-permute-start(bf16[64,2048]{1,0:T(8,128)(2,1)S(1)} %add_convert_fusion.2), channel_id=1, source_target_pairs={{0,2},{1,3},{2,0},{3,1},{4,6},{5,7},{6,4},{7,5},{8,10},{9,11},{10,... | collective-permute-start | bytes 786440 | tf_op jit(solution)/shard_map/ppermute | solution.py:426
  (35 other events, 511.7 us)

commit v4 on v3

--- a/solution.py
+++ b/solution.py
@@ -89,9 +89,10 @@
     groups = node_ref.shape[1] // WIDE
     table = node_groups(node_ref)
     bias = spread(vec_ref[0], piece)
+    place = lax.broadcasted_iota(jnp.int32, (WIDE, piece), 0).astype(bf16)
     for start in range(0, width, piece):
         ids = row_join(send_ref, start // LANES, piece // LANES)
-        onehot = onehot_rows(ids & (WIDE - 1), WIDE)
+        onehot = onehot_low(ids & (WIDE - 1), place)
         group = lax.shift_right_logical(ids, 8)
         found = dot(table, onehot)
         rows = found[:feat]
@@ -214,8 +215,8 @@
     base_ref[...] = upstream + input_grad[:feat]
     back_ref[...] = input_grad[feat:].astype(bf16)
     pack_ref[...] = jnp.zeros_like(pack_ref)
-    pack_ref[:feat, : 2 * feat] = dot_nt(third, node_inputs)
-    pack_ref[:feat, 2 * feat : 3 * feat] = dot_nt(act_low, grad)
+    pack_ref[:feat, 4 * feat : 6 * feat] = dot_nt(third, node_inputs)
+    pack_ref[:feat, 6 * feat : 7 * feat] = dot_nt(act_low, grad)
     ones = jnp.ones((8, LANES), f32)
     sums = (
         fold(third.astype(f32)),
@@ -224,7 +225,7 @@
         fold(upstream),
     )
     for k in range(4):
-        pack_ref[feat + k : feat + k + 1, :feat] = dot_nt_exact(ones, sums[k])[:1]
+        pack_ref[feat + k : feat + k + 1, 4 * feat : 5 * feat] = dot_nt_exact(ones, sums[k])[:1]
 
 
 def backward_kernel(masks, blocks, piece, extra, meta_ref, code_ref, cot_ref, normed_ref, act_ref, slope_ref, inv_ref, edge_ref, pick_ref, out_ref, in_ref, vec_ref, *rest):
@@ -306,15 +307,22 @@
         ones = jnp.ones((8, LANES), f32)
         for k in range(4):
             pack_ref[feat + k : feat + k + 1, :feat] = dot_nt_exact(ones, sum_ref[k])[:1]
-        if extra:
-            pack_ref[...] += prior_refs[2][...]
-
-
-def sender_sum_kernel(grad_ref, send_ref, sum_ref, token_ref, total_ref):
+        pack_ref[...] += prior_refs[0][...]
+
+
+def sender_sum_kernel(starts, me_ref, send_ref, *rest):
+    grad_refs = rest[: len(starts)]
+    sum_ref, token_ref, total_ref, grad_ref = rest[len(starts) :]
     feat, width = grad_ref.shape
     groups = sum_ref.shape[1] // WIDE
     step = pl.program_id(0)
     token_ref[...] = jnp.zeros_like(token_ref)
+    for k, start in enumerate(starts):
+        after = starts[k + 1] if k + 1 < len(starts) else pl.num_programs(0)
+
+        @pl.when((step >= start) & (step < after))
+        def _():
+            grad_ref[...] = grad_refs[k][...]
 
     @pl.when(step == 0)
     def _():
@@ -439,15 +447,8 @@
             found[m | 1] = swap(tie(found[m], gate), 1)
         return found
 
-    def swap_near(parts):
-        return {m: swap(parts[m | 1], 1) for m in routed + [0]}
-
-    def sum_out(parts, got):
-        sums = [parts[0], got[0]]
-        for m in routed:
-            both = (parts[m].astype(f32) + got[m].astype(f32)).astype(bf16)
-            sums.append(both)
-        return sums[:2] + [swap(both, m) for both, m in zip(sums[2:], routed)], sums[-1]
+    def join(parts, got, m):
+        return (parts[m].astype(f32) + got[m].astype(f32)).astype(bf16)
 
     def add_groups(value):
         if groups > 4:
@@ -459,23 +460,14 @@
         others = [lax.ppermute(value, "grp", [(i, i ^ mask) for i in range(groups)]) for mask in range(1, groups)]
         return sum(others, value)
 
-    def add_far(value):
-        if peers > 8:
-            mask = 2
-            while mask < peers:
-                value = value + swap(value, mask)
-                mask *= 2
-            return value
-        return sum([swap(value, m) for m in routed], value)
-
     halves = [tuple(range(0, peers, 2)), tuple(range(1, peers, 2))]
-    send_teams = halves
-    quarter = (peers + 3) // 4
-    teams = [halves[0][:quarter], halves[1], halves[0][quarter:]]
-    teams = [masks for masks in teams if masks]
-    back_teams = [(0, 1), (2, 3)][: (peers + 3) // 4]
-    for m in range(4, peers, 4):
-        back_teams += [(m, m + 2), (m + 1, m + 3)]
+    firsts_of = list(range(0, peers, 4))
+    pair = lambda m: (m, m + 2) if m + 2 < peers else (m,)
+    teams = [pair(m + side) for m in firsts_of[::-1] for side in (1, 0)]
+    back_teams = [pair(0)]
+    for m in firsts_of[1:]:
+        back_teams += [pair(m), pair(m + 1)]
+    back_teams.append(pair(1))
 
     node_t = nodes.T
     edge_t = edges.T
@@ -503,7 +495,7 @@
     wide = min(4096, per_peer)
     chunks = per_peer // wide
     sub = wide // LANES
-    piece = min(1024, wide)
+    piece = min(2048, wide)
 
     def slab_of(masks):
         return pl.BlockSpec((feat, wide), lambda i, j, ref: (0, owner(masks, i, ref) * chunks + j))
@@ -526,92 +518,108 @@
     token_spec = whole((8, LANES))
     slab_shape = struct((feat, edge_total), bf16)
     shard_shape = struct((feat, node_total), bf16)
-    chain = []
-    for masks in send_teams:
+    picks, bases = [], []
+    for masks in halves:
         count = len(masks)
-        extra = len(chain)
         pick, base, gate = pl.pallas_call(
-            functools.partial(sender_kernel, min(512, wide), extra),
+            functools.partial(sender_kernel, min(1024, wide), 0),
             grid_spec=pltpu.PrefetchScalarGridSpec(
                 num_scalar_prefetch=1,
                 grid=(count, chunks),
-                in_specs=[shard_spec, rows_of(masks), slab_of(masks), whole((feat, 2 * feat)), whole((8, feat, LANES))] + [keep_spec] * extra,
-                out_specs=[slab_of(masks), slab_of(masks), token_spec],
+                in_specs=[shard_spec, rows_of(masks), slab_of(masks), whole((feat, 2 * feat)), whole((8, feat, LANES))],
+                out_specs=[own_slab, own_slab, token_spec],
             ),
-            out_shape=[slab_shape, struct((feat, edge_total), f32), token],
-            input_output_aliases={6 + k: k for k in range(extra)},
+            out_shape=[struct((feat, count * per_peer), bf16), struct((feat, count * per_peer), f32), token],
             compiler_params=params(),
             name="sender",
-        )(me, node_t, send, edge_t, se_weight, vec, *chain)
-        if not chain:
+        )(me, node_t, send, edge_t, se_weight, vec)
+        if not picks:
             shards = gather_rest(shards, gate)
             send = tie(send, *[shards[m] for m in routed])
-            live = jnp.arange(LANES, dtype=jnp.int32)[None, :] < tie(block_count, gate, *[shards[m] for m in routed])[:, None]
+            live = jnp.arange(LANES, dtype=jnp.int32)[None, :] < tie(block_count, gate, *[shards[m] for m in [1] + routed])[:, None]
             code = slot_ids.reshape(block_total, LANES) + jnp.where(live, 0, LANES) + 2 * LANES * block_tile[:, None]
             code = lax.all_to_all(code, "peer", 0, 0, tiled=True)
             meta = jnp.concatenate([me, code[:, 0] // (2 * LANES)])
             code = (code & (2 * LANES - 1)).reshape(peers, blocks, LANES)
-        chain = [pick, base]
+        picks.append(pick)
+        bases.append(base)
 
     parts = {}
     chain = []
+    saved = {}
+    got = {}
+    both = {}
     for masks in teams:
         count = len(masks)
         extra = len(chain)
-        *outs, = pl.pallas_call(
+        half_at, place = masks[0] % 2, masks[0] // 2
+        base = bases[half_at]
+        if masks == teams[-1] and len(teams) > 2:
+            both = {m: join(parts, got, m) for m in routed if m in parts}
+            base = tie(base, *both.values())
+        result, act, slope, normed, inv, gate, *pieces = pl.pallas_call(
             functools.partial(forward_kernel, masks, blocks, piece, extra),
             grid_spec=pltpu.PrefetchScalarGridSpec(
                 num_scalar_prefetch=1,
                 grid=(count, chunks),
-                in_specs=[code_of(masks), slab_of(masks), slab_of(masks), whole((feat, feat)), whole((feat, feat)), whole((8, feat, LANES))]
+                in_specs=[code_of(masks), kept_slab(place), slab_of(masks), whole((feat, feat)), whole((feat, feat)), whole((8, feat, LANES))]
                 + [shard_spec] * count
                 + [keep_spec] * extra,
-                out_specs=[slab_of(masks)] * 4 + [rows_of(masks), token_spec] + [shard_spec] * count,
+                out_specs=[slab_of(masks)] + [own_slab] * 3 + [own_rows, token_spec] + [shard_spec] * count,
                 scratch_shapes=[pltpu.VMEM((feat, node_total), f32), pltpu.VMEM((feat, node_total), f32)],
             ),
-            out_shape=[slab_shape] * 4 + [struct((rows, LANES), f32), token] + [shard_shape] * count,
-            input_output_aliases={7 + count + k: k for k in range(extra)},
+            out_shape=[slab_shape] + [struct((feat, count * per_peer), bf16)] * 3
+            + [struct((count * blocks, LANES), f32), token]
+            + [shard_shape] * count,
+            input_output_aliases={7 + count: 0} if extra else {},
             compiler_params=params(),
             name="forward",
         )(meta, code, base, edge_t, re_weight, out_t, vec, *[shards[m] for m in masks], *chain)
-        chain = outs[:5]
-        parts.update(zip(masks, outs[6:]))
-    result, act, slope, normed, inv = chain
+        chain = [result]
+        saved[masks] = (normed, act, slope, inv)
+        parts.update(zip(masks, pieces))
+        if half_at:
+            got.update({m - 1: swap(parts[m], 1) for m in masks})
     edge_result = result
-
-    sums, _ = sum_out(parts, swap_near(parts))
+    for m in routed:
+        if m not in both:
+            both[m] = join(parts, got, m)
+    sums = [parts[0], got[0]] + [swap(both[m], m) for m in routed]
+
     node_result, node_base, back, node_pack = pl.pallas_call(
         functools.partial(node_kernel, len(sums)),
         out_shape=[
             struct((feat, node_total), bf16),
             struct((feat, node_total), f32),
             struct((feat, node_total), bf16),
-            struct((feat + 8, 4 * feat), f32),
+            struct((feat + 8, 8 * feat), f32),
         ],
         compiler_params=params(),
         name="node",
     )(node_t, node_cot_t, node_in_weight.T, node_back, node_out_t, node_out_weight, vec, *sums)
 
-    near_pack = swap(node_pack, 1)
     backs = gather_first(back)
 
     parts = {}
-    chain = []
+    got = {}
+    chain = [node_pack]
+    first_grads = {}
     for masks in back_teams:
         count = len(masks)
         extra = len(chain)
-        if masks == back_teams[-1] and extra:
-            chain[2] = tie(chain[2], node_sum)
+        half_at, place = masks[0] % 2, masks[0] // 2
+        normed, act, slope, inv = saved[masks]
         *outs, = pl.pallas_call(
             functools.partial(backward_kernel, masks, blocks, piece, extra),
             grid_spec=pltpu.PrefetchScalarGridSpec(
                 num_scalar_prefetch=1,
                 grid=(count, chunks),
-                in_specs=[code_of(masks)] + [slab_of(masks)] * 4 + [rows_of(masks)] + [slab_of(masks)] * 2
+                in_specs=[code_of(masks), slab_of(masks)] + [own_slab] * 3 + [own_rows, slab_of(masks), kept_slab(place)]
                 + [whole((feat, feat)), whole((feat, feat)), whole((8, feat, LANES))]
                 + [shard_spec] * (2 * count)
-                + ([keep_spec] * 2 + [whole((feat + 8, 4 * feat))] if extra else []),
-                out_specs=[slab_of(masks), slab_of(masks), whole((feat + 8, 4 * feat)), token_spec] + [shard_spec] * count,
+                + [whole((feat + 8, 8 * feat))]
+                + [keep_spec] * (extra - 1),
+                out_specs=[slab_of(masks), own_slab, whole((feat + 8, 8 * feat)), token_spec] + [shard_spec] * count,
                 scratch_shapes=[
                     pltpu.VMEM((feat, node_total), f32),
                     pltpu.VMEM((feat, node_total), f32),
@@ -623,56 +631,91 @@
             ),
             out_shape=[
                 struct((feat, edge_total), f32),
-                slab_shape,
-                struct((feat + 8, 4 * feat), f32),
+                struct((feat, count * per_peer), bf16),
+                struct((feat + 8, 8 * feat), f32),
                 token,
             ]
             + [shard_shape] * count,
-            input_output_aliases={12 + 2 * count + k: k for k in range(2 if extra else 0)},
+            input_output_aliases={13 + 2 * count: 0} if extra > 1 else {},
             compiler_params=params(),
             name="backward",
         )(
-            meta, code, edge_cot_t, normed, act, slope, inv, edge_t, pick, back_weight, edge_back, vec,
+            meta, code, edge_cot_t, normed, act, slope, inv, edge_t, picks[half_at], back_weight, edge_back, vec,
             *[backs[m] for m in masks], *[shards[m] for m in masks], *chain,
         )
-        chain, gate = outs[:3], outs[3]
-        parts.update(zip(masks, outs[4:]))
-        if not extra:
+        edge_grad, first_grads[masks], edge_pack, gate, *pieces = outs
+        chain = [edge_pack, edge_grad]
+        parts.update(zip(masks, pieces))
+        if half_at:
+            got.update({m - 1: swap(parts[m], 1) for m in masks})
+        if masks == back_teams[0]:
             backs = gather_rest(backs, gate)
-            node_sum = node_pack + near_pack
-        elif masks == back_teams[1]:
-            node_sum = add_far(tie(node_sum, gate))
-    edge_grad, first_grad, edge_pack = chain
 
     near_pack = swap(edge_pack, 1)
-    got = swap_near(parts)
-
-    sent, gates = [], []
+    late = [m for m in routed if m + 1 in back_teams[-1]]
+    early = [m for m in routed if m not in late]
+    both = {}
+    marks = []
+    if early:
+        marks = lax.optimization_barrier([got[m] for m in early])
+        both = {m: join(parts, {m: value}, m) for m, value in zip(early, marks)}
+        marks = [both[m] for m in early]
+    there = {m: swap(both[m], m) for m in early}
+    edge_pack = edge_pack + tie(near_pack, *marks)
+    far = swap(edge_pack, peers // 2) if peers > 2 else None
+
     sum_wide = min(2048, per_peer)
-    steps = edge_total // sum_wide // 2
-    for start in (0, steps):
-        if gates:
-            got = {m: tie(value, gates[0]) for m, value in got.items()}
-            sums, mark = sum_out(parts, got)
-            edge_pack = add_far(tie(edge_pack + tie(near_pack, gates[0]), mark))
-            first_grad = tie(first_grad, mark)
-        total, gate = pl.pallas_call(
-            sender_sum_kernel,
-            grid=(steps,),
-            in_specs=[
-                pl.BlockSpec((feat, sum_wide), lambda i, start=start: (0, start + i)),
-                pl.BlockSpec((sum_wide // LANES, LANES), lambda i, start=start: (start + i, 0)),
-            ],
-            out_specs=[shard_spec, token_spec],
+    sum_chunks = per_peer // sum_wide
+
+    def add_sent(masks_list, hold):
+        masks = [m for masks in masks_list for m in masks]
+        arrays = [first_grads[masks] for masks in masks_list]
+        if hold:
+            arrays[0] = tie(arrays[0], *hold)
+        spans = [a.shape[1] // sum_wide for a in arrays]
+        starts = [sum(spans[:k]) for k in range(len(spans))]
+
+        def send_at(i, ref):
+            step = i // sum_chunks
+            mask = masks[0]
+            for k in range(1, len(masks)):
+                mask = jnp.where(step == k, masks[k], mask)
+            return ((ref[0] ^ mask) * sum_chunks + i % sum_chunks, 0)
+
+        return pl.pallas_call(
+            functools.partial(sender_sum_kernel, tuple(starts)),
+            grid_spec=pltpu.PrefetchScalarGridSpec(
+                num_scalar_prefetch=1,
+                grid=(len(masks) * sum_chunks,),
+                in_specs=[pl.BlockSpec((sum_wide // LANES, LANES), send_at)]
+                + [
+                    pl.BlockSpec((feat, sum_wide), lambda i, ref, start=start, span=span: (0, jnp.clip(i - start, 0, span - 1)))
+                    for start, span in zip(starts, spans)
+                ],
+                out_specs=[shard_spec, token_spec],
+                scratch_shapes=[pltpu.VMEM((node_total // WIDE * feat, WIDE), f32), pltpu.VMEM((feat, sum_wide), bf16)],
+            ),
             out_shape=[struct((feat, node_total), f32), token],
-            scratch_shapes=[pltpu.VMEM((node_total // WIDE * feat, WIDE), f32)],
             compiler_params=params(),
             name="sender_sum",
-        )(first_grad, send)
-        sent.append(total)
-        gates.append(gate)
-
-    both_packs = add_groups(jnp.concatenate([tie(edge_pack, gates[1]), node_sum], axis=1))
+        )(me, send, *arrays)
+
+    sent_first, gate = add_sent(back_teams[:-1], marks)
+    for m in late:
+        both[m] = join(parts, {m: tie(got[m], gate)}, m)
+        there[m] = swap(both[m], m)
+    if far is not None:
+        edge_pack = edge_pack + tie(far, gate)
+        edge_pack = add_groups(edge_pack)
+        mask = 2
+        while mask < peers // 2:
+            edge_pack = edge_pack + swap(edge_pack, mask)
+            mask *= 2
+    sent_last, gate = add_sent(back_teams[-1:], [there[m] for m in early])
+    sent = [sent_first, sent_last]
+    both_packs = tie(edge_pack, gate)
+    sums = [parts[0], got[0]] + [there[m] for m in routed]
+
     vec_out = struct((1, feat), f32)
     node_grad, e1, b1, e2, b2, g1, s1, n1, c1, n2, c2, g2, s2 = pl.pallas_call(
         functools.partial(finish_kernel, len(sent), len(sums)),

time: 221 us -> 207 us (0.937)
  waiting for transfers between devices: 36 us -> 48.9 us
  starting transfers between devices: 55.6 us -> 44.5 us
  local copies, waits for them, and re-layouts: 18.4 us -> 10.2 us
  Pallas kernels: 107 us -> 100 us
    ppermute x36 -> x31, starting transfers between devices: 48.3 us -> 37.8 us  [swap(): return lax.ppermute(value, 'peer', [(i, i ^ mask) for i in range(peers)])]
    unnamed x55 -> x65, local copies, waits for them, and re-layouts: 18.2 us -> 10.1 us
    ppermute x36 -> x31, waiting for transfers between devices: 36 us -> 43.4 us  [swap(): return lax.ppermute(value, 'peer', [(i, i ^ mask) for i in range(peers)])]
    ppermute x3, waiting for transfers between devices: 0.01 us -> 5.52 us  [add_groups(): lax.ppermute(value, 'grp', [(i, i ^ mask) for i in range(groups)])]
    pallas_call x4, Pallas kernels: 40 us -> 35.1 us  [the longest x2 20.4 us: per_device(): pl.pallas_call(functools.partial(sender_kernel, min(1024, wide), 0), grid...]
    pallas_call x4, Pallas kernels: 37.5 us -> 34.7 us  [per_device(): pl.pallas_call(functools.partial(backward_kernel, masks, blocks, piece, e...]
    pallas_call x3 -> x4, Pallas kernels: 24.9 us -> 25.2 us  [per_device(): pl.pallas_call(functools.partial(forward_kernel, masks, blocks, piece, ex...]
  transfers between devices with their start and end apart: 40 -> 35, of which waited for: 12 -> 13; matrix products, arithmetic and copies ran while one was open for 1% -> 1% of each run, Pallas kernels for 42% -> 47%
where the time goes in v4:
time: 207 us
  Pallas kernels  100 us (48%)
  waiting for transfers between devices  48.9 us (24%)
  starting transfers between devices  44.5 us (21%)
  local copies, waits for them, and re-layouts  10.2 us (5%)
  other arithmetic  2.09 us (1%)
    ppermute x31, waiting for transfers between devices, swap(): return lax.ppermute(value, 'peer', [(i, i ^ mask) for i in range(peers)])  43.4 us
    ppermute x31, starting transfers between devices, swap(): return lax.ppermute(value, 'peer', [(i, i ^ mask) for i in range(peers)])  37.8 us
    pallas_call x4, Pallas kernels, per_device(): pl.pallas_call(functools.partial(backward_kernel, masks, blocks, piece, e...  34.7 us
    pallas_call x4, Pallas kernels, per_device(): pl.pallas_call(functools.partial(forward_kernel, masks, blocks, piece, ex...  25.2 us
    pallas_call x2, Pallas kernels, per_device(): pl.pallas_call(functools.partial(sender_kernel, min(1024, wide), 0), grid...  20.4 us
    pallas_call x2, Pallas kernels, add_sent(): pl.pallas_call(functools.partial(sender_sum_kernel, tuple(starts)), grid_...  14.6 us
    unnamed x65, local copies, waits for them, and re-layouts  10.1 us
    ppermute x3, waiting for transfers between devices, add_groups(): lax.ppermute(value, 'grp', [(i, i ^ mask) for i in range(groups)])  5.52 us
  transfers between devices with their start and end apart: 35, of which 13 were waited for; matrix products, arithmetic and copies ran while one was open for 1% of the time, Pallas kernels for 47%

profile of v4, /device:TPU:0, one launch (start us, length us, event | category | flops | bytes accessed | tf_op | source)
XLA Modules:
  0.0 206.9 jit_solution(9384201521061191937)
XLA Ops:
  0.7 3.1 %collective-permute-start.3 = (bf16[64,2048]{1,0:T(8,128)(2,1)}, bf16[64,2048]{1,0:T(8,128)(2,1)S(1)}, u32[]{:S(2)}, u32[]{:S(2)}) collective-permute-start(bf16[64,2048]{1,0:T(8,128)(2,1)} %bitcast.34), channel_id=1, source_target_pairs={{0,2},{1,3},{2,0},{3,1},{4,6},{5,7},{6,4},{7,5},{8,10},{9,11},{10,... | collective-permute-start | bytes 786440 | tf_op jit(solution)/shard_map/ppermute | solution.py:434
  3.8 2.5 %collective-permute-start.2 = (bf16[64,2048]{1,0:T(8,128)(2,1)}, bf16[64,2048]{1,0:T(8,128)(2,1)S(1)}, u32[]{:S(2)}, u32[]{:S(2)}) collective-permute-start(bf16[64,2048]{1,0:T(8,128)(2,1)} %bitcast.35), channel_id=1, source_target_pairs={{0,6},{1,7},{2,4},{3,5},{4,2},{5,3},{6,0},{7,1},{8,14},{9,15},{10,... | collective-permute-start | bytes 786440 | tf_op jit(solution)/shard_map/ppermute | solution.py:434
  8.6 1.8 prepare.1
  14.0 10.3 %sender.2 = (bf16[64,16384]{1,0:T(8,128)(2,1)S(1)}, f32[64,16384]{1,0:T(8,128)}, f32[8,128]{1,0:T(8,128)}) custom-call(s32[1]{0:T(128)} %bitcast.12.me_ref, bf16[64,2048]{1,0:T(8,128)(2,1)S(1)} %bitcast.38, s32[256,128]{1,0:T(8,128)S(1)} %bitcast.43, bf16[64,32768]{1,0:T(8,128)(2,1)} %bitcast.50, bf16[64,128]{1,0:T(8,128)(2,1)S(1)} %copy-done.23, ...), custom_call_target="tpu_custom_call" | custom-call | tf_op jit(solution)/shard_map/sender/pallas_call | solution.py:524
  25.6 3.9 %collective-permute-done.1.rest_0_.rest_2_ = bf16[64,2048]{1,0:T(8,128)(2,1)S(1)} collective-permute-done((bf16[64,2048]{1,0:T(8,128)(2,1)}, bf16[64,2048]{1,0:T(8,128)(2,1)S(1)}, u32[]{:S(2)}, u32[]{:S(2)}) %collective-permute-start.1) | collective-permute-done | bytes 262176 | tf_op jit(solution)/shard_map/ppermute | solution.py:434
  30.4 4.8 %all-to-all-start = ((s32[8,32,128]{2,1,0:T(8,128)}), s32[8,32,128]{2,1,0:T(8,128)S(1)}, u32[]{:S(2)}, u32[]{:S(2)}) async-start(s32[8,32,128]{2,1,0:T(8,128)} %add_add_fusion.1), calls=%async_computation | async-start | bytes 262144 | tf_op jit(solution)/shard_map/all_to_all | solution.py:541
  35.2 2.0 collective-permute-start.4
  37.2 2.0 collective-permute-start.8
  39.2 10.2 %sender.3 = (bf16[64,16384]{1,0:T(8,128)(2,1)S(1)}, f32[64,16384]{1,0:T(8,128)}, f32[8,128]{1,0:T(8,128)}) custom-call(s32[1]{0:T(128)} %bitcast.12.me_ref, bf16[64,2048]{1,0:T(8,128)(2,1)S(1)} %bitcast.39, s32[256,128]{1,0:T(8,128)S(1)} %bitcast.44, bf16[64,32768]{1,0:T(8,128)(2,1)} %bitcast.51, bf16[64,128]{1,0:T(8,128)(2,1)S(1)} %copy-done.24, ...), custom_call_target="tpu_custom_call" | custom-call | tf_op jit(solution)/shard_map/sender/pallas_call | solution.py:524
  51.9 6.3 %forward.4 = (bf16[64,32768]{1,0:T(8,128)(2,1)}, bf16[64,8192]{1,0:T(8,128)(2,1)S(1)}, bf16[64,8192]{1,0:T(8,128)(2,1)S(1)}, bf16[64,8192]{1,0:T(8,128)(2,1)S(1)...) custom-call(s32[257]{0:T(512)S(1)} %pad_add_fusion.meta_ref, ...), custom_call_target="tpu_custom_call" | custom-call | tf_op jit(solution)/shard_map/forward/pallas_call | solution.py:560
  62.2 6.3 %forward.5 = (bf16[64,32768]{1,0:T(8,128)(2,1)}, bf16[64,8192]{1,0:T(8,128)(2,1)S(1)}, bf16[64,8192]{1,0:T(8,128)(2,1)S(1)}, bf16[64,8192]{1,0:T(8,128)(2,1)S(1)...) custom-call(s32[257]{0:T(512)S(1)} %pad_add_fusion.meta_ref, ...), custom_call_target="tpu_custom_call", output_to_operand_aliasing={{0}: (9, {})} | custom-call | tf_op jit(solution)/shard_map/forward/pallas_call | solution.py:560
  68.5 6.4 %forward.6 = (bf16[64,32768]{1,0:T(8,128)(2,1)}, bf16[64,8192]{1,0:T(8,128)(2,1)S(1)}, bf16[64,8192]{1,0:T(8,128)(2,1)S(1)}, bf16[64,8192]{1,0:T(8,128)(2,1)S(1)...) custom-call(s32[257]{0:T(512)S(1)} %pad_add_fusion.meta_ref, ...), custom_call_target="tpu_custom_call", output_to_operand_aliasing={{0}: (9, {})} | custom-call | tf_op jit(solution)/shard_map/forward/pallas_call | solution.py:560
  77.1 3.2 %collective-permute-start.11 = (bf16[64,2048]{1,0:T(8,128)(2,1)S(1)}, bf16[64,2048]{1,0:T(8,128)(2,1)S(1)}, u32[]{:S(2)}, u32[]{:S(2)}) collective-permute-start(bf16[64,2048]{1,0:T(8,128)(2,1)S(1)} %add_convert_fusion.4), channel_id=1, source_target_pairs={{0,6},{1,7},{2,4},{3,5},{4,2},{5,3},{6,0},{7,1},{8,14},{9,15},{10,... | collective-permute-start | bytes 786440 | tf_op jit(solution)/shard_map/ppermute | solution.py:434
  80.5 6.3 %forward.7 = (bf16[64,32768]{1,0:T(8,128)(2,1)}, bf16[64,8192]{1,0:T(8,128)(2,1)S(1)}, bf16[64,8192]{1,0:T(8,128)(2,1)S(1)}, bf16[64,8192]{1,0:T(8,128)(2,1)S(1)...) custom-call(s32[257]{0:T(512)S(1)} %pad_add_fusion.meta_ref, ...), custom_call_target="tpu_custom_call", output_to_operand_aliasing={{0}: (9, {})} | custom-call | tf_op jit(solution)/shard_map/forward/pallas_call | solution.py:560
  89.1 10.0 %collective-permute-done.10.rest_2_ = bf16[64,2048]{1,0:T(8,128)(2,1)S(1)} collective-permute-done((bf16[64,2048]{1,0:T(8,128)(2,1)S(1)}, bf16[64,2048]{1,0:T(8,128)(2,1)S(1)}, u32[]{:S(2)}, u32[]{:S(2)}) %collective-permute-start.10) | collective-permute-done | bytes 262176 | tf_op jit(solution)/shard_map/ppermute | solution.py:434
  99.9 1.7 node.1
  101.5 2.1 %collective-permute-start.19 = (bf16[64,2048]{1,0:T(8,128)(2,1)S(1)}, bf16[64,2048]{1,0:T(8,128)(2,1)S(1)}, u32[]{:S(2)}, u32[]{:S(2)}) collective-permute-start(bf16[64,2048]{1,0:T(8,128)(2,1)S(1)} %get-tuple-element.152.rest_0_), channel_id=1, source_target_pairs={{0,6},{1,7},{2,4},{3,5},{4,2},{5,3},{6,0},{7,1},{8,14},{9,15},{10,... | collective-permute-start | bytes 786440 | tf_op jit(solution)/shard_map/ppermute | solution.py:434
  105.1 6.8 %collective-permute-done.15.rest_1_ = bf16[64,2048]{1,0:T(8,128)(2,1)S(1)} collective-permute-done((bf16[64,2048]{1,0:T(8,128)(2,1)S(1)}, bf16[64,2048]{1,0:T(8,128)(2,1)S(1)}, u32[]{:S(2)}, u32[]{:S(2)}) %collective-permute-start.15) | collective-permute-done | bytes 262176 | tf_op jit(solution)/shard_map/ppermute | solution.py:434
  111.9 8.8 %backward.4 = (f32[64,32768]{1,0:T(8,128)}, bf16[64,8192]{1,0:T(8,128)(2,1)S(1)}, f32[72,512]{1,0:T(8,128)S(1)}, f32[8,128]{1,0:T(8,128)}, bf16[64,2048]{1,0:T(8,128)(2,1)S(1)}, /*index=5*/bf16[64,2048]{1,0:T(8,128)(2,1)S(1)}) custom-call(s32[257]{0:T(512)S(1)} %pad_add_fusion.meta_ref, s32[8,32,128]{2,1,0:T(8,128)S(1)} %broadcast_and_fusion.code_ref, ...), custom_call_target="tpu_custom_call" | custom-call | tf_op jit(solution)/shard_map/backward/pallas_call | solution.py:612
  120.7 5.5 %collective-permute-done.17.rest_0_ = bf16[64,2048]{1,0:T(8,128)(2,1)S(1)} collective-permute-done((bf16[64,2048]{1,0:T(8,128)(2,1)S(1)}, bf16[64,2048]{1,0:T(8,128)(2,1)S(1)}, u32[]{:S(2)}, u32[]{:S(2)}) %collective-permute-start.17) | collective-permute-done | bytes 262176 | tf_op jit(solution)/shard_map/ppermute | solution.py:434
  130.3 8.6 %backward.5 = (f32[64,32768]{1,0:T(8,128)}, bf16[64,8192]{1,0:T(8,128)(2,1)S(1)}, f32[72,512]{1,0:T(8,128)S(1)}, f32[8,128]{1,0:T(8,128)}, bf16[64,2048]{1,0:T(8,128)(2,1)S(1)}, /*index=5*/bf16[64,2048]{1,0:T(8,128)(2,1)S(1)}) custom-call(s32[257]{0:T(512)S(1)} %pad_add_fusion.meta_ref, ...), custom_call_target="tpu_custom_call", output_to_operand_aliasing={{0}: (17, {})} | custom-call | tf_op jit(solution)/shard_map/backward/pallas_call | solution.py:612
  138.9 2.1 %collective-permute-done.20.rest_1_ = bf16[64,2048]{1,0:T(8,128)(2,1)S(1)} collective-permute-done((bf16[64,2048]{1,0:T(8,128)(2,1)S(1)}, bf16[64,2048]{1,0:T(8,128)(2,1)S(1)}, u32[]{:S(2)}, u32[]{:S(2)}) %collective-permute-start.20) | collective-permute-done | bytes 262176 | tf_op jit(solution)/shard_map/ppermute | solution.py:434
  141.0 8.6 %backward.6 = (f32[64,32768]{1,0:T(8,128)}, bf16[64,8192]{1,0:T(8,128)(2,1)S(1)}, f32[72,512]{1,0:T(8,128)S(1)}, f32[8,128]{1,0:T(8,128)}, bf16[64,2048]{1,0:T(8,128)(2,1)S(1)}, /*index=5*/bf16[64,2048]{1,0:T(8,128)(2,1)S(1)}) custom-call(s32[257]{0:T(512)S(1)} %pad_add_fusion.meta_ref, ...), custom_call_target="tpu_custom_call", output_to_operand_aliasing={{0}: (17, {})} | custom-call | tf_op jit(solution)/shard_map/backward/pallas_call | solution.py:612
  151.7 8.6 %backward.7 = (f32[64,32768]{1,0:T(8,128)}, bf16[64,8192]{1,0:T(8,128)(2,1)S(1)}, f32[72,512]{1,0:T(8,128)S(1)}, f32[8,128]{1,0:T(8,128)}, bf16[64,2048]{1,0:T(8,128)(2,1)S(1)}, /*index=5*/bf16[64,2048]{1,0:T(8,128)(2,1)S(1)}) custom-call(s32[257]{0:T(512)S(1)} %pad_add_fusion.meta_ref, ...), custom_call_target="tpu_custom_call", output_to_operand_aliasing={{0}: (17, {})} | custom-call | tf_op jit(solution)/shard_map/backward/pallas_call | solution.py:612
  163.6 3.4 %collective-permute-done.21 = f32[72,512]{1,0:T(8,128)S(1)} collective-permute-done((f32[72,512]{1,0:T(8,128)S(1)}, f32[72,512]{1,0:T(8,128)S(1)}, u32[]{:S(2)}, u32[]{:S(2)}) %collective-permute-start.21) | collective-permute-done | bytes 147488 | tf_op jit(solution)/shard_map/ppermute | solution.py:434
  169.2 10.8 %sender_sum.2 = (f32[64,2048]{1,0:T(8,128)S(1)}, f32[8,128]{1,0:T(8,128)}) custom-call(s32[1]{0:T(128)} %bitcast.12.me_ref, s32[256,128]{1,0:T(8,128)S(1)} %bitcast.45, bf16[64,8192]{1,0:T(8,128)(2,1)S(1)} %get-tuple-element.186.rest_0_, bf16[64,8192]{1,0:T(8,128)(2,1)S(1)} %get-tuple-element.187.rest_1_, bf16[64,8192]{1,0:T(8,128)(2,1)S(1)} %get-tuple-element.188.rest_2_), custom_call_target="tpu_custom_call" | custom-call | tf_op jit(solution)/shard_map/sender_sum/pallas_call | solution.py:685
  180.1 1.5 collective-permute-start.26
  182.0 4.2 %collective-permute-done.27 = f32[72,512]{1,0:T(8,128)S(1)} collective-permute-done((f32[72,512]{1,0:T(8,128)S(1)}, f32[72,512]{1,0:T(8,128)S(1)}, u32[]{:S(2)}, u32[]{:S(2)}) %collective-permute-start.27) | collective-permute-done | bytes 147488 | tf_op jit(solution)/shard_map/ppermute | solution.py:460
  186.2 1.9 collective-permute-start.29
  189.4 2.2 %collective-permute-start.33 = (bf16[64,2048]{1,0:T(8,128)(2,1)S(1)}, bf16[64,2048]{1,0:T(8,128)(2,1)S(1)}, u32[]{:S(2)}, u32[]{:S(2)}) collective-permute-start(bf16[64,2048]{1,0:T(8,128)(2,1)S(1)} %add_convert_fusion), channel_id=1, source_target_pairs={{0,2},{1,3},{2,0},{3,1},{4,6},{5,7},{6,4},{7,5},{8,10},{9,11},{10,... | collective-permute-start | bytes 786440 | tf_op jit(solution)/shard_map/ppermute | solution.py:434
  191.7 9.4 %collective-permute-done.29.rest_4_ = bf16[64,2048]{1,0:T(8,128)(2,1)S(1)} collective-permute-done((bf16[64,2048]{1,0:T(8,128)(2,1)S(1)}, bf16[64,2048]{1,0:T(8,128)(2,1)S(1)}, u32[]{:S(2)}, u32[]{:S(2)}) %collective-permute-start.29) | collective-permute-done | bytes 262176 | tf_op jit(solution)/shard_map/ppermute | solution.py:434
  201.1 3.9 %sender_sum.3 = (f32[64,2048]{1,0:T(8,128)S(1)}, f32[8,128]{1,0:T(8,128)}) custom-call(s32[1]{0:T(128)} %bitcast.12.me_ref, s32[256,128]{1,0:T(8,128)S(1)} %bitcast.46, bf16[64,8192]{1,0:T(8,128)(2,1)S(1)} %get-tuple-element.193.rest_0_), custom_call_target="tpu_custom_call" | custom-call | tf_op jit(solution)/shard_map/sender_sum/pallas_call | solution.py:685
  (135 shorter events, 36.6 us)
Async XLA Ops:
  0.7 25.0 %collective-permute-start.3 = (bf16[64,2048]{1,0:T(8,128)(2,1)}, bf16[64,2048]{1,0:T(8,128)(2,1)S(1)}, u32[]{:S(2)}, u32[]{:S(2)}) collective-permute-start(bf16[64,2048]{1,0:T(8,128)(2,1)} %bitcast.34), channel_id=1, source_target_pairs={{0,2},{1,3},{2,0},{3,1},{4,6},{5,7},{6,4},{7,5},{8,10},{9,11},{10,... | collective-permute-start | bytes 786440 | tf_op jit(solution)/shard_map/ppermute | solution.py:434
  3.8 21.9 %collective-permute-start.2 = (bf16[64,2048]{1,0:T(8,128)(2,1)}, bf16[64,2048]{1,0:T(8,128)(2,1)S(1)}, u32[]{:S(2)}, u32[]{:S(2)}) collective-permute-start(bf16[64,2048]{1,0:T(8,128)(2,1)} %bitcast.35), channel_id=1, source_target_pairs={{0,6},{1,7},{2,4},{3,5},{4,2},{5,3},{6,0},{7,1},{8,14},{9,15},{10,... | collective-permute-start | bytes 786440 | tf_op jit(solution)/shard_map/ppermute | solution.py:434
  6.2 23.2 %collective-permute-start.1 = (bf16[64,2048]{1,0:T(8,128)(2,1)}, bf16[64,2048]{1,0:T(8,128)(2,1)S(1)}, u32[]{:S(2)}, u32[]{:S(2)}) collective-permute-start(bf16[64,2048]{1,0:T(8,128)(2,1)} %bitcast.36), channel_id=1, source_target_pairs={{0,4},{1,5},{2,6},{3,7},{4,0},{5,1},{6,2},{7,3},{8,12},{9,13},{10,... | collective-permute-start | bytes 786440 | tf_op jit(solution)/shard_map/ppermute | solution.py:434
  6.4 23.1 %collective-permute-start = (bf16[64,2048]{1,0:T(8,128)(2,1)}, bf16[64,2048]{1,0:T(8,128)(2,1)S(1)}, u32[]{:S(2)}, u32[]{:S(2)}) collective-permute-start(bf16[64,2048]{1,0:T(8,128)(2,1)} %bitcast.37), channel_id=1, source_target_pairs={{0,1},{1,0},{2,3},{3,2},{4,5},{5,4},{6,7},{7,6},{8,9},{9,8},{10,11... | collective-permute-start | bytes 786440 | tf_op jit(solution)/shard_map/ppermute | solution.py:434
  30.4 20.4 %all-to-all-start = ((s32[8,32,128]{2,1,0:T(8,128)}), s32[8,32,128]{2,1,0:T(8,128)S(1)}, u32[]{:S(2)}, u32[]{:S(2)}) async-start(s32[8,32,128]{2,1,0:T(8,128)} %add_add_fusion.1), calls=%async_computation | async-start | bytes 262144 | tf_op jit(solution)/shard_map/all_to_all | solution.py:541
  35.2 15.8 %collective-permute-start.4 = (bf16[64,2048]{1,0:T(8,128)(2,1)S(1)}, bf16[64,2048]{1,0:T(8,128)(2,1)S(1)}, u32[]{:S(2)}, u32[]{:S(2)}) collective-permute-start(bf16[64,2048]{1,0:T(8,128)(2,1)S(1)} %collective-permute-done.1.rest_0_.rest_2_), channel_id=1, source_target_pairs={{0,1},{1,0},{2,3},{3,2},{4,5},{5,4},{6,7},{7,6},{8,9},{9,8},{10,11... | collective-permute-start | bytes 786440 | tf_op jit(solution)/shard_map/ppermute | solution.py:434
  37.2 14.0 %collective-permute-start.5 = (bf16[64,2048]{1,0:T(8,128)(2,1)S(1)}, bf16[64,2048]{1,0:T(8,128)(2,1)S(1)}, u32[]{:S(2)}, u32[]{:S(2)}) collective-permute-start(bf16[64,2048]{1,0:T(8,128)(2,1)S(1)} %collective-permute-done.2.rest_1_.rest_3_), channel_id=1, source_target_pairs={{0,1},{1,0},{2,3},{3,2},{4,5},{5,4},{6,7},{7,6},{8,9},{9,8},{10,11... | collective-permute-start | bytes 786440 | tf_op jit(solution)/shard_map/ppermute | solution.py:434
  37.2 31.3 %collective-permute-start.8 = (bf16[64,2048]{1,0:T(8,128)(2,1)S(1)}, bf16[64,2048]{1,0:T(8,128)(2,1)S(1)}, u32[]{:S(2)}, u32[]{:S(2)}) collective-permute-start(bf16[64,2048]{1,0:T(8,128)(2,1)S(1)} %collective-permute-done.3.rest_1_.rest_3_), channel_id=1, source_target_pairs={{0,1},{1,0},{2,3},{3,2},{4,5},{5,4},{6,7},{7,6},{8,9},{9,8},{10,11... | collective-permute-start | bytes 786440 | tf_op jit(solution)/shard_map/ppermute | solution.py:434
  60.2 16.8 %collective-permute-start.7 = (bf16[64,2048]{1,0:T(8,128)(2,1)S(1)}, bf16[64,2048]{1,0:T(8,128)(2,1)S(1)}, u32[]{:S(2)}, u32[]{:S(2)}) collective-permute-start(bf16[64,2048]{1,0:T(8,128)(2,1)S(1)} %get-tuple-element.132), channel_id=1, source_target_pairs={{0,1},{1,0},{2,3},{3,2},{4,5},{5,4},{6,7},{7,6},{8,9},{9,8},{10,11... | collective-permute-start | bytes 786440 | tf_op jit(solution)/shard_map/ppermute | solution.py:434
  61.3 18.9 %collective-permute-start.6 = (bf16[64,2048]{1,0:T(8,128)(2,1)S(1)}, bf16[64,2048]{1,0:T(8,128)(2,1)S(1)}, u32[]{:S(2)}, u32[]{:S(2)}) collective-permute-start(bf16[64,2048]{1,0:T(8,128)(2,1)S(1)} %get-tuple-element.130), channel_id=1, source_target_pairs={{0,1},{1,0},{2,3},{3,2},{4,5},{5,4},{6,7},{7,6},{8,9},{9,8},{10,11... | collective-permute-start | bytes 786440 | tf_op jit(solution)/shard_map/ppermute | solution.py:434
  74.9 14.2 %collective-permute-start.9 = (bf16[64,2048]{1,0:T(8,128)(2,1)S(1)}, bf16[64,2048]{1,0:T(8,128)(2,1)S(1)}, u32[]{:S(2)}, u32[]{:S(2)}) collective-permute-start(bf16[64,2048]{1,0:T(8,128)(2,1)S(1)} %get-tuple-element.138), channel_id=1, source_target_pairs={{0,1},{1,0},{2,3},{3,2},{4,5},{5,4},{6,7},{7,6},{8,9},{9,8},{10,11... | collective-permute-start | bytes 786440 | tf_op jit(solution)/shard_map/ppermute | solution.py:434
  76.1 11.6 %collective-permute-start.12 = (bf16[64,2048]{1,0:T(8,128)(2,1)S(1)}, bf16[64,2048]{1,0:T(8,128)(2,1)S(1)}, u32[]{:S(2)}, u32[]{:S(2)}) collective-permute-start(bf16[64,2048]{1,0:T(8,128)(2,1)S(1)} %get-tuple-element.140), channel_id=1, source_target_pairs={{0,1},{1,0},{2,3},{3,2},{4,5},{5,4},{6,7},{7,6},{8,9},{9,8},{10,11... | collective-permute-start | bytes 786440 | tf_op jit(solution)/shard_map/ppermute | solution.py:434
  77.1 12.0 %collective-permute-start.11 = (bf16[64,2048]{1,0:T(8,128)(2,1)S(1)}, bf16[64,2048]{1,0:T(8,128)(2,1)S(1)}, u32[]{:S(2)}, u32[]{:S(2)}) collective-permute-start(bf16[64,2048]{1,0:T(8,128)(2,1)S(1)} %add_convert_fusion.4), channel_id=1, source_target_pairs={{0,6},{1,7},{2,4},{3,5},{4,2},{5,3},{6,0},{7,1},{8,14},{9,15},{10,... | collective-permute-start | bytes 786440 | tf_op jit(solution)/shard_map/ppermute | solution.py:434
  80.3 18.9 %collective-permute-start.10 = (bf16[64,2048]{1,0:T(8,128)(2,1)S(1)}, bf16[64,2048]{1,0:T(8,128)(2,1)S(1)}, u32[]{:S(2)}, u32[]{:S(2)}) collective-permute-start(bf16[64,2048]{1,0:T(8,128)(2,1)S(1)} %add_convert_fusion.5), channel_id=1, source_target_pairs={{0,4},{1,5},{2,6},{3,7},{4,0},{5,1},{6,2},{7,3},{8,12},{9,13},{10,... | collective-permute-start | bytes 786440 | tf_op jit(solution)/shard_map/ppermute | solution.py:434
  87.8 12.1 %collective-permute-start.13 = (bf16[64,2048]{1,0:T(8,128)(2,1)S(1)}, bf16[64,2048]{1,0:T(8,128)(2,1)S(1)}, u32[]{:S(2)}, u32[]{:S(2)}) collective-permute-start(bf16[64,2048]{1,0:T(8,128)(2,1)S(1)} %add_convert_fusion.3), channel_id=1, source_target_pairs={{0,2},{1,3},{2,0},{3,1},{4,6},{5,7},{6,4},{7,5},{8,10},{9,11},{10,... | collective-permute-start | bytes 786440 | tf_op jit(solution)/shard_map/ppermute | solution.py:434
  101.5 10.3 %collective-permute-start.15 = (bf16[64,2048]{1,0:T(8,128)(2,1)S(1)}, bf16[64,2048]{1,0:T(8,128)(2,1)S(1)}, u32[]{:S(2)}, u32[]{:S(2)}) collective-permute-start(bf16[64,2048]{1,0:T(8,128)(2,1)S(1)} %get-tuple-element.152.rest_0_), channel_id=1, source_target_pairs={{0,2},{1,3},{2,0},{3,1},{4,6},{5,7},{6,4},{7,5},{8,10},{9,11},{10,... | collective-permute-start | bytes 786440 | tf_op jit(solution)/shard_map/ppermute | solution.py:434
  101.5 19.2 %collective-permute-start.19 = (bf16[64,2048]{1,0:T(8,128)(2,1)S(1)}, bf16[64,2048]{1,0:T(8,128)(2,1)S(1)}, u32[]{:S(2)}, u32[]{:S(2)}) collective-permute-start(bf16[64,2048]{1,0:T(8,128)(2,1)S(1)} %get-tuple-element.152.rest_0_), channel_id=1, source_target_pairs={{0,6},{1,7},{2,4},{3,5},{4,2},{5,3},{6,0},{7,1},{8,14},{9,15},{10,... | collective-permute-start | bytes 786440 | tf_op jit(solution)/shard_map/ppermute | solution.py:434
  103.7 22.5 %collective-permute-start.17 = (bf16[64,2048]{1,0:T(8,128)(2,1)S(1)}, bf16[64,2048]{1,0:T(8,128)(2,1)S(1)}, u32[]{:S(2)}, u32[]{:S(2)}) collective-permute-start(bf16[64,2048]{1,0:T(8,128)(2,1)S(1)} %get-tuple-element.152.rest_0_), channel_id=1, source_target_pairs={{0,4},{1,5},{2,6},{3,7},{4,0},{5,1},{6,2},{7,3},{8,12},{9,13},{10,... | collective-permute-start | bytes 786440 | tf_op jit(solution)/shard_map/ppermute | solution.py:434
  126.2 12.7 %collective-permute-start.18 = (bf16[64,2048]{1,0:T(8,128)(2,1)S(1)}, bf16[64,2048]{1,0:T(8,128)(2,1)S(1)}, u32[]{:S(2)}, u32[]{:S(2)}) collective-permute-start(bf16[64,2048]{1,0:T(8,128)(2,1)S(1)} %collective-permute-done.17.rest_0_), channel_id=1, source_target_pairs={{0,1},{1,0},{2,3},{3,2},{4,5},{5,4},{6,7},{7,6},{8,9},{9,8},{10,11... | collective-permute-start | bytes 786440 | tf_op jit(solution)/shard_map/ppermute | solution.py:434
  127.0 14.0 %collective-permute-start.20 = (bf16[64,2048]{1,0:T(8,128)(2,1)S(1)}, bf16[64,2048]{1,0:T(8,128)(2,1)S(1)}, u32[]{:S(2)}, u32[]{:S(2)}) collective-permute-start(bf16[64,2048]{1,0:T(8,128)(2,1)S(1)} %collective-permute-done.19.rest_1_), channel_id=1, source_target_pairs={{0,1},{1,0},{2,3},{3,2},{4,5},{5,4},{6,7},{7,6},{8,9},{9,8},{10,11... | collective-permute-start | bytes 786440 | tf_op jit(solution)/shard_map/ppermute | solution.py:434
  128.2 23.4 %collective-permute-start.14 = (bf16[64,2048]{1,0:T(8,128)(2,1)S(1)}, bf16[64,2048]{1,0:T(8,128)(2,1)S(1)}, u32[]{:S(2)}, u32[]{:S(2)}) collective-permute-start(bf16[64,2048]{1,0:T(8,128)(2,1)S(1)} %get-tuple-element.152.rest_0_), channel_id=1, source_target_pairs={{0,1},{1,0},{2,3},{3,2},{4,5},{5,4},{6,7},{7,6},{8,9},{9,8},{10,11... | collective-permute-start | bytes 786440 | tf_op jit(solution)/shard_map/ppermute | solution.py:434
  129.1 22.6 %collective-permute-start.16 = (bf16[64,2048]{1,0:T(8,128)(2,1)S(1)}, bf16[64,2048]{1,0:T(8,128)(2,1)S(1)}, u32[]{:S(2)}, u32[]{:S(2)}) collective-permute-start(bf16[64,2048]{1,0:T(8,128)(2,1)S(1)} %collective-permute-done.15.rest_1_), channel_id=1, source_target_pairs={{0,1},{1,0},{2,3},{3,2},{4,5},{5,4},{6,7},{7,6},{8,9},{9,8},{10,11... | collective-permute-start | bytes 786440 | tf_op jit(solution)/shard_map/ppermute | solution.py:434
  149.6 12.7 %collective-permute-start.22 = (bf16[64,2048]{1,0:T(8,128)(2,1)S(1)}, bf16[64,2048]{1,0:T(8,128)(2,1)S(1)}, u32[]{:S(2)}, u32[]{:S(2)}) collective-permute-start(bf16[64,2048]{1,0:T(8,128)(2,1)S(1)} %get-tuple-element.179), channel_id=1, source_target_pairs={{0,1},{1,0},{2,3},{3,2},{4,5},{5,4},{6,7},{7,6},{8,9},{9,8},{10,11... | collective-permute-start | bytes 786440 | tf_op jit(solution)/shard_map/ppermute | solution.py:434
  150.4 12.9 %collective-permute-start.23 = (bf16[64,2048]{1,0:T(8,128)(2,1)S(1)}, bf16[64,2048]{1,0:T(8,128)(2,1)S(1)}, u32[]{:S(2)}, u32[]{:S(2)}) collective-permute-start(bf16[64,2048]{1,0:T(8,128)(2,1)S(1)} %get-tuple-element.180), channel_id=1, source_target_pairs={{0,1},{1,0},{2,3},{3,2},{4,5},{5,4},{6,7},{7,6},{8,9},{9,8},{10,11... | collective-permute-start | bytes 786440 | tf_op jit(solution)/shard_map/ppermute | solution.py:434
  161.2 18.8 %collective-permute-start.32 = (bf16[64,2048]{1,0:T(8,128)(2,1)S(1)}, bf16[64,2048]{1,0:T(8,128)(2,1)S(1)}, u32[]{:S(2)}, u32[]{:S(2)}) collective-permute-start(bf16[64,2048]{1,0:T(8,128)(2,1)S(1)} %get-tuple-element.198), channel_id=1, source_target_pairs={{0,1},{1,0},{2,3},{3,2},{4,5},{5,4},{6,7},{7,6},{8,9},{9,8},{10,11... | collective-permute-start | bytes 786440 | tf_op jit(solution)/shard_map/ppermute | solution.py:434
  167.0 12.9 %collective-permute-start.24 = (f32[72,512]{1,0:T(8,128)S(1)}, f32[72,512]{1,0:T(8,128)S(1)}, u32[]{:S(2)}, u32[]{:S(2)}) collective-permute-start(f32[72,512]{1,0:T(8,128)S(1)} %add.61), channel_id=1, source_target_pairs={{0,4},{1,5},{2,6},{3,7},{4,0},{5,1},{6,2},{7,3},{8,12},{9,13},{10,... | collective-permute-start | bytes 442376 | tf_op jit(solution)/shard_map/ppermute | solution.py:434
  167.1 38.1 %collective-permute-start.31 = (bf16[64,2048]{1,0:T(8,128)(2,1)S(1)}, bf16[64,2048]{1,0:T(8,128)(2,1)S(1)}, u32[]{:S(2)}, u32[]{:S(2)}) collective-permute-start(bf16[64,2048]{1,0:T(8,128)(2,1)S(1)} %get-tuple-element.196), channel_id=1, source_target_pairs={{0,1},{1,0},{2,3},{3,2},{4,5},{5,4},{6,7},{7,6},{8,9},{9,8},{10,11... | collective-permute-start | bytes 786440 | tf_op jit(solution)/shard_map/ppermute | solution.py:434
  168.1 23.6 %collective-permute-start.30 = (bf16[64,2048]{1,0:T(8,128)(2,1)S(1)}, bf16[64,2048]{1,0:T(8,128)(2,1)S(1)}, u32[]{:S(2)}, u32[]{:S(2)}) collective-permute-start(bf16[64,2048]{1,0:T(8,128)(2,1)S(1)} %add_convert_fusion.1), channel_id=1, source_target_pairs={{0,6},{1,7},{2,4},{3,5},{4,2},{5,3},{6,0},{7,1},{8,14},{9,15},{10,... | collective-permute-start | bytes 786440 | tf_op jit(solution)/shard_map/ppermute | solution.py:434
  181.6 10.0 %collective-permute-start.25 = (f32[72,512]{1,0:T(8,128)S(1)}, f32[72,512]{1,0:T(8,128)S(1)}, u32[]{:S(2)}, u32[]{:S(2)}) collective-permute-start(f32[72,512]{1,0:T(8,128)S(1)} %add.62), channel_id=1, source_target_pairs={{0,8},{8,0},{16,24},{24,16},{1,9},{9,1},{17,25},{25,17},{2,10},{10... | collective-permute-start | bytes 442376 | tf_op jit(solution)/shard_map/ppermute | solution.py:460
  186.2 14.9 %collective-permute-start.29 = (bf16[64,2048]{1,0:T(8,128)(2,1)S(1)}, bf16[64,2048]{1,0:T(8,128)(2,1)S(1)}, u32[]{:S(2)}, u32[]{:S(2)}) collective-permute-start(bf16[64,2048]{1,0:T(8,128)(2,1)S(1)} %add_convert_fusion.2), channel_id=1, source_target_pairs={{0,4},{1,5},{2,6},{3,7},{4,0},{5,1},{6,2},{7,3},{8,12},{9,13},{10,... | collective-permute-start | bytes 786440 | tf_op jit(solution)/shard_map/ppermute | solution.py:434
  189.4 15.8 %collective-permute-start.33 = (bf16[64,2048]{1,0:T(8,128)(2,1)S(1)}, bf16[64,2048]{1,0:T(8,128)(2,1)S(1)}, u32[]{:S(2)}, u32[]{:S(2)}) collective-permute-start(bf16[64,2048]{1,0:T(8,128)(2,1)S(1)} %add_convert_fusion), channel_id=1, source_target_pairs={{0,2},{1,3},{2,0},{3,1},{4,6},{5,7},{6,4},{7,5},{8,10},{9,11},{10,... | collective-permute-start | bytes 786440 | tf_op jit(solution)/shard_map/ppermute | solution.py:434
  191.6 13.5 %collective-permute-start.28 = (f32[72,512]{1,0:T(8,128)S(1)}, f32[72,512]{1,0:T(8,128)S(1)}, u32[]{:S(2)}, u32[]{:S(2)}) collective-permute-start(f32[72,512]{1,0:T(8,128)S(1)} %add_add_fusion), channel_id=1, source_target_pairs={{0,2},{1,3},{2,0},{3,1},{4,6},{5,7},{6,4},{7,5},{8,10},{9,11},{10,... | collective-permute-start | bytes 442376 | tf_op jit(solution)/shard_map/ppermute | solution.py:434
  (35 other events, 531.6 us)

commit v5 on v4

--- a/solution.py
+++ b/solution.py
@@ -522,7 +522,7 @@
     for masks in halves:
         count = len(masks)
         pick, base, gate = pl.pallas_call(
-            functools.partial(sender_kernel, min(1024, wide), 0),
+            functools.partial(sender_kernel, min(2048, wide), 0),
             grid_spec=pltpu.PrefetchScalarGridSpec(
                 num_scalar_prefetch=1,
                 grid=(count, chunks),
@@ -706,7 +706,7 @@
         there[m] = swap(both[m], m)
     if far is not None:
         edge_pack = edge_pack + tie(far, gate)
-        edge_pack = add_groups(edge_pack)
+        edge_pack = add_groups(tie(edge_pack, got[0]))
         mask = 2
         while mask < peers // 2:
             edge_pack = edge_pack + swap(edge_pack, mask)

time: 207 us -> 202 us (0.976)
  Pallas kernels: 100 us -> 97.2 us
  waiting for transfers between devices: 48.9 us -> 46.8 us
    ppermute x31, waiting for transfers between devices: 43.4 us -> 40.5 us  [swap(): return lax.ppermute(value, 'peer', [(i, i ^ mask) for i in range(peers)])]
    pallas_call x2, Pallas kernels: 20.4 us -> 17.6 us  [per_device(): pl.pallas_call(functools.partial(sender_kernel, min(2048, wide), 0), grid...]
  transfers between devices with their start and end apart: 35 -> 35, of which waited for: 13 -> 14; matrix products, arithmetic and copies ran while one was open for 1% -> 1% of each run, Pallas kernels for 47% -> 47%
where the time goes in v5:
time: 202 us; the launch traced here: 201 us
  Pallas kernels  97.2 us (48%)
  waiting for transfers between devices  46.8 us (23%)
  starting transfers between devices  44 us (22%)
  local copies, waits for them, and re-layouts  10.2 us (5%)
  other arithmetic  2.09 us (1%)
    ppermute x31, waiting for transfers between devices, swap(): return lax.ppermute(value, 'peer', [(i, i ^ mask) for i in range(peers)])  40.5 us
    ppermute x31, starting transfers between devices, swap(): return lax.ppermute(value, 'peer', [(i, i ^ mask) for i in range(peers)])  37.3 us
    pallas_call x4, Pallas kernels, per_device(): pl.pallas_call(functools.partial(backward_kernel, masks, blocks, piece, e...  34.7 us
    pallas_call x4, Pallas kernels, per_device(): pl.pallas_call(functools.partial(forward_kernel, masks, blocks, piece, ex...  25.3 us
    pallas_call x2, Pallas kernels, per_device(): pl.pallas_call(functools.partial(sender_kernel, min(2048, wide), 0), grid...  17.6 us
    pallas_call x2, Pallas kernels, add_sent(): pl.pallas_call(functools.partial(sender_sum_kernel, tuple(starts)), grid_...  14.6 us
    unnamed x65, local copies, waits for them, and re-layouts  10.1 us
    ppermute x3, waiting for transfers between devices, add_groups(): lax.ppermute(value, 'grp', [(i, i ^ mask) for i in range(groups)])  6.29 us
  transfers between devices with their start and end apart: 35, of which 14 were waited for; matrix products, arithmetic and copies ran while one was open for 1% of the time, Pallas kernels for 47%

profile of v5, /device:TPU:0, one launch (start us, length us, event | category | flops | bytes accessed | tf_op | source)
XLA Modules:
  0.0 201.5 jit_solution(5424189934164324579)
XLA Ops:
  0.7 3.1 %collective-permute-start.3 = (bf16[64,2048]{1,0:T(8,128)(2,1)}, bf16[64,2048]{1,0:T(8,128)(2,1)S(1)}, u32[]{:S(2)}, u32[]{:S(2)}) collective-permute-start(bf16[64,2048]{1,0:T(8,128)(2,1)} %bitcast.34), channel_id=1, source_target_pairs={{0,2},{1,3},{2,0},{3,1},{4,6},{5,7},{6,4},{7,5},{8,10},{9,11},{10,... | collective-permute-start | bytes 786440 | tf_op jit(solution)/shard_map/ppermute | solution.py:434
  3.8 2.5 %collective-permute-start.2 = (bf16[64,2048]{1,0:T(8,128)(2,1)}, bf16[64,2048]{1,0:T(8,128)(2,1)S(1)}, u32[]{:S(2)}, u32[]{:S(2)}) collective-permute-start(bf16[64,2048]{1,0:T(8,128)(2,1)} %bitcast.35), channel_id=1, source_target_pairs={{0,6},{1,7},{2,4},{3,5},{4,2},{5,3},{6,0},{7,1},{8,14},{9,15},{10,... | collective-permute-start | bytes 786440 | tf_op jit(solution)/shard_map/ppermute | solution.py:434
  8.6 1.8 prepare.1
  14.0 8.8 %sender.2 = (bf16[64,16384]{1,0:T(8,128)(2,1)S(1)}, f32[64,16384]{1,0:T(8,128)}, f32[8,128]{1,0:T(8,128)}) custom-call(s32[1]{0:T(128)} %bitcast.12.me_ref, bf16[64,2048]{1,0:T(8,128)(2,1)S(1)} %bitcast.38, s32[256,128]{1,0:T(8,128)S(1)} %bitcast.43, bf16[64,32768]{1,0:T(8,128)(2,1)} %bitcast.50, bf16[64,128]{1,0:T(8,128)(2,1)S(1)} %copy-done.23, ...), custom_call_target="tpu_custom_call" | custom-call | tf_op jit(solution)/shard_map/sender/pallas_call | solution.py:524
  24.2 5.3 %collective-permute-done.1.rest_0_.rest_2_ = bf16[64,2048]{1,0:T(8,128)(2,1)S(1)} collective-permute-done((bf16[64,2048]{1,0:T(8,128)(2,1)}, bf16[64,2048]{1,0:T(8,128)(2,1)S(1)}, u32[]{:S(2)}, u32[]{:S(2)}) %collective-permute-start.1) | collective-permute-done | bytes 262176 | tf_op jit(solution)/shard_map/ppermute | solution.py:434
  30.4 4.8 %all-to-all-start = ((s32[8,32,128]{2,1,0:T(8,128)}), s32[8,32,128]{2,1,0:T(8,128)S(1)}, u32[]{:S(2)}, u32[]{:S(2)}) async-start(s32[8,32,128]{2,1,0:T(8,128)} %add_add_fusion.1), calls=%async_computation | async-start | bytes 262144 | tf_op jit(solution)/shard_map/all_to_all | solution.py:541
  35.2 2.0 %collective-permute-start.4 = (bf16[64,2048]{1,0:T(8,128)(2,1)S(1)}, bf16[64,2048]{1,0:T(8,128)(2,1)S(1)}, u32[]{:S(2)}, u32[]{:S(2)}) collective-permute-start(bf16[64,2048]{1,0:T(8,128)(2,1)S(1)} %collective-permute-done.1.rest_0_.rest_2_), channel_id=1, source_target_pairs={{0,1},{1,0},{2,3},{3,2},{4,5},{5,4},{6,7},{7,6},{8,9},{9,8},{10,11... | collective-permute-start | bytes 786440 | tf_op jit(solution)/shard_map/ppermute | solution.py:434
  37.2 2.0 collective-permute-start.8
  39.2 8.8 %sender.3 = (bf16[64,16384]{1,0:T(8,128)(2,1)S(1)}, f32[64,16384]{1,0:T(8,128)}, f32[8,128]{1,0:T(8,128)}) custom-call(s32[1]{0:T(128)} %bitcast.12.me_ref, bf16[64,2048]{1,0:T(8,128)(2,1)S(1)} %bitcast.39, s32[256,128]{1,0:T(8,128)S(1)} %bitcast.44, bf16[64,32768]{1,0:T(8,128)(2,1)} %bitcast.51, bf16[64,128]{1,0:T(8,128)(2,1)S(1)} %copy-done.24, ...), custom_call_target="tpu_custom_call" | custom-call | tf_op jit(solution)/shard_map/sender/pallas_call | solution.py:524
  51.9 6.3 %forward.4 = (bf16[64,32768]{1,0:T(8,128)(2,1)}, bf16[64,8192]{1,0:T(8,128)(2,1)S(1)}, bf16[64,8192]{1,0:T(8,128)(2,1)S(1)}, bf16[64,8192]{1,0:T(8,128)(2,1)S(1)...) custom-call(s32[257]{0:T(512)S(1)} %pad_add_fusion.meta_ref, ...), custom_call_target="tpu_custom_call" | custom-call | tf_op jit(solution)/shard_map/forward/pallas_call | solution.py:560
  62.2 6.3 %forward.5 = (bf16[64,32768]{1,0:T(8,128)(2,1)}, bf16[64,8192]{1,0:T(8,128)(2,1)S(1)}, bf16[64,8192]{1,0:T(8,128)(2,1)S(1)}, bf16[64,8192]{1,0:T(8,128)(2,1)S(1)...) custom-call(s32[257]{0:T(512)S(1)} %pad_add_fusion.meta_ref, ...), custom_call_target="tpu_custom_call", output_to_operand_aliasing={{0}: (9, {})} | custom-call | tf_op jit(solution)/shard_map/forward/pallas_call | solution.py:560
  68.5 6.4 %forward.6 = (bf16[64,32768]{1,0:T(8,128)(2,1)}, bf16[64,8192]{1,0:T(8,128)(2,1)S(1)}, bf16[64,8192]{1,0:T(8,128)(2,1)S(1)}, bf16[64,8192]{1,0:T(8,128)(2,1)S(1)...) custom-call(s32[257]{0:T(512)S(1)} %pad_add_fusion.meta_ref, ...), custom_call_target="tpu_custom_call", output_to_operand_aliasing={{0}: (9, {})} | custom-call | tf_op jit(solution)/shard_map/forward/pallas_call | solution.py:560
  77.1 3.1 %collective-permute-start.11 = (bf16[64,2048]{1,0:T(8,128)(2,1)S(1)}, bf16[64,2048]{1,0:T(8,128)(2,1)S(1)}, u32[]{:S(2)}, u32[]{:S(2)}) collective-permute-start(bf16[64,2048]{1,0:T(8,128)(2,1)S(1)} %add_convert_fusion.4), channel_id=1, source_target_pairs={{0,6},{1,7},{2,4},{3,5},{4,2},{5,3},{6,0},{7,1},{8,14},{9,15},{10,... | collective-permute-start | bytes 786440 | tf_op jit(solution)/shard_map/ppermute | solution.py:434
  80.5 6.3 %forward.7 = (bf16[64,32768]{1,0:T(8,128)(2,1)}, bf16[64,8192]{1,0:T(8,128)(2,1)S(1)}, bf16[64,8192]{1,0:T(8,128)(2,1)S(1)}, bf16[64,8192]{1,0:T(8,128)(2,1)S(1)...) custom-call(s32[257]{0:T(512)S(1)} %pad_add_fusion.meta_ref, ...), custom_call_target="tpu_custom_call", output_to_operand_aliasing={{0}: (9, {})} | custom-call | tf_op jit(solution)/shard_map/forward/pallas_call | solution.py:560
  89.2 8.9 %collective-permute-done.10.rest_2_ = bf16[64,2048]{1,0:T(8,128)(2,1)S(1)} collective-permute-done((bf16[64,2048]{1,0:T(8,128)(2,1)S(1)}, bf16[64,2048]{1,0:T(8,128)(2,1)S(1)}, u32[]{:S(2)}, u32[]{:S(2)}) %collective-permute-start.10) | collective-permute-done | bytes 262176 | tf_op jit(solution)/shard_map/ppermute | solution.py:434
  98.0 1.8 collective-permute-done.13.rest_4_
  101.6 1.7 collective-permute-start.19
  103.3 1.8 collective-permute-start.17
  105.1 5.0 %collective-permute-done.15.rest_1_ = bf16[64,2048]{1,0:T(8,128)(2,1)S(1)} collective-permute-done((bf16[64,2048]{1,0:T(8,128)(2,1)S(1)}, bf16[64,2048]{1,0:T(8,128)(2,1)S(1)}, u32[]{:S(2)}, u32[]{:S(2)}) %collective-permute-start.15) | collective-permute-done | bytes 262176 | tf_op jit(solution)/shard_map/ppermute | solution.py:434
  110.1 8.8 %backward.4 = (f32[64,32768]{1,0:T(8,128)}, bf16[64,8192]{1,0:T(8,128)(2,1)S(1)}, f32[72,512]{1,0:T(8,128)S(1)}, f32[8,128]{1,0:T(8,128)}, bf16[64,2048]{1,0:T(8,128)(2,1)S(1)}, /*index=5*/bf16[64,2048]{1,0:T(8,128)(2,1)S(1)}) custom-call(s32[257]{0:T(512)S(1)} %pad_add_fusion.meta_ref, s32[8,32,128]{2,1,0:T(8,128)S(1)} %broadcast_and_fusion.code_ref, ...), custom_call_target="tpu_custom_call" | custom-call | tf_op jit(solution)/shard_map/backward/pallas_call | solution.py:612
  119.0 6.3 %collective-permute-done.17.rest_0_ = bf16[64,2048]{1,0:T(8,128)(2,1)S(1)} collective-permute-done((bf16[64,2048]{1,0:T(8,128)(2,1)S(1)}, bf16[64,2048]{1,0:T(8,128)(2,1)S(1)}, u32[]{:S(2)}, u32[]{:S(2)}) %collective-permute-start.17) | collective-permute-done | bytes 262176 | tf_op jit(solution)/shard_map/ppermute | solution.py:434
  129.3 8.6 %backward.5 = (f32[64,32768]{1,0:T(8,128)}, bf16[64,8192]{1,0:T(8,128)(2,1)S(1)}, f32[72,512]{1,0:T(8,128)S(1)}, f32[8,128]{1,0:T(8,128)}, bf16[64,2048]{1,0:T(8,128)(2,1)S(1)}, /*index=5*/bf16[64,2048]{1,0:T(8,128)(2,1)S(1)}) custom-call(s32[257]{0:T(512)S(1)} %pad_add_fusion.meta_ref, ...), custom_call_target="tpu_custom_call", output_to_operand_aliasing={{0}: (17, {})} | custom-call | tf_op jit(solution)/shard_map/backward/pallas_call | solution.py:612
  137.9 2.1 %collective-permute-done.20.rest_1_ = bf16[64,2048]{1,0:T(8,128)(2,1)S(1)} collective-permute-done((bf16[64,2048]{1,0:T(8,128)(2,1)S(1)}, bf16[64,2048]{1,0:T(8,128)(2,1)S(1)}, u32[]{:S(2)}, u32[]{:S(2)}) %collective-permute-start.20) | collective-permute-done | bytes 262176 | tf_op jit(solution)/shard_map/ppermute | solution.py:434
  140.1 8.6 %backward.6 = (f32[64,32768]{1,0:T(8,128)}, bf16[64,8192]{1,0:T(8,128)(2,1)S(1)}, f32[72,512]{1,0:T(8,128)S(1)}, f32[8,128]{1,0:T(8,128)}, bf16[64,2048]{1,0:T(8,128)(2,1)S(1)}, /*index=5*/bf16[64,2048]{1,0:T(8,128)(2,1)S(1)}) custom-call(s32[257]{0:T(512)S(1)} %pad_add_fusion.meta_ref, ...), custom_call_target="tpu_custom_call", output_to_operand_aliasing={{0}: (17, {})} | custom-call | tf_op jit(solution)/shard_map/backward/pallas_call | solution.py:612
  150.7 8.6 %backward.7 = (f32[64,32768]{1,0:T(8,128)}, bf16[64,8192]{1,0:T(8,128)(2,1)S(1)}, f32[72,512]{1,0:T(8,128)S(1)}, f32[8,128]{1,0:T(8,128)}, bf16[64,2048]{1,0:T(8,128)(2,1)S(1)}, /*index=5*/bf16[64,2048]{1,0:T(8,128)(2,1)S(1)}) custom-call(s32[257]{0:T(512)S(1)} %pad_add_fusion.meta_ref, ...), custom_call_target="tpu_custom_call", output_to_operand_aliasing={{0}: (17, {})} | custom-call | tf_op jit(solution)/shard_map/backward/pallas_call | solution.py:612
  162.6 3.5 %collective-permute-done.21 = f32[72,512]{1,0:T(8,128)S(1)} collective-permute-done((f32[72,512]{1,0:T(8,128)S(1)}, f32[72,512]{1,0:T(8,128)S(1)}, u32[]{:S(2)}, u32[]{:S(2)}) %collective-permute-start.21) | collective-permute-done | bytes 147488 | tf_op jit(solution)/shard_map/ppermute | solution.py:434
  167.5 1.9 collective-permute-start.30
  169.4 10.7 %sender_sum.2 = (f32[64,2048]{1,0:T(8,128)S(1)}, f32[8,128]{1,0:T(8,128)}) custom-call(s32[1]{0:T(128)} %bitcast.12.me_ref, s32[256,128]{1,0:T(8,128)S(1)} %bitcast.45, bf16[64,8192]{1,0:T(8,128)(2,1)S(1)} %get-tuple-element.187.rest_0_, bf16[64,8192]{1,0:T(8,128)(2,1)S(1)} %get-tuple-element.188.rest_1_, bf16[64,8192]{1,0:T(8,128)(2,1)S(1)} %get-tuple-element.189.rest_2_), custom_call_target="tpu_custom_call" | custom-call | tf_op jit(solution)/shard_map/sender_sum/pallas_call | solution.py:685
  182.8 4.2 %collective-permute-done.28 = f32[72,512]{1,0:T(8,128)S(1)} collective-permute-done((f32[72,512]{1,0:T(8,128)S(1)}, f32[72,512]{1,0:T(8,128)S(1)}, u32[]{:S(2)}, u32[]{:S(2)}) %collective-permute-start.28) | collective-permute-done | bytes 147488 | tf_op jit(solution)/shard_map/ppermute | solution.py:460
  187.6 2.1 %collective-permute-done.27 = f32[72,512]{1,0:T(8,128)S(1)} collective-permute-done((f32[72,512]{1,0:T(8,128)S(1)}, f32[72,512]{1,0:T(8,128)S(1)}, u32[]{:S(2)}, u32[]{:S(2)}) %collective-permute-start.27) | collective-permute-done | bytes 147488 | tf_op jit(solution)/shard_map/ppermute | solution.py:460
  191.0 3.9 %sender_sum.3 = (f32[64,2048]{1,0:T(8,128)S(1)}, f32[8,128]{1,0:T(8,128)}) custom-call(s32[1]{0:T(128)} %bitcast.12.me_ref, s32[256,128]{1,0:T(8,128)S(1)} %bitcast.46, bf16[64,8192]{1,0:T(8,128)(2,1)S(1)} %get-tuple-element.196.rest_0_), custom_call_target="tpu_custom_call" | custom-call | tf_op jit(solution)/shard_map/sender_sum/pallas_call | solution.py:685
  194.9 4.8 %collective-permute-done.29 = f32[72,512]{1,0:T(8,128)S(1)} collective-permute-done((f32[72,512]{1,0:T(8,128)S(1)}, f32[72,512]{1,0:T(8,128)S(1)}, u32[]{:S(2)}, u32[]{:S(2)}) %collective-permute-start.29) | collective-permute-done | bytes 147488 | tf_op jit(solution)/shard_map/ppermute | solution.py:434
  (135 shorter events, 39.3 us)
Async XLA Ops:
  0.7 23.5 %collective-permute-start.3 = (bf16[64,2048]{1,0:T(8,128)(2,1)}, bf16[64,2048]{1,0:T(8,128)(2,1)S(1)}, u32[]{:S(2)}, u32[]{:S(2)}) collective-permute-start(bf16[64,2048]{1,0:T(8,128)(2,1)} %bitcast.34), channel_id=1, source_target_pairs={{0,2},{1,3},{2,0},{3,1},{4,6},{5,7},{6,4},{7,5},{8,10},{9,11},{10,... | collective-permute-start | bytes 786440 | tf_op jit(solution)/shard_map/ppermute | solution.py:434
  3.8 20.4 %collective-permute-start.2 = (bf16[64,2048]{1,0:T(8,128)(2,1)}, bf16[64,2048]{1,0:T(8,128)(2,1)S(1)}, u32[]{:S(2)}, u32[]{:S(2)}) collective-permute-start(bf16[64,2048]{1,0:T(8,128)(2,1)} %bitcast.35), channel_id=1, source_target_pairs={{0,6},{1,7},{2,4},{3,5},{4,2},{5,3},{6,0},{7,1},{8,14},{9,15},{10,... | collective-permute-start | bytes 786440 | tf_op jit(solution)/shard_map/ppermute | solution.py:434
  6.2 23.2 %collective-permute-start.1 = (bf16[64,2048]{1,0:T(8,128)(2,1)}, bf16[64,2048]{1,0:T(8,128)(2,1)S(1)}, u32[]{:S(2)}, u32[]{:S(2)}) collective-permute-start(bf16[64,2048]{1,0:T(8,128)(2,1)} %bitcast.36), channel_id=1, source_target_pairs={{0,4},{1,5},{2,6},{3,7},{4,0},{5,1},{6,2},{7,3},{8,12},{9,13},{10,... | collective-permute-start | bytes 786440 | tf_op jit(solution)/shard_map/ppermute | solution.py:434
  6.4 23.1 %collective-permute-start = (bf16[64,2048]{1,0:T(8,128)(2,1)}, bf16[64,2048]{1,0:T(8,128)(2,1)S(1)}, u32[]{:S(2)}, u32[]{:S(2)}) collective-permute-start(bf16[64,2048]{1,0:T(8,128)(2,1)} %bitcast.37), channel_id=1, source_target_pairs={{0,1},{1,0},{2,3},{3,2},{4,5},{5,4},{6,7},{7,6},{8,9},{9,8},{10,11... | collective-permute-start | bytes 786440 | tf_op jit(solution)/shard_map/ppermute | solution.py:434
  30.4 19.0 %all-to-all-start = ((s32[8,32,128]{2,1,0:T(8,128)}), s32[8,32,128]{2,1,0:T(8,128)S(1)}, u32[]{:S(2)}, u32[]{:S(2)}) async-start(s32[8,32,128]{2,1,0:T(8,128)} %add_add_fusion.1), calls=%async_computation | async-start | bytes 262144 | tf_op jit(solution)/shard_map/all_to_all | solution.py:541
  35.2 14.4 %collective-permute-start.4 = (bf16[64,2048]{1,0:T(8,128)(2,1)S(1)}, bf16[64,2048]{1,0:T(8,128)(2,1)S(1)}, u32[]{:S(2)}, u32[]{:S(2)}) collective-permute-start(bf16[64,2048]{1,0:T(8,128)(2,1)S(1)} %collective-permute-done.1.rest_0_.rest_2_), channel_id=1, source_target_pairs={{0,1},{1,0},{2,3},{3,2},{4,5},{5,4},{6,7},{7,6},{8,9},{9,8},{10,11... | collective-permute-start | bytes 786440 | tf_op jit(solution)/shard_map/ppermute | solution.py:434
  37.2 14.0 %collective-permute-start.5 = (bf16[64,2048]{1,0:T(8,128)(2,1)S(1)}, bf16[64,2048]{1,0:T(8,128)(2,1)S(1)}, u32[]{:S(2)}, u32[]{:S(2)}) collective-permute-start(bf16[64,2048]{1,0:T(8,128)(2,1)S(1)} %collective-permute-done.2.rest_1_.rest_3_), channel_id=1, source_target_pairs={{0,1},{1,0},{2,3},{3,2},{4,5},{5,4},{6,7},{7,6},{8,9},{9,8},{10,11... | collective-permute-start | bytes 786440 | tf_op jit(solution)/shard_map/ppermute | solution.py:434
  37.2 31.3 %collective-permute-start.8 = (bf16[64,2048]{1,0:T(8,128)(2,1)S(1)}, bf16[64,2048]{1,0:T(8,128)(2,1)S(1)}, u32[]{:S(2)}, u32[]{:S(2)}) collective-permute-start(bf16[64,2048]{1,0:T(8,128)(2,1)S(1)} %collective-permute-done.3.rest_1_.rest_3_), channel_id=1, source_target_pairs={{0,1},{1,0},{2,3},{3,2},{4,5},{5,4},{6,7},{7,6},{8,9},{9,8},{10,11... | collective-permute-start | bytes 786440 | tf_op jit(solution)/shard_map/ppermute | solution.py:434
  60.2 16.9 %collective-permute-start.7 = (bf16[64,2048]{1,0:T(8,128)(2,1)S(1)}, bf16[64,2048]{1,0:T(8,128)(2,1)S(1)}, u32[]{:S(2)}, u32[]{:S(2)}) collective-permute-start(bf16[64,2048]{1,0:T(8,128)(2,1)S(1)} %get-tuple-element.133), channel_id=1, source_target_pairs={{0,1},{1,0},{2,3},{3,2},{4,5},{5,4},{6,7},{7,6},{8,9},{9,8},{10,11... | collective-permute-start | bytes 786440 | tf_op jit(solution)/shard_map/ppermute | solution.py:434
  61.3 19.0 %collective-permute-start.6 = (bf16[64,2048]{1,0:T(8,128)(2,1)S(1)}, bf16[64,2048]{1,0:T(8,128)(2,1)S(1)}, u32[]{:S(2)}, u32[]{:S(2)}) collective-permute-start(bf16[64,2048]{1,0:T(8,128)(2,1)S(1)} %get-tuple-element.131), channel_id=1, source_target_pairs={{0,1},{1,0},{2,3},{3,2},{4,5},{5,4},{6,7},{7,6},{8,9},{9,8},{10,11... | collective-permute-start | bytes 786440 | tf_op jit(solution)/shard_map/ppermute | solution.py:434
  75.0 14.2 %collective-permute-start.9 = (bf16[64,2048]{1,0:T(8,128)(2,1)S(1)}, bf16[64,2048]{1,0:T(8,128)(2,1)S(1)}, u32[]{:S(2)}, u32[]{:S(2)}) collective-permute-start(bf16[64,2048]{1,0:T(8,128)(2,1)S(1)} %get-tuple-element.139), channel_id=1, source_target_pairs={{0,1},{1,0},{2,3},{3,2},{4,5},{5,4},{6,7},{7,6},{8,9},{9,8},{10,11... | collective-permute-start | bytes 786440 | tf_op jit(solution)/shard_map/ppermute | solution.py:434
  76.1 11.7 %collective-permute-start.12 = (bf16[64,2048]{1,0:T(8,128)(2,1)S(1)}, bf16[64,2048]{1,0:T(8,128)(2,1)S(1)}, u32[]{:S(2)}, u32[]{:S(2)}) collective-permute-start(bf16[64,2048]{1,0:T(8,128)(2,1)S(1)} %get-tuple-element.141), channel_id=1, source_target_pairs={{0,1},{1,0},{2,3},{3,2},{4,5},{5,4},{6,7},{7,6},{8,9},{9,8},{10,11... | collective-permute-start | bytes 786440 | tf_op jit(solution)/shard_map/ppermute | solution.py:434
  77.1 12.0 %collective-permute-start.11 = (bf16[64,2048]{1,0:T(8,128)(2,1)S(1)}, bf16[64,2048]{1,0:T(8,128)(2,1)S(1)}, u32[]{:S(2)}, u32[]{:S(2)}) collective-permute-start(bf16[64,2048]{1,0:T(8,128)(2,1)S(1)} %add_convert_fusion.4), channel_id=1, source_target_pairs={{0,6},{1,7},{2,4},{3,5},{4,2},{5,3},{6,0},{7,1},{8,14},{9,15},{10,... | collective-permute-start | bytes 786440 | tf_op jit(solution)/shard_map/ppermute | solution.py:434
  80.3 17.7 %collective-permute-start.10 = (bf16[64,2048]{1,0:T(8,128)(2,1)S(1)}, bf16[64,2048]{1,0:T(8,128)(2,1)S(1)}, u32[]{:S(2)}, u32[]{:S(2)}) collective-permute-start(bf16[64,2048]{1,0:T(8,128)(2,1)S(1)} %add_convert_fusion.5), channel_id=1, source_target_pairs={{0,4},{1,5},{2,6},{3,7},{4,0},{5,1},{6,2},{7,3},{8,12},{9,13},{10,... | collective-permute-start | bytes 786440 | tf_op jit(solution)/shard_map/ppermute | solution.py:434
  87.8 12.1 %collective-permute-start.13 = (bf16[64,2048]{1,0:T(8,128)(2,1)S(1)}, bf16[64,2048]{1,0:T(8,128)(2,1)S(1)}, u32[]{:S(2)}, u32[]{:S(2)}) collective-permute-start(bf16[64,2048]{1,0:T(8,128)(2,1)S(1)} %add_convert_fusion.3), channel_id=1, source_target_pairs={{0,2},{1,3},{2,0},{3,1},{4,6},{5,7},{6,4},{7,5},{8,10},{9,11},{10,... | collective-permute-start | bytes 786440 | tf_op jit(solution)/shard_map/ppermute | solution.py:434
  101.6 8.5 %collective-permute-start.15 = (bf16[64,2048]{1,0:T(8,128)(2,1)S(1)}, bf16[64,2048]{1,0:T(8,128)(2,1)S(1)}, u32[]{:S(2)}, u32[]{:S(2)}) collective-permute-start(bf16[64,2048]{1,0:T(8,128)(2,1)S(1)} %get-tuple-element.153.rest_0_), channel_id=1, source_target_pairs={{0,2},{1,3},{2,0},{3,1},{4,6},{5,7},{6,4},{7,5},{8,10},{9,11},{10,... | collective-permute-start | bytes 786440 | tf_op jit(solution)/shard_map/ppermute | solution.py:434
  101.6 17.4 %collective-permute-start.19 = (bf16[64,2048]{1,0:T(8,128)(2,1)S(1)}, bf16[64,2048]{1,0:T(8,128)(2,1)S(1)}, u32[]{:S(2)}, u32[]{:S(2)}) collective-permute-start(bf16[64,2048]{1,0:T(8,128)(2,1)S(1)} %get-tuple-element.153.rest_0_), channel_id=1, source_target_pairs={{0,6},{1,7},{2,4},{3,5},{4,2},{5,3},{6,0},{7,1},{8,14},{9,15},{10,... | collective-permute-start | bytes 786440 | tf_op jit(solution)/shard_map/ppermute | solution.py:434
  103.3 22.0 %collective-permute-start.17 = (bf16[64,2048]{1,0:T(8,128)(2,1)S(1)}, bf16[64,2048]{1,0:T(8,128)(2,1)S(1)}, u32[]{:S(2)}, u32[]{:S(2)}) collective-permute-start(bf16[64,2048]{1,0:T(8,128)(2,1)S(1)} %get-tuple-element.153.rest_0_), channel_id=1, source_target_pairs={{0,4},{1,5},{2,6},{3,7},{4,0},{5,1},{6,2},{7,3},{8,12},{9,13},{10,... | collective-permute-start | bytes 786440 | tf_op jit(solution)/shard_map/ppermute | solution.py:434
  125.3 12.7 %collective-permute-start.18 = (bf16[64,2048]{1,0:T(8,128)(2,1)S(1)}, bf16[64,2048]{1,0:T(8,128)(2,1)S(1)}, u32[]{:S(2)}, u32[]{:S(2)}) collective-permute-start(bf16[64,2048]{1,0:T(8,128)(2,1)S(1)} %collective-permute-done.17.rest_0_), channel_id=1, source_target_pairs={{0,1},{1,0},{2,3},{3,2},{4,5},{5,4},{6,7},{7,6},{8,9},{9,8},{10,11... | collective-permute-start | bytes 786440 | tf_op jit(solution)/shard_map/ppermute | solution.py:434
  126.0 14.1 %collective-permute-start.20 = (bf16[64,2048]{1,0:T(8,128)(2,1)S(1)}, bf16[64,2048]{1,0:T(8,128)(2,1)S(1)}, u32[]{:S(2)}, u32[]{:S(2)}) collective-permute-start(bf16[64,2048]{1,0:T(8,128)(2,1)S(1)} %collective-permute-done.19.rest_1_), channel_id=1, source_target_pairs={{0,1},{1,0},{2,3},{3,2},{4,5},{5,4},{6,7},{7,6},{8,9},{9,8},{10,11... | collective-permute-start | bytes 786440 | tf_op jit(solution)/shard_map/ppermute | solution.py:434
  127.3 23.4 %collective-permute-start.14 = (bf16[64,2048]{1,0:T(8,128)(2,1)S(1)}, bf16[64,2048]{1,0:T(8,128)(2,1)S(1)}, u32[]{:S(2)}, u32[]{:S(2)}) collective-permute-start(bf16[64,2048]{1,0:T(8,128)(2,1)S(1)} %get-tuple-element.153.rest_0_), channel_id=1, source_target_pairs={{0,1},{1,0},{2,3},{3,2},{4,5},{5,4},{6,7},{7,6},{8,9},{9,8},{10,11... | collective-permute-start | bytes 786440 | tf_op jit(solution)/shard_map/ppermute | solution.py:434
  128.0 22.7 %collective-permute-start.16 = (bf16[64,2048]{1,0:T(8,128)(2,1)S(1)}, bf16[64,2048]{1,0:T(8,128)(2,1)S(1)}, u32[]{:S(2)}, u32[]{:S(2)}) collective-permute-start(bf16[64,2048]{1,0:T(8,128)(2,1)S(1)} %collective-permute-done.15.rest_1_), channel_id=1, source_target_pairs={{0,1},{1,0},{2,3},{3,2},{4,5},{5,4},{6,7},{7,6},{8,9},{9,8},{10,11... | collective-permute-start | bytes 786440 | tf_op jit(solution)/shard_map/ppermute | solution.py:434
  148.7 13.4 %collective-permute-start.22 = (bf16[64,2048]{1,0:T(8,128)(2,1)S(1)}, bf16[64,2048]{1,0:T(8,128)(2,1)S(1)}, u32[]{:S(2)}, u32[]{:S(2)}) collective-permute-start(bf16[64,2048]{1,0:T(8,128)(2,1)S(1)} %get-tuple-element.180), channel_id=1, source_target_pairs={{0,1},{1,0},{2,3},{3,2},{4,5},{5,4},{6,7},{7,6},{8,9},{9,8},{10,11... | collective-permute-start | bytes 786440 | tf_op jit(solution)/shard_map/ppermute | solution.py:434
  149.4 13.0 %collective-permute-start.23 = (bf16[64,2048]{1,0:T(8,128)(2,1)S(1)}, bf16[64,2048]{1,0:T(8,128)(2,1)S(1)}, u32[]{:S(2)}, u32[]{:S(2)}) collective-permute-start(bf16[64,2048]{1,0:T(8,128)(2,1)S(1)} %get-tuple-element.181), channel_id=1, source_target_pairs={{0,1},{1,0},{2,3},{3,2},{4,5},{5,4},{6,7},{7,6},{8,9},{9,8},{10,11... | collective-permute-start | bytes 786440 | tf_op jit(solution)/shard_map/ppermute | solution.py:434
  160.1 20.7 %collective-permute-start.25 = (bf16[64,2048]{1,0:T(8,128)(2,1)S(1)}, bf16[64,2048]{1,0:T(8,128)(2,1)S(1)}, u32[]{:S(2)}, u32[]{:S(2)}) collective-permute-start(bf16[64,2048]{1,0:T(8,128)(2,1)S(1)} %get-tuple-element.192), channel_id=1, source_target_pairs={{0,1},{1,0},{2,3},{3,2},{4,5},{5,4},{6,7},{7,6},{8,9},{9,8},{10,11... | collective-permute-start | bytes 786440 | tf_op jit(solution)/shard_map/ppermute | solution.py:434
  161.4 18.7 %collective-permute-start.32 = (bf16[64,2048]{1,0:T(8,128)(2,1)S(1)}, bf16[64,2048]{1,0:T(8,128)(2,1)S(1)}, u32[]{:S(2)}, u32[]{:S(2)}) collective-permute-start(bf16[64,2048]{1,0:T(8,128)(2,1)S(1)} %get-tuple-element.200), channel_id=1, source_target_pairs={{0,1},{1,0},{2,3},{3,2},{4,5},{5,4},{6,7},{7,6},{8,9},{9,8},{10,11... | collective-permute-start | bytes 786440 | tf_op jit(solution)/shard_map/ppermute | solution.py:434
  166.1 14.7 %collective-permute-start.24 = (f32[72,512]{1,0:T(8,128)S(1)}, f32[72,512]{1,0:T(8,128)S(1)}, u32[]{:S(2)}, u32[]{:S(2)}) collective-permute-start(f32[72,512]{1,0:T(8,128)S(1)} %add.61), channel_id=1, source_target_pairs={{0,4},{1,5},{2,6},{3,7},{4,0},{5,1},{6,2},{7,3},{8,12},{9,13},{10,... | collective-permute-start | bytes 442376 | tf_op jit(solution)/shard_map/ppermute | solution.py:434
  166.2 24.7 %collective-permute-start.31 = (bf16[64,2048]{1,0:T(8,128)(2,1)S(1)}, bf16[64,2048]{1,0:T(8,128)(2,1)S(1)}, u32[]{:S(2)}, u32[]{:S(2)}) collective-permute-start(bf16[64,2048]{1,0:T(8,128)(2,1)S(1)} %add_convert_fusion.1), channel_id=1, source_target_pairs={{0,6},{1,7},{2,4},{3,5},{4,2},{5,3},{6,0},{7,1},{8,14},{9,15},{10,... | collective-permute-start | bytes 786440 | tf_op jit(solution)/shard_map/ppermute | solution.py:434
  167.5 23.6 %collective-permute-start.30 = (bf16[64,2048]{1,0:T(8,128)(2,1)S(1)}, bf16[64,2048]{1,0:T(8,128)(2,1)S(1)}, u32[]{:S(2)}, u32[]{:S(2)}) collective-permute-start(bf16[64,2048]{1,0:T(8,128)(2,1)S(1)} %add_convert_fusion.2), channel_id=1, source_target_pairs={{0,4},{1,5},{2,6},{3,7},{4,0},{5,1},{6,2},{7,3},{8,12},{9,13},{10,... | collective-permute-start | bytes 786440 | tf_op jit(solution)/shard_map/ppermute | solution.py:434
  180.9 8.8 %collective-permute-start.27 = (f32[72,512]{1,0:T(8,128)S(1)}, f32[72,512]{1,0:T(8,128)S(1)}, u32[]{:S(2)}, u32[]{:S(2)}) collective-permute-start(f32[72,512]{1,0:T(8,128)S(1)} %add.62), channel_id=1, source_target_pairs={{0,16},{8,24},{16,0},{24,8},{1,17},{9,25},{17,1},{25,9},{2,18},{10... | collective-permute-start | bytes 442376 | tf_op jit(solution)/shard_map/ppermute | solution.py:460
  187.0 12.7 %collective-permute-start.33 = (bf16[64,2048]{1,0:T(8,128)(2,1)S(1)}, bf16[64,2048]{1,0:T(8,128)(2,1)S(1)}, u32[]{:S(2)}, u32[]{:S(2)}) collective-permute-start(bf16[64,2048]{1,0:T(8,128)(2,1)S(1)} %add_convert_fusion), channel_id=1, source_target_pairs={{0,2},{1,3},{2,0},{3,1},{4,6},{5,7},{6,4},{7,5},{8,10},{9,11},{10,... | collective-permute-start | bytes 786440 | tf_op jit(solution)/shard_map/ppermute | solution.py:434
  189.7 10.0 %collective-permute-start.29 = (f32[72,512]{1,0:T(8,128)S(1)}, f32[72,512]{1,0:T(8,128)S(1)}, u32[]{:S(2)}, u32[]{:S(2)}) collective-permute-start(f32[72,512]{1,0:T(8,128)S(1)} %add_add_fusion), channel_id=1, source_target_pairs={{0,2},{1,3},{2,0},{3,1},{4,6},{5,7},{6,4},{7,5},{8,10},{9,11},{10,... | collective-permute-start | bytes 442376 | tf_op jit(solution)/shard_map/ppermute | solution.py:434
  (35 other events, 516.3 us)

commit v6 on v5

--- a/solution.py
+++ b/solution.py
@@ -440,7 +440,7 @@
         return lax.optimization_barrier((value,) + others)[0]
 
     def gather_first(value):
-        return {m: swap(value, m) for m in [0, 1] + routed}
+        return {m: swap(value, m) for m in [0] + routed + [1]}
 
     def gather_rest(found, gate):
         for m in routed:
@@ -664,7 +664,7 @@
     edge_pack = edge_pack + tie(near_pack, *marks)
     far = swap(edge_pack, peers // 2) if peers > 2 else None
 
-    sum_wide = min(2048, per_peer)
+    sum_wide = min(4096, per_peer)
     sum_chunks = per_peer // sum_wide
 
     def add_sent(masks_list, hold):

time: 202 us -> 202 us (level)
  waiting for transfers between devices: 46.8 us -> 50 us
  Pallas kernels: 97.2 us -> 95 us
    ppermute x31, waiting for transfers between devices: 40.5 us -> 42.6 us  [swap(): return lax.ppermute(value, 'peer', [(i, i ^ mask) for i in range(peers)])]
    pallas_call x2, Pallas kernels: 14.6 us -> 12.5 us  [add_sent(): pl.pallas_call(functools.partial(sender_sum_kernel, tuple(starts)), grid_...]
  transfers between devices with their start and end apart: 35 -> 35, of which waited for: 14 -> 14; matrix products, arithmetic and copies ran while one was open for 1% -> 1% of each run, Pallas kernels for 47% -> 46%
where the time goes in v6:
time: 202 us; the launch traced here: 201 us
  Pallas kernels  95 us (47%)
  waiting for transfers between devices  50 us (25%)
  starting transfers between devices  42.6 us (21%)
  local copies, waits for them, and re-layouts  10.2 us (5%)
  other arithmetic  2.09 us (1%)
    ppermute x31, waiting for transfers between devices, swap(): return lax.ppermute(value, 'peer', [(i, i ^ mask) for i in range(peers)])  42.6 us
    ppermute x31, starting transfers between devices, swap(): return lax.ppermute(value, 'peer', [(i, i ^ mask) for i in range(peers)])  35.9 us
    pallas_call x4, Pallas kernels, per_device(): pl.pallas_call(functools.partial(backward_kernel, masks, blocks, piece, e...  34.7 us
    pallas_call x4, Pallas kernels, per_device(): pl.pallas_call(functools.partial(forward_kernel, masks, blocks, piece, ex...  25.3 us
    pallas_call x2, Pallas kernels, per_device(): pl.pallas_call(functools.partial(sender_kernel, min(2048, wide), 0), grid...  17.6 us
    pallas_call x2, Pallas kernels, add_sent(): pl.pallas_call(functools.partial(sender_sum_kernel, tuple(starts)), grid_...  12.5 us
    unnamed x65, local copies, waits for them, and re-layouts  10.1 us
    ppermute x3, waiting for transfers between devices, add_groups(): lax.ppermute(value, 'grp', [(i, i ^ mask) for i in range(groups)])  7.37 us
  transfers between devices with their start and end apart: 35, of which 14 were waited for; matrix products, arithmetic and copies ran while one was open for 1% of the time, Pallas kernels for 46%

profile of v6, /device:TPU:0, one launch (start us, length us, event | category | flops | bytes accessed | tf_op | source)
XLA Modules:
  0.0 201.1 jit_solution(7729593899431911681)
XLA Ops:
  0.7 3.1 %collective-permute-start.3 = (bf16[64,2048]{1,0:T(8,128)(2,1)}, bf16[64,2048]{1,0:T(8,128)(2,1)S(1)}, u32[]{:S(2)}, u32[]{:S(2)}) collective-permute-start(bf16[64,2048]{1,0:T(8,128)(2,1)} %bitcast.34), channel_id=1, source_target_pairs={{0,2},{1,3},{2,0},{3,1},{4,6},{5,7},{6,4},{7,5},{8,10},{9,11},{10,... | collective-permute-start | bytes 786440 | tf_op jit(solution)/shard_map/ppermute | solution.py:434
  3.8 2.5 %collective-permute-start.2 = (bf16[64,2048]{1,0:T(8,128)(2,1)}, bf16[64,2048]{1,0:T(8,128)(2,1)S(1)}, u32[]{:S(2)}, u32[]{:S(2)}) collective-permute-start(bf16[64,2048]{1,0:T(8,128)(2,1)} %bitcast.35), channel_id=1, source_target_pairs={{0,6},{1,7},{2,4},{3,5},{4,2},{5,3},{6,0},{7,1},{8,14},{9,15},{10,... | collective-permute-start | bytes 786440 | tf_op jit(solution)/shard_map/ppermute | solution.py:434
  8.6 1.8 prepare.1
  14.0 8.8 %sender.2 = (bf16[64,16384]{1,0:T(8,128)(2,1)S(1)}, f32[64,16384]{1,0:T(8,128)}, f32[8,128]{1,0:T(8,128)}) custom-call(s32[1]{0:T(128)} %bitcast.12.me_ref, bf16[64,2048]{1,0:T(8,128)(2,1)S(1)} %bitcast.38, s32[256,128]{1,0:T(8,128)S(1)} %bitcast.43, bf16[64,32768]{1,0:T(8,128)(2,1)} %bitcast.50, bf16[64,128]{1,0:T(8,128)(2,1)S(1)} %copy-done.23, ...), custom_call_target="tpu_custom_call" | custom-call | tf_op jit(solution)/shard_map/sender/pallas_call | solution.py:524
  24.2 5.3 %collective-permute-done.1.rest_0_.rest_2_ = bf16[64,2048]{1,0:T(8,128)(2,1)S(1)} collective-permute-done((bf16[64,2048]{1,0:T(8,128)(2,1)}, bf16[64,2048]{1,0:T(8,128)(2,1)S(1)}, u32[]{:S(2)}, u32[]{:S(2)}) %collective-permute-start.1) | collective-permute-done | bytes 262176 | tf_op jit(solution)/shard_map/ppermute | solution.py:434
  30.4 4.8 %all-to-all-start = ((s32[8,32,128]{2,1,0:T(8,128)}), s32[8,32,128]{2,1,0:T(8,128)S(1)}, u32[]{:S(2)}, u32[]{:S(2)}) async-start(s32[8,32,128]{2,1,0:T(8,128)} %add_add_fusion.1), calls=%async_computation | async-start | bytes 262144 | tf_op jit(solution)/shard_map/all_to_all | solution.py:541
  35.2 2.0 %collective-permute-start.4 = (bf16[64,2048]{1,0:T(8,128)(2,1)S(1)}, bf16[64,2048]{1,0:T(8,128)(2,1)S(1)}, u32[]{:S(2)}, u32[]{:S(2)}) collective-permute-start(bf16[64,2048]{1,0:T(8,128)(2,1)S(1)} %collective-permute-done.1.rest_0_.rest_2_), channel_id=1, source_target_pairs={{0,1},{1,0},{2,3},{3,2},{4,5},{5,4},{6,7},{7,6},{8,9},{9,8},{10,11... | collective-permute-start | bytes 786440 | tf_op jit(solution)/shard_map/ppermute | solution.py:434
  37.2 2.0 collective-permute-start.8
  39.2 8.8 %sender.3 = (bf16[64,16384]{1,0:T(8,128)(2,1)S(1)}, f32[64,16384]{1,0:T(8,128)}, f32[8,128]{1,0:T(8,128)}) custom-call(s32[1]{0:T(128)} %bitcast.12.me_ref, bf16[64,2048]{1,0:T(8,128)(2,1)S(1)} %bitcast.39, s32[256,128]{1,0:T(8,128)S(1)} %bitcast.44, bf16[64,32768]{1,0:T(8,128)(2,1)} %bitcast.51, bf16[64,128]{1,0:T(8,128)(2,1)S(1)} %copy-done.24, ...), custom_call_target="tpu_custom_call" | custom-call | tf_op jit(solution)/shard_map/sender/pallas_call | solution.py:524
  51.9 6.3 %forward.4 = (bf16[64,32768]{1,0:T(8,128)(2,1)}, bf16[64,8192]{1,0:T(8,128)(2,1)S(1)}, bf16[64,8192]{1,0:T(8,128)(2,1)S(1)}, bf16[64,8192]{1,0:T(8,128)(2,1)S(1)...) custom-call(s32[257]{0:T(512)S(1)} %pad_add_fusion.meta_ref, ...), custom_call_target="tpu_custom_call" | custom-call | tf_op jit(solution)/shard_map/forward/pallas_call | solution.py:560
  62.2 6.3 %forward.5 = (bf16[64,32768]{1,0:T(8,128)(2,1)}, bf16[64,8192]{1,0:T(8,128)(2,1)S(1)}, bf16[64,8192]{1,0:T(8,128)(2,1)S(1)}, bf16[64,8192]{1,0:T(8,128)(2,1)S(1)...) custom-call(s32[257]{0:T(512)S(1)} %pad_add_fusion.meta_ref, ...), custom_call_target="tpu_custom_call", output_to_operand_aliasing={{0}: (9, {})} | custom-call | tf_op jit(solution)/shard_map/forward/pallas_call | solution.py:560
  68.5 6.4 %forward.6 = (bf16[64,32768]{1,0:T(8,128)(2,1)}, bf16[64,8192]{1,0:T(8,128)(2,1)S(1)}, bf16[64,8192]{1,0:T(8,128)(2,1)S(1)}, bf16[64,8192]{1,0:T(8,128)(2,1)S(1)...) custom-call(s32[257]{0:T(512)S(1)} %pad_add_fusion.meta_ref, ...), custom_call_target="tpu_custom_call", output_to_operand_aliasing={{0}: (9, {})} | custom-call | tf_op jit(solution)/shard_map/forward/pallas_call | solution.py:560
  77.1 3.1 %collective-permute-start.11 = (bf16[64,2048]{1,0:T(8,128)(2,1)S(1)}, bf16[64,2048]{1,0:T(8,128)(2,1)S(1)}, u32[]{:S(2)}, u32[]{:S(2)}) collective-permute-start(bf16[64,2048]{1,0:T(8,128)(2,1)S(1)} %add_convert_fusion.4), channel_id=1, source_target_pairs={{0,6},{1,7},{2,4},{3,5},{4,2},{5,3},{6,0},{7,1},{8,14},{9,15},{10,... | collective-permute-start | bytes 786440 | tf_op jit(solution)/shard_map/ppermute | solution.py:434
  80.5 6.3 %forward.7 = (bf16[64,32768]{1,0:T(8,128)(2,1)}, bf16[64,8192]{1,0:T(8,128)(2,1)S(1)}, bf16[64,8192]{1,0:T(8,128)(2,1)S(1)}, bf16[64,8192]{1,0:T(8,128)(2,1)S(1)...) custom-call(s32[257]{0:T(512)S(1)} %pad_add_fusion.meta_ref, ...), custom_call_target="tpu_custom_call", output_to_operand_aliasing={{0}: (9, {})} | custom-call | tf_op jit(solution)/shard_map/forward/pallas_call | solution.py:560
  89.1 8.9 %collective-permute-done.10.rest_2_ = bf16[64,2048]{1,0:T(8,128)(2,1)S(1)} collective-permute-done((bf16[64,2048]{1,0:T(8,128)(2,1)S(1)}, bf16[64,2048]{1,0:T(8,128)(2,1)S(1)}, u32[]{:S(2)}, u32[]{:S(2)}) %collective-permute-start.10) | collective-permute-done | bytes 262176 | tf_op jit(solution)/shard_map/ppermute | solution.py:434
  98.0 1.9 collective-permute-done.13.rest_4_
  105.1 5.1 %collective-permute-done.15.rest_1_ = bf16[64,2048]{1,0:T(8,128)(2,1)S(1)} collective-permute-done((bf16[64,2048]{1,0:T(8,128)(2,1)S(1)}, bf16[64,2048]{1,0:T(8,128)(2,1)S(1)}, u32[]{:S(2)}, u32[]{:S(2)}) %collective-permute-start.15) | collective-permute-done | bytes 262176 | tf_op jit(solution)/shard_map/ppermute | solution.py:434
  110.2 8.8 %backward.4 = (f32[64,32768]{1,0:T(8,128)}, bf16[64,8192]{1,0:T(8,128)(2,1)S(1)}, f32[72,512]{1,0:T(8,128)S(1)}, f32[8,128]{1,0:T(8,128)}, bf16[64,2048]{1,0:T(8,128)(2,1)S(1)}, /*index=5*/bf16[64,2048]{1,0:T(8,128)(2,1)S(1)}) custom-call(s32[257]{0:T(512)S(1)} %pad_add_fusion.meta_ref, s32[8,32,128]{2,1,0:T(8,128)S(1)} %broadcast_and_fusion.code_ref, ...), custom_call_target="tpu_custom_call" | custom-call | tf_op jit(solution)/shard_map/backward/pallas_call | solution.py:612
  119.0 6.1 %collective-permute-done.17.rest_0_ = bf16[64,2048]{1,0:T(8,128)(2,1)S(1)} collective-permute-done((bf16[64,2048]{1,0:T(8,128)(2,1)S(1)}, bf16[64,2048]{1,0:T(8,128)(2,1)S(1)}, u32[]{:S(2)}, u32[]{:S(2)}) %collective-permute-start.17) | collective-permute-done | bytes 262176 | tf_op jit(solution)/shard_map/ppermute | solution.py:434
  129.2 8.6 %backward.5 = (f32[64,32768]{1,0:T(8,128)}, bf16[64,8192]{1,0:T(8,128)(2,1)S(1)}, f32[72,512]{1,0:T(8,128)S(1)}, f32[8,128]{1,0:T(8,128)}, bf16[64,2048]{1,0:T(8,128)(2,1)S(1)}, /*index=5*/bf16[64,2048]{1,0:T(8,128)(2,1)S(1)}) custom-call(s32[257]{0:T(512)S(1)} %pad_add_fusion.meta_ref, ...), custom_call_target="tpu_custom_call", output_to_operand_aliasing={{0}: (17, {})} | custom-call | tf_op jit(solution)/shard_map/backward/pallas_call | solution.py:612
  137.9 2.1 %collective-permute-done.20.rest_1_ = bf16[64,2048]{1,0:T(8,128)(2,1)S(1)} collective-permute-done((bf16[64,2048]{1,0:T(8,128)(2,1)S(1)}, bf16[64,2048]{1,0:T(8,128)(2,1)S(1)}, u32[]{:S(2)}, u32[]{:S(2)}) %collective-permute-start.20) | collective-permute-done | bytes 262176 | tf_op jit(solution)/shard_map/ppermute | solution.py:434
  140.0 8.6 %backward.6 = (f32[64,32768]{1,0:T(8,128)}, bf16[64,8192]{1,0:T(8,128)(2,1)S(1)}, f32[72,512]{1,0:T(8,128)S(1)}, f32[8,128]{1,0:T(8,128)}, bf16[64,2048]{1,0:T(8,128)(2,1)S(1)}, /*index=5*/bf16[64,2048]{1,0:T(8,128)(2,1)S(1)}) custom-call(s32[257]{0:T(512)S(1)} %pad_add_fusion.meta_ref, ...), custom_call_target="tpu_custom_call", output_to_operand_aliasing={{0}: (17, {})} | custom-call | tf_op jit(solution)/shard_map/backward/pallas_call | solution.py:612
  150.6 8.6 %backward.7 = (f32[64,32768]{1,0:T(8,128)}, bf16[64,8192]{1,0:T(8,128)(2,1)S(1)}, f32[72,512]{1,0:T(8,128)S(1)}, f32[8,128]{1,0:T(8,128)}, bf16[64,2048]{1,0:T(8,128)(2,1)S(1)}, /*index=5*/bf16[64,2048]{1,0:T(8,128)(2,1)S(1)}) custom-call(s32[257]{0:T(512)S(1)} %pad_add_fusion.meta_ref, ...), custom_call_target="tpu_custom_call", output_to_operand_aliasing={{0}: (17, {})} | custom-call | tf_op jit(solution)/shard_map/backward/pallas_call | solution.py:612
  162.5 3.5 %collective-permute-done.21 = f32[72,512]{1,0:T(8,128)S(1)} collective-permute-done((f32[72,512]{1,0:T(8,128)S(1)}, f32[72,512]{1,0:T(8,128)S(1)}, u32[]{:S(2)}, u32[]{:S(2)}) %collective-permute-start.21) | collective-permute-done | bytes 147488 | tf_op jit(solution)/shard_map/ppermute | solution.py:434
  167.5 1.9 collective-permute-start.30
  169.5 9.1 %sender_sum.2 = (f32[64,2048]{1,0:T(8,128)S(1)}, f32[8,128]{1,0:T(8,128)}) custom-call(s32[1]{0:T(128)} %bitcast.12.me_ref, s32[256,128]{1,0:T(8,128)S(1)} %bitcast.45, bf16[64,8192]{1,0:T(8,128)(2,1)S(1)} %get-tuple-element.187.rest_0_, bf16[64,8192]{1,0:T(8,128)(2,1)S(1)} %get-tuple-element.188.rest_1_, bf16[64,8192]{1,0:T(8,128)(2,1)S(1)} %get-tuple-element.189.rest_2_), custom_call_target="tpu_custom_call" | custom-call | tf_op jit(solution)/shard_map/sender_sum/pallas_call | solution.py:685
  178.6 1.8 collective-permute-done.24
  180.5 1.8 collective-permute-start.27
  182.5 3.9 %collective-permute-done.28 = f32[72,512]{1,0:T(8,128)S(1)} collective-permute-done((f32[72,512]{1,0:T(8,128)S(1)}, f32[72,512]{1,0:T(8,128)S(1)}, u32[]{:S(2)}, u32[]{:S(2)}) %collective-permute-start.28) | collective-permute-done | bytes 147488 | tf_op jit(solution)/shard_map/ppermute | solution.py:460
  186.4 3.4 %collective-permute-done.27 = f32[72,512]{1,0:T(8,128)S(1)} collective-permute-done((f32[72,512]{1,0:T(8,128)S(1)}, f32[72,512]{1,0:T(8,128)S(1)}, u32[]{:S(2)}, u32[]{:S(2)}) %collective-permute-start.27) | collective-permute-done | bytes 147488 | tf_op jit(solution)/shard_map/ppermute | solution.py:460
  190.7 3.4 %sender_sum.3 = (f32[64,2048]{1,0:T(8,128)S(1)}, f32[8,128]{1,0:T(8,128)}) custom-call(s32[1]{0:T(128)} %bitcast.12.me_ref, s32[256,128]{1,0:T(8,128)S(1)} %bitcast.46, bf16[64,8192]{1,0:T(8,128)(2,1)S(1)} %get-tuple-element.196.rest_0_), custom_call_target="tpu_custom_call" | custom-call | tf_op jit(solution)/shard_map/sender_sum/pallas_call | solution.py:685
  194.1 5.3 %collective-permute-done.29 = f32[72,512]{1,0:T(8,128)S(1)} collective-permute-done((f32[72,512]{1,0:T(8,128)S(1)}, f32[72,512]{1,0:T(8,128)S(1)}, u32[]{:S(2)}, u32[]{:S(2)}) %collective-permute-start.29) | collective-permute-done | bytes 147488 | tf_op jit(solution)/shard_map/ppermute | solution.py:434
  (135 shorter events, 39.5 us)
Async XLA Ops:
  0.7 23.5 %collective-permute-start.3 = (bf16[64,2048]{1,0:T(8,128)(2,1)}, bf16[64,2048]{1,0:T(8,128)(2,1)S(1)}, u32[]{:S(2)}, u32[]{:S(2)}) collective-permute-start(bf16[64,2048]{1,0:T(8,128)(2,1)} %bitcast.34), channel_id=1, source_target_pairs={{0,2},{1,3},{2,0},{3,1},{4,6},{5,7},{6,4},{7,5},{8,10},{9,11},{10,... | collective-permute-start | bytes 786440 | tf_op jit(solution)/shard_map/ppermute | solution.py:434
  3.8 20.4 %collective-permute-start.2 = (bf16[64,2048]{1,0:T(8,128)(2,1)}, bf16[64,2048]{1,0:T(8,128)(2,1)S(1)}, u32[]{:S(2)}, u32[]{:S(2)}) collective-permute-start(bf16[64,2048]{1,0:T(8,128)(2,1)} %bitcast.35), channel_id=1, source_target_pairs={{0,6},{1,7},{2,4},{3,5},{4,2},{5,3},{6,0},{7,1},{8,14},{9,15},{10,... | collective-permute-start | bytes 786440 | tf_op jit(solution)/shard_map/ppermute | solution.py:434
  6.2 23.2 %collective-permute-start.1 = (bf16[64,2048]{1,0:T(8,128)(2,1)}, bf16[64,2048]{1,0:T(8,128)(2,1)S(1)}, u32[]{:S(2)}, u32[]{:S(2)}) collective-permute-start(bf16[64,2048]{1,0:T(8,128)(2,1)} %bitcast.36), channel_id=1, source_target_pairs={{0,4},{1,5},{2,6},{3,7},{4,0},{5,1},{6,2},{7,3},{8,12},{9,13},{10,... | collective-permute-start | bytes 786440 | tf_op jit(solution)/shard_map/ppermute | solution.py:434
  6.4 23.1 %collective-permute-start = (bf16[64,2048]{1,0:T(8,128)(2,1)}, bf16[64,2048]{1,0:T(8,128)(2,1)S(1)}, u32[]{:S(2)}, u32[]{:S(2)}) collective-permute-start(bf16[64,2048]{1,0:T(8,128)(2,1)} %bitcast.37), channel_id=1, source_target_pairs={{0,1},{1,0},{2,3},{3,2},{4,5},{5,4},{6,7},{7,6},{8,9},{9,8},{10,11... | collective-permute-start | bytes 786440 | tf_op jit(solution)/shard_map/ppermute | solution.py:434
  30.4 19.0 %all-to-all-start = ((s32[8,32,128]{2,1,0:T(8,128)}), s32[8,32,128]{2,1,0:T(8,128)S(1)}, u32[]{:S(2)}, u32[]{:S(2)}) async-start(s32[8,32,128]{2,1,0:T(8,128)} %add_add_fusion.1), calls=%async_computation | async-start | bytes 262144 | tf_op jit(solution)/shard_map/all_to_all | solution.py:541
  35.2 14.4 %collective-permute-start.4 = (bf16[64,2048]{1,0:T(8,128)(2,1)S(1)}, bf16[64,2048]{1,0:T(8,128)(2,1)S(1)}, u32[]{:S(2)}, u32[]{:S(2)}) collective-permute-start(bf16[64,2048]{1,0:T(8,128)(2,1)S(1)} %collective-permute-done.1.rest_0_.rest_2_), channel_id=1, source_target_pairs={{0,1},{1,0},{2,3},{3,2},{4,5},{5,4},{6,7},{7,6},{8,9},{9,8},{10,11... | collective-permute-start | bytes 786440 | tf_op jit(solution)/shard_map/ppermute | solution.py:434
  37.2 14.0 %collective-permute-start.5 = (bf16[64,2048]{1,0:T(8,128)(2,1)S(1)}, bf16[64,2048]{1,0:T(8,128)(2,1)S(1)}, u32[]{:S(2)}, u32[]{:S(2)}) collective-permute-start(bf16[64,2048]{1,0:T(8,128)(2,1)S(1)} %collective-permute-done.2.rest_1_.rest_3_), channel_id=1, source_target_pairs={{0,1},{1,0},{2,3},{3,2},{4,5},{5,4},{6,7},{7,6},{8,9},{9,8},{10,11... | collective-permute-start | bytes 786440 | tf_op jit(solution)/shard_map/ppermute | solution.py:434
  37.2 31.3 %collective-permute-start.8 = (bf16[64,2048]{1,0:T(8,128)(2,1)S(1)}, bf16[64,2048]{1,0:T(8,128)(2,1)S(1)}, u32[]{:S(2)}, u32[]{:S(2)}) collective-permute-start(bf16[64,2048]{1,0:T(8,128)(2,1)S(1)} %collective-permute-done.3.rest_1_.rest_3_), channel_id=1, source_target_pairs={{0,1},{1,0},{2,3},{3,2},{4,5},{5,4},{6,7},{7,6},{8,9},{9,8},{10,11... | collective-permute-start | bytes 786440 | tf_op jit(solution)/shard_map/ppermute | solution.py:434
  60.2 16.8 %collective-permute-start.7 = (bf16[64,2048]{1,0:T(8,128)(2,1)S(1)}, bf16[64,2048]{1,0:T(8,128)(2,1)S(1)}, u32[]{:S(2)}, u32[]{:S(2)}) collective-permute-start(bf16[64,2048]{1,0:T(8,128)(2,1)S(1)} %get-tuple-element.133), channel_id=1, source_target_pairs={{0,1},{1,0},{2,3},{3,2},{4,5},{5,4},{6,7},{7,6},{8,9},{9,8},{10,11... | collective-permute-start | bytes 786440 | tf_op jit(solution)/shard_map/ppermute | solution.py:434
  61.3 18.9 %collective-permute-start.6 = (bf16[64,2048]{1,0:T(8,128)(2,1)S(1)}, bf16[64,2048]{1,0:T(8,128)(2,1)S(1)}, u32[]{:S(2)}, u32[]{:S(2)}) collective-permute-start(bf16[64,2048]{1,0:T(8,128)(2,1)S(1)} %get-tuple-element.131), channel_id=1, source_target_pairs={{0,1},{1,0},{2,3},{3,2},{4,5},{5,4},{6,7},{7,6},{8,9},{9,8},{10,11... | collective-permute-start | bytes 786440 | tf_op jit(solution)/shard_map/ppermute | solution.py:434
  74.9 14.2 %collective-permute-start.9 = (bf16[64,2048]{1,0:T(8,128)(2,1)S(1)}, bf16[64,2048]{1,0:T(8,128)(2,1)S(1)}, u32[]{:S(2)}, u32[]{:S(2)}) collective-permute-start(bf16[64,2048]{1,0:T(8,128)(2,1)S(1)} %get-tuple-element.139), channel_id=1, source_target_pairs={{0,1},{1,0},{2,3},{3,2},{4,5},{5,4},{6,7},{7,6},{8,9},{9,8},{10,11... | collective-permute-start | bytes 786440 | tf_op jit(solution)/shard_map/ppermute | solution.py:434
  76.1 11.6 %collective-permute-start.12 = (bf16[64,2048]{1,0:T(8,128)(2,1)S(1)}, bf16[64,2048]{1,0:T(8,128)(2,1)S(1)}, u32[]{:S(2)}, u32[]{:S(2)}) collective-permute-start(bf16[64,2048]{1,0:T(8,128)(2,1)S(1)} %get-tuple-element.141), channel_id=1, source_target_pairs={{0,1},{1,0},{2,3},{3,2},{4,5},{5,4},{6,7},{7,6},{8,9},{9,8},{10,11... | collective-permute-start | bytes 786440 | tf_op jit(solution)/shard_map/ppermute | solution.py:434
  77.1 12.0 %collective-permute-start.11 = (bf16[64,2048]{1,0:T(8,128)(2,1)S(1)}, bf16[64,2048]{1,0:T(8,128)(2,1)S(1)}, u32[]{:S(2)}, u32[]{:S(2)}) collective-permute-start(bf16[64,2048]{1,0:T(8,128)(2,1)S(1)} %add_convert_fusion.4), channel_id=1, source_target_pairs={{0,6},{1,7},{2,4},{3,5},{4,2},{5,3},{6,0},{7,1},{8,14},{9,15},{10,... | collective-permute-start | bytes 786440 | tf_op jit(solution)/shard_map/ppermute | solution.py:434
  80.3 17.7 %collective-permute-start.10 = (bf16[64,2048]{1,0:T(8,128)(2,1)S(1)}, bf16[64,2048]{1,0:T(8,128)(2,1)S(1)}, u32[]{:S(2)}, u32[]{:S(2)}) collective-permute-start(bf16[64,2048]{1,0:T(8,128)(2,1)S(1)} %add_convert_fusion.5), channel_id=1, source_target_pairs={{0,4},{1,5},{2,6},{3,7},{4,0},{5,1},{6,2},{7,3},{8,12},{9,13},{10,... | collective-permute-start | bytes 786440 | tf_op jit(solution)/shard_map/ppermute | solution.py:434
  87.8 12.0 %collective-permute-start.13 = (bf16[64,2048]{1,0:T(8,128)(2,1)S(1)}, bf16[64,2048]{1,0:T(8,128)(2,1)S(1)}, u32[]{:S(2)}, u32[]{:S(2)}) collective-permute-start(bf16[64,2048]{1,0:T(8,128)(2,1)S(1)} %add_convert_fusion.3), channel_id=1, source_target_pairs={{0,2},{1,3},{2,0},{3,1},{4,6},{5,7},{6,4},{7,5},{8,10},{9,11},{10,... | collective-permute-start | bytes 786440 | tf_op jit(solution)/shard_map/ppermute | solution.py:434
  101.6 8.6 %collective-permute-start.15 = (bf16[64,2048]{1,0:T(8,128)(2,1)S(1)}, bf16[64,2048]{1,0:T(8,128)(2,1)S(1)}, u32[]{:S(2)}, u32[]{:S(2)}) collective-permute-start(bf16[64,2048]{1,0:T(8,128)(2,1)S(1)} %get-tuple-element.153.rest_0_), channel_id=1, source_target_pairs={{0,2},{1,3},{2,0},{3,1},{4,6},{5,7},{6,4},{7,5},{8,10},{9,11},{10,... | collective-permute-start | bytes 786440 | tf_op jit(solution)/shard_map/ppermute | solution.py:434
  101.6 17.5 %collective-permute-start.19 = (bf16[64,2048]{1,0:T(8,128)(2,1)S(1)}, bf16[64,2048]{1,0:T(8,128)(2,1)S(1)}, u32[]{:S(2)}, u32[]{:S(2)}) collective-permute-start(bf16[64,2048]{1,0:T(8,128)(2,1)S(1)} %get-tuple-element.153.rest_0_), channel_id=1, source_target_pairs={{0,6},{1,7},{2,4},{3,5},{4,2},{5,3},{6,0},{7,1},{8,14},{9,15},{10,... | collective-permute-start | bytes 786440 | tf_op jit(solution)/shard_map/ppermute | solution.py:434
  103.3 21.9 %collective-permute-start.17 = (bf16[64,2048]{1,0:T(8,128)(2,1)S(1)}, bf16[64,2048]{1,0:T(8,128)(2,1)S(1)}, u32[]{:S(2)}, u32[]{:S(2)}) collective-permute-start(bf16[64,2048]{1,0:T(8,128)(2,1)S(1)} %get-tuple-element.153.rest_0_), channel_id=1, source_target_pairs={{0,4},{1,5},{2,6},{3,7},{4,0},{5,1},{6,2},{7,3},{8,12},{9,13},{10,... | collective-permute-start | bytes 786440 | tf_op jit(solution)/shard_map/ppermute | solution.py:434
  125.2 12.7 %collective-permute-start.18 = (bf16[64,2048]{1,0:T(8,128)(2,1)S(1)}, bf16[64,2048]{1,0:T(8,128)(2,1)S(1)}, u32[]{:S(2)}, u32[]{:S(2)}) collective-permute-start(bf16[64,2048]{1,0:T(8,128)(2,1)S(1)} %collective-permute-done.17.rest_0_), channel_id=1, source_target_pairs={{0,1},{1,0},{2,3},{3,2},{4,5},{5,4},{6,7},{7,6},{8,9},{9,8},{10,11... | collective-permute-start | bytes 786440 | tf_op jit(solution)/shard_map/ppermute | solution.py:434
  126.0 14.0 %collective-permute-start.20 = (bf16[64,2048]{1,0:T(8,128)(2,1)S(1)}, bf16[64,2048]{1,0:T(8,128)(2,1)S(1)}, u32[]{:S(2)}, u32[]{:S(2)}) collective-permute-start(bf16[64,2048]{1,0:T(8,128)(2,1)S(1)} %collective-permute-done.19.rest_1_), channel_id=1, source_target_pairs={{0,1},{1,0},{2,3},{3,2},{4,5},{5,4},{6,7},{7,6},{8,9},{9,8},{10,11... | collective-permute-start | bytes 786440 | tf_op jit(solution)/shard_map/ppermute | solution.py:434
  127.2 23.4 %collective-permute-start.14 = (bf16[64,2048]{1,0:T(8,128)(2,1)S(1)}, bf16[64,2048]{1,0:T(8,128)(2,1)S(1)}, u32[]{:S(2)}, u32[]{:S(2)}) collective-permute-start(bf16[64,2048]{1,0:T(8,128)(2,1)S(1)} %get-tuple-element.153.rest_0_), channel_id=1, source_target_pairs={{0,1},{1,0},{2,3},{3,2},{4,5},{5,4},{6,7},{7,6},{8,9},{9,8},{10,11... | collective-permute-start | bytes 786440 | tf_op jit(solution)/shard_map/ppermute | solution.py:434
  128.0 22.6 %collective-permute-start.16 = (bf16[64,2048]{1,0:T(8,128)(2,1)S(1)}, bf16[64,2048]{1,0:T(8,128)(2,1)S(1)}, u32[]{:S(2)}, u32[]{:S(2)}) collective-permute-start(bf16[64,2048]{1,0:T(8,128)(2,1)S(1)} %collective-permute-done.15.rest_1_), channel_id=1, source_target_pairs={{0,1},{1,0},{2,3},{3,2},{4,5},{5,4},{6,7},{7,6},{8,9},{9,8},{10,11... | collective-permute-start | bytes 786440 | tf_op jit(solution)/shard_map/ppermute | solution.py:434
  148.6 13.5 %collective-permute-start.22 = (bf16[64,2048]{1,0:T(8,128)(2,1)S(1)}, bf16[64,2048]{1,0:T(8,128)(2,1)S(1)}, u32[]{:S(2)}, u32[]{:S(2)}) collective-permute-start(bf16[64,2048]{1,0:T(8,128)(2,1)S(1)} %get-tuple-element.180), channel_id=1, source_target_pairs={{0,1},{1,0},{2,3},{3,2},{4,5},{5,4},{6,7},{7,6},{8,9},{9,8},{10,11... | collective-permute-start | bytes 786440 | tf_op jit(solution)/shard_map/ppermute | solution.py:434
  149.4 12.9 %collective-permute-start.23 = (bf16[64,2048]{1,0:T(8,128)(2,1)S(1)}, bf16[64,2048]{1,0:T(8,128)(2,1)S(1)}, u32[]{:S(2)}, u32[]{:S(2)}) collective-permute-start(bf16[64,2048]{1,0:T(8,128)(2,1)S(1)} %get-tuple-element.181), channel_id=1, source_target_pairs={{0,1},{1,0},{2,3},{3,2},{4,5},{5,4},{6,7},{7,6},{8,9},{9,8},{10,11... | collective-permute-start | bytes 786440 | tf_op jit(solution)/shard_map/ppermute | solution.py:434
  160.1 20.4 %collective-permute-start.25 = (bf16[64,2048]{1,0:T(8,128)(2,1)S(1)}, bf16[64,2048]{1,0:T(8,128)(2,1)S(1)}, u32[]{:S(2)}, u32[]{:S(2)}) collective-permute-start(bf16[64,2048]{1,0:T(8,128)(2,1)S(1)} %get-tuple-element.192), channel_id=1, source_target_pairs={{0,1},{1,0},{2,3},{3,2},{4,5},{5,4},{6,7},{7,6},{8,9},{9,8},{10,11... | collective-permute-start | bytes 786440 | tf_op jit(solution)/shard_map/ppermute | solution.py:434
  161.3 17.3 %collective-permute-start.32 = (bf16[64,2048]{1,0:T(8,128)(2,1)S(1)}, bf16[64,2048]{1,0:T(8,128)(2,1)S(1)}, u32[]{:S(2)}, u32[]{:S(2)}) collective-permute-start(bf16[64,2048]{1,0:T(8,128)(2,1)S(1)} %get-tuple-element.200), channel_id=1, source_target_pairs={{0,1},{1,0},{2,3},{3,2},{4,5},{5,4},{6,7},{7,6},{8,9},{9,8},{10,11... | collective-permute-start | bytes 786440 | tf_op jit(solution)/shard_map/ppermute | solution.py:434
  166.0 14.4 %collective-permute-start.24 = (f32[72,512]{1,0:T(8,128)S(1)}, f32[72,512]{1,0:T(8,128)S(1)}, u32[]{:S(2)}, u32[]{:S(2)}) collective-permute-start(f32[72,512]{1,0:T(8,128)S(1)} %add.61), channel_id=1, source_target_pairs={{0,4},{1,5},{2,6},{3,7},{4,0},{5,1},{6,2},{7,3},{8,12},{9,13},{10,... | collective-permute-start | bytes 442376 | tf_op jit(solution)/shard_map/ppermute | solution.py:434
  166.1 23.9 %collective-permute-start.31 = (bf16[64,2048]{1,0:T(8,128)(2,1)S(1)}, bf16[64,2048]{1,0:T(8,128)(2,1)S(1)}, u32[]{:S(2)}, u32[]{:S(2)}) collective-permute-start(bf16[64,2048]{1,0:T(8,128)(2,1)S(1)} %add_convert_fusion.1), channel_id=1, source_target_pairs={{0,6},{1,7},{2,4},{3,5},{4,2},{5,3},{6,0},{7,1},{8,14},{9,15},{10,... | collective-permute-start | bytes 786440 | tf_op jit(solution)/shard_map/ppermute | solution.py:434
  167.5 23.1 %collective-permute-start.30 = (bf16[64,2048]{1,0:T(8,128)(2,1)S(1)}, bf16[64,2048]{1,0:T(8,128)(2,1)S(1)}, u32[]{:S(2)}, u32[]{:S(2)}) collective-permute-start(bf16[64,2048]{1,0:T(8,128)(2,1)S(1)} %add_convert_fusion.2), channel_id=1, source_target_pairs={{0,4},{1,5},{2,6},{3,7},{4,0},{5,1},{6,2},{7,3},{8,12},{9,13},{10,... | collective-permute-start | bytes 786440 | tf_op jit(solution)/shard_map/ppermute | solution.py:434
  180.5 9.3 %collective-permute-start.27 = (f32[72,512]{1,0:T(8,128)S(1)}, f32[72,512]{1,0:T(8,128)S(1)}, u32[]{:S(2)}, u32[]{:S(2)}) collective-permute-start(f32[72,512]{1,0:T(8,128)S(1)} %add.62), channel_id=1, source_target_pairs={{0,16},{8,24},{16,0},{24,8},{1,17},{9,25},{17,1},{25,9},{2,18},{10... | collective-permute-start | bytes 442376 | tf_op jit(solution)/shard_map/ppermute | solution.py:460
  186.4 13.0 %collective-permute-start.33 = (bf16[64,2048]{1,0:T(8,128)(2,1)S(1)}, bf16[64,2048]{1,0:T(8,128)(2,1)S(1)}, u32[]{:S(2)}, u32[]{:S(2)}) collective-permute-start(bf16[64,2048]{1,0:T(8,128)(2,1)S(1)} %add_convert_fusion), channel_id=1, source_target_pairs={{0,2},{1,3},{2,0},{3,1},{4,6},{5,7},{6,4},{7,5},{8,10},{9,11},{10,... | collective-permute-start | bytes 786440 | tf_op jit(solution)/shard_map/ppermute | solution.py:434
  189.9 9.5 %collective-permute-start.29 = (f32[72,512]{1,0:T(8,128)S(1)}, f32[72,512]{1,0:T(8,128)S(1)}, u32[]{:S(2)}, u32[]{:S(2)}) collective-permute-start(f32[72,512]{1,0:T(8,128)S(1)} %add_add_fusion), channel_id=1, source_target_pairs={{0,2},{1,3},{2,0},{3,1},{4,6},{5,7},{6,4},{7,5},{8,10},{9,11},{10,... | collective-permute-start | bytes 442376 | tf_op jit(solution)/shard_map/ppermute | solution.py:434
  (35 other events, 515.5 us)
